TPU v7x, 512 devices: a whole 4x8x8 slice. The times are simulated.
512 devices in a mesh: band: 32 (over x_lo, z, core), grid: 16 (over x_hi, y).
Axes of the slice: x: 4 (x_hi: 2, x_lo: 2; x = x_hi * 2 + x_lo), y: 8, z: 8, core: 2. Of those that a mesh axis runs over, the one named last changes fastest.
Arguments:
- orbitals: float32 [32, 48, 2304], P('band', 'grid'), may hold values from -6 to 6
Outputs:
- compressed: float32 [32, 48, 2304], P('band', 'grid')
All inputs are finite; a program needn't handle non-finite values.
Results may differ from a plain program's by a relative error of at most 0.000092.
Values sent between devices are 32-bit elements; how exact they have to be, the bound alone decides.
No kernel may reach another device: no remote copies, remote signals or barrier semaphores. Data moves between devices by JAX's collectives and lax.ppermute only.
A program may use at most 64 MiB of HBM per device.

v0:
```python
import math

import jax
import jax.numpy as jnp
from jax import lax
from jax.sharding import PartitionSpec as P

NG = 48


full_precision = lax.Precision.HIGHEST
coulomb_scale = 50.0


def in_order(tiles, dim):
    dims = list(tiles.shape[1:])
    dims[dim] *= tiles.shape[0]
    return jnp.moveaxis(tiles, 0, dim).reshape(dims)


def from_everyone(array, axis):
    devices = lax.axis_size(axis)
    return lax.all_to_all(
        jnp.broadcast_to(array[None], (devices, *array.shape)), axis, 0, 0, tiled=True
    )


def collect(array, axis, dim):
    return in_order(from_everyone(array, axis), dim)


def split_up(array, dim, devices):
    dims = array.shape
    tiles = array.reshape(*dims[:dim], devices, dims[dim] // devices, *dims[dim + 1 :])
    return jnp.moveaxis(tiles, dim, 0)


def sent_and_summed(array, axis, dim):
    devices = lax.axis_size(axis)
    tiles = lax.all_to_all(split_up(array, dim, devices), axis, 0, 0, tiled=True)
    return jnp.sum(tiles, axis=0)


def of_everyone(array, axis):
    everything = from_everyone(array, axis)
    return jnp.sum(everything, axis=0)


def wave_tables(length):
    counter = jnp.arange(length, dtype=jnp.int32)
    product = counter[:, None] * counter[None, :] % length
    angles = product.astype(jnp.float32) * (2.0 * math.pi / length)
    return (jnp.cos(angles), jnp.sin(angles))


def signed_squares(indices, length):
    signed = jnp.where(indices < length // 2, indices, indices - length).astype(jnp.float32)
    return signed * signed


def kernel_block(length, row_count):
    counter = jnp.arange(length, dtype=jnp.int32)
    across = signed_squares(counter, length)
    middle = signed_squares(jnp.arange(row_count, dtype=jnp.int32), length)
    squared = across[:, None, None] + middle[None, :, None] + across[None, None, :]
    kernel = jnp.where(squared > 0.0, coulomb_scale / jnp.maximum(squared, 1.0), 0.0)
    return kernel.reshape(length, row_count * length)


def contract(operand, matrix, pattern):
    return jnp.einsum(pattern, operand, matrix, precision=full_precision)


def forward_planes(density, cosine, sine):
    number, planes, flat_cells = density.shape
    length = cosine.shape[0]
    lattice = density.reshape(number, planes, length, length)
    real_part = contract(lattice, cosine, "pxyz,zk->pxyk")
    imag_part = -contract(lattice, sine, "pxyz,zk->pxyk")
    real_next = contract(real_part, cosine, "pxyk,yl->pxlk") + contract(
        imag_part, sine, "pxyk,yl->pxlk"
    )
    imag_next = contract(imag_part, cosine, "pxyk,yl->pxlk") - contract(
        real_part, sine, "pxyk,yl->pxlk"
    )
    return jnp.stack([real_next, imag_next]).reshape(2, number, planes, length * length)


def inverse_planes(spectrum, cosine, sine):
    number = spectrum.shape[1]
    planes = spectrum.shape[2]
    length = cosine.shape[0]
    real_in = spectrum[0].reshape(number, planes, length, length)
    imag_in = spectrum[1].reshape(number, planes, length, length)
    real_mid = contract(real_in, cosine, "pxlk,ly->pxyk") - contract(imag_in, sine, "pxlk,ly->pxyk")
    imag_mid = contract(real_in, sine, "pxlk,ly->pxyk") + contract(imag_in, cosine, "pxlk,ly->pxyk")
    result = contract(real_mid, cosine, "pxyk,kz->pxyz") - contract(imag_mid, sine, "pxyk,kz->pxyz")
    return result.reshape(number, planes, length * length) / float(length**3)


def edge_solve(columns, cosine, sine, kernel):
    real_in = columns[0]
    imag_in = columns[1]
    real_fwd = contract(real_in, cosine, "pxr,xk->pkr") + contract(imag_in, sine, "pxr,xk->pkr")
    imag_fwd = contract(imag_in, cosine, "pxr,xk->pkr") - contract(real_in, sine, "pxr,xk->pkr")
    real_fwd = real_fwd * kernel
    imag_fwd = imag_fwd * kernel
    real_back = contract(real_fwd, cosine, "pkr,kx->pxr") - contract(imag_fwd, sine, "pkr,kx->pxr")
    imag_back = contract(real_fwd, sine, "pkr,kx->pxr") + contract(imag_fwd, cosine, "pkr,kx->pxr")
    return jnp.stack([real_back, imag_back])


def whole_potential(density, cosine, sine, kernel_full):
    planar = forward_planes(density[None], cosine, sine)
    solved = edge_solve(planar, cosine, sine, kernel_full)
    return inverse_planes(solved, cosine, sine)[0]


def per_device(orbitals):
    blocks, planes, flat_cells = orbitals.shape
    length = NG
    band_count = lax.axis_size("band")
    band_rank = lax.axis_index("band")
    cosine, sine = wave_tables(length)
    kernel_full = kernel_block(length, length)
    own_whole = collect(orbitals, "grid", 1)
    every_slab = collect(orbitals, "band", 0)
    partners = lax.all_to_all(every_slab, "grid", split_axis=0, concat_axis=1, tiled=True)
    partner_count = partners.shape[0]

    def pair_step(pair_index, running):
        mine_index = pair_index // partner_count
        other_index = pair_index % partner_count
        mine = lax.dynamic_index_in_dim(own_whole, mine_index, 0, keepdims=False)
        other = lax.dynamic_index_in_dim(partners, other_index, 0, keepdims=False)
        potential = whole_potential(mine * other, cosine, sine, kernel_full)
        current = lax.dynamic_index_in_dim(running, mine_index, 0, keepdims=False)
        return lax.dynamic_update_index_in_dim(running, current + other * potential, mine_index, 0)

    partial_field = lax.fori_loop(0, blocks * partner_count, pair_step, jnp.zeros_like(own_whole))
    summed = sent_and_summed(partial_field, "grid", 1)
    exchange_field = -summed
    total_bands = blocks * band_count
    cells_total = float(length**3)
    partial_rows = jnp.einsum(
        "nxc,bxc->nb", collect(orbitals, "band", 0), exchange_field, precision=full_precision
    )
    column_sums = of_everyone(partial_rows, "grid")
    projected = collect(column_sums, "band", 1) / cells_total
    definite = -0.5 * (projected + projected.T)
    lower = jnp.linalg.cholesky(definite)
    inverse_lower = jax.scipy.linalg.solve_triangular(
        lower, jnp.eye(total_bands, dtype=jnp.float32), lower=True
    )
    own_rows = lax.dynamic_slice_in_dim(inverse_lower, band_rank * blocks, blocks, 0)
    return jnp.einsum(
        "bl,lxc->bxc", own_rows, collect(exchange_field, "band", 0), precision=full_precision
    )


def solution(mesh):
    placed = (P("band", "grid", None),)
    return jax.shard_map(
        per_device, mesh=mesh, in_specs=placed, out_specs=P("band", "grid", None), check_vma=False
    )
```

profile of v0, /device:TPU:1, one launch (start us, length us, event | category | flops | bytes accessed | tf_op | source)
XLA Modules:
  0.0 292.7 jit_solution(397371213149815037)
XLA Ops:
  1.2 35.7 %all_to_all.49 = f32[32,1,3,2304]{3,1,2,0:T(1,128)S(1)} all-to-all(f32[32,1,3,2304]{3,1,2,0:T(1,128)S(1)} %broadcast_in_dim.26), channel_id=1, replica_groups=mesh['band'=32,'grid'=16] {'band'}, dimensions={0} | all-to-all | bytes 1769472 | tf_op jit(solution)/shard_map/all_to_all | solution.py:23
  38.1 9.1 %all-to-all-start.2 = ((f32[16,1,3,2304]{3,1,2,0:T(1,128)}), f32[16,1,3,2304]{3,1,2,0:T(1,128)S(1)}, u32[]{:S(2)}, u32[]{:S(2)}) async-start(f32[16,1,3,2304]{3,1,2,0:T(1,128)} %broadcast_in_dim.27), calls=%async_computation.2 | async-start | bytes 884736 | tf_op jit(solution)/shard_map/all_to_all | solution.py:23
  48.9 9.7 %all-to-all-done.2 = f32[16,1,3,2304]{3,1,2,0:T(1,128)S(1)} async-done(((f32[16,1,3,2304]{3,1,2,0:T(1,128)}), f32[16,1,3,2304]{3,1,2,0:T(1,128)S(1)}, u32[]{:S(2)}, u32[]{:S(2)}) %all-to-all-start.2) | async-done | bytes 442400 | tf_op jit(solution)/shard_map/all_to_all | solution.py:23
  58.5 7.3 %all-to-all-start.1 = ((f32[32,3,2304]{2,1,0:T(4,128)}), f32[32,3,2304]{2,1,0:T(4,128)S(1)}, u32[]{:S(2)}, u32[]{:S(2)}) async-start(f32[32,3,2304]{2,1,0:T(4,128)} %copy.103), calls=%async_computation.1 | async-start | bytes 2359296 | tf_op jit(solution)/shard_map/all_to_all | solution.py:128
  66.6 27.6 %all-to-all-done.1 = f32[32,3,2304]{2,1,0:T(4,128)S(1)} async-done(((f32[32,3,2304]{2,1,0:T(4,128)}), f32[32,3,2304]{2,1,0:T(4,128)S(1)}, u32[]{:S(2)}, u32[]{:S(2)}) %all-to-all-start.1) | async-done | bytes 884768 | tf_op jit(solution)/shard_map/all_to_all | solution.py:128
  95.6 112.0 %while.17 = (s32[]{:T(128)}, f32[1,48,2304]{2,1,0:T(8,128)}, f32[2,48,2304]{2,0,1:T(2,128)}, f32[1,48,2304]{2,1,0:T(8,128)S(1)}, f32[48]{0:T(128)S(1)}, /*index=...) while((s32[]{:T(128)}, f32[1,48,2304]{2,1,0:T(8,128)}, f32[2,48,2304]{2,0,1:T(2,128)}, ...), condition=%wide.region_1.2_spmd.clone.clone, body=%wide.region_0.1_spmd.clone.clone.sunk | while | flops 1276867584 | bytes 42071568 | solution.py:140
  121.4 2.0 fusion.327
  123.4 4.3 %fusion.323 = f32[48,48,48]{1,2,0:T(8,128)S(1)} fusion(f32[48,48,48]{2,1,0:T(8,128)S(1)} %mul.1031), kind=kOutput, calls=%fused_computation.49.clone.1 | convolution fusion | flops 63721728 | bytes 884736 | tf_op jit(solution)/shard_map/while/body/eval_jaxpr/pxyz,zk->pxyk/dot_general | solution.py:71
  134.6 2.0 fusion.325
  145.9 2.0 fusion.339
  147.9 2.0 fusion.340
  149.9 2.0 fusion.334
  151.9 2.0 fusion.337
  153.9 2.0 fusion.338
  156.0 2.0 fusion.341
  164.3 2.0 fusion.327
  166.3 4.3 %fusion.323 = f32[48,48,48]{1,2,0:T(8,128)S(1)} fusion(f32[48,48,48]{2,1,0:T(8,128)S(1)} %mul.1031), kind=kOutput, calls=%fused_computation.49.clone.1 | convolution fusion | flops 63721728 | bytes 884736 | tf_op jit(solution)/shard_map/while/body/eval_jaxpr/pxyz,zk->pxyk/dot_general | solution.py:71
  177.5 2.0 fusion.325
  188.8 2.0 fusion.339
  190.8 2.0 fusion.340
  192.8 2.0 fusion.334
  194.8 2.0 fusion.337
  196.8 2.0 fusion.338
  198.9 2.0 fusion.341
  201.9 1.9 select_add_fusion.2
  209.1 19.7 %all_to_all.50 = f32[16,1,3,2304]{3,1,2,0:T(1,128)S(1)} all-to-all(f32[16,1,3,2304]{3,1,2,0:T(1,128)S(1)} %transpose_reshape.3), channel_id=1, replica_groups=mesh['band'=32,'grid'=16] {'grid'}, dimensions={0} | all-to-all | bytes 884736 | tf_op jit(solution)/shard_map/all_to_all | solution.py:40
  230.0 14.8 %all_to_all.51 = f32[16,32,1]{1,2,0:T(1,128)S(1)} all-to-all(f32[16,32,1]{1,2,0:T(1,128)S(1)} %broadcast_in_dim.28), channel_id=1, replica_groups=mesh['band'=32,'grid'=16] {'grid'}, dimensions={0} | all-to-all | bytes 4096 | tf_op jit(solution)/shard_map/all_to_all | solution.py:23
  244.8 17.6 %all_to_all.52 = f32[32,32,1]{1,2,0:T(1,128)S(1)} all-to-all(f32[32,32,1]{1,2,0:T(1,128)S(1)} %broadcast_in_dim.29), channel_id=1, replica_groups=mesh['band'=32,'grid'=16] {'band'}, dimensions={0} | all-to-all | bytes 8192 | tf_op jit(solution)/shard_map/all_to_all | solution.py:23
  263.9 4.4 %all-to-all-start.6 = ((f32[32,1,3,2304]{3,1,2,0:T(1,128)}), f32[32,1,3,2304]{3,1,2,0:T(1,128)S(1)}, u32[]{:S(2)}, u32[]{:S(2)}) async-start(f32[32,1,3,2304]{3,1,2,0:T(1,128)} %broadcast_in_dim.30), calls=%async_computation.6 | async-start | bytes 1769472 | tf_op jit(solution)/shard_map/all_to_all | solution.py:23
  268.5 2.9 cholesky.17
  272.8 2.4 custom-call.7
  275.4 16.0 %all-to-all-done.6 = f32[32,1,3,2304]{3,1,2,0:T(1,128)S(1)} async-done(((f32[32,1,3,2304]{3,1,2,0:T(1,128)}), f32[32,1,3,2304]{3,1,2,0:T(1,128)S(1)}, u32[]{:S(2)}, u32[]{:S(2)}) %all-to-all-start.6) | async-done | bytes 884768 | tf_op jit(solution)/shard_map/all_to_all | solution.py:23
  (102 shorter events, 56.9 us)
Async XLA Ops:
  37.0 10.3 %copy-start.4 = (f32[32,1,3,2304]{3,1,2,0:T(1,128)}, f32[32,1,3,2304]{3,1,2,0:T(1,128)S(1)}, u32[]{:S(2)}) copy-start(f32[32,1,3,2304]{3,1,2,0:T(1,128)S(1)} %all_to_all.49) | copy-start | bytes 2654212
  38.1 20.5 %all-to-all-start.2 = ((f32[16,1,3,2304]{3,1,2,0:T(1,128)}), f32[16,1,3,2304]{3,1,2,0:T(1,128)S(1)}, u32[]{:S(2)}, u32[]{:S(2)}) async-start(f32[16,1,3,2304]{3,1,2,0:T(1,128)} %broadcast_in_dim.27), calls=%async_computation.2 | async-start | bytes 884736 | tf_op jit(solution)/shard_map/all_to_all | solution.py:23
  58.5 35.7 %all-to-all-start.1 = ((f32[32,3,2304]{2,1,0:T(4,128)}), f32[32,3,2304]{2,1,0:T(4,128)S(1)}, u32[]{:S(2)}, u32[]{:S(2)}) async-start(f32[32,3,2304]{2,1,0:T(4,128)} %copy.103), calls=%async_computation.1 | async-start | bytes 2359296 | tf_op jit(solution)/shard_map/all_to_all | solution.py:128
  116.9 2.5 copy-start.2
  118.7 0.8 copy-start
  137.0 0.7 copy-start.6
  158.0 1.0 copy-start.1
  158.5 1.4 copy-start.3
  159.9 2.5 copy-start.2
  161.6 0.8 copy-start
  179.9 0.7 copy-start.6
  200.9 1.0 copy-start.1
  201.4 2.4 copy-start.3
  207.6 21.6 %copy-start.5 = (f32[32,1,3,2304]{3,1,2,0:T(1,128)S(1)}, f32[32,1,3,2304]{3,1,2,0:T(1,128)}, u32[]{:S(2)}) copy-start(f32[32,1,3,2304]{3,1,2,0:T(1,128)} %copy-done.4) | copy-start | bytes 2654212
  263.9 27.5 %all-to-all-start.6 = ((f32[32,1,3,2304]{3,1,2,0:T(1,128)}), f32[32,1,3,2304]{3,1,2,0:T(1,128)S(1)}, u32[]{:S(2)}, u32[]{:S(2)}) async-start(f32[32,1,3,2304]{3,1,2,0:T(1,128)} %broadcast_in_dim.30), calls=%async_computation.6 | async-start | bytes 1769472 | tf_op jit(solution)/shard_map/all_to_all | solution.py:23
where the time goes:
time: 297 us; the launch traced here: 293 us
  blocking collectives  87.9 us (30%)
  matrix products  63.5 us (21%)
  waiting for transfers between devices  53.3 us (18%)
  local copies, waits for them, and re-layouts  30 us (10%)
  loops' own time  25.6 us (9%)
  starting transfers between devices  20.8 us (7%)
  other arithmetic  11.4 us (4%)
    all_to_all x3, blocking collectives, from_everyone(): lax.all_to_all(jnp.broadcast_to(array[None], (devices, *array.shape)), ax...  68.2 us
    dot_general x40, matrix products, contract(): return jnp.einsum(pattern, operand, matrix, precision=full_precision)  62 us
    all_to_all x1, waiting for transfers between devices, per_device(): lax.all_to_all(every_slab, 'grid', split_axis=0, concat_axis=1, tiled=True)  27.6 us
    all_to_all x2, waiting for transfers between devices, from_everyone(): lax.all_to_all(jnp.broadcast_to(array[None], (devices, *array.shape)), ax...  25.6 us
    another operation x1, loops' own time, per_device(): lax.fori_loop(0, blocks * partner_count, pair_step, jnp.zeros_like(own_wh...  25.6 us
    all_to_all x1, blocking collectives, sent_and_summed(): lax.all_to_all(split_up(array, dim, devices), axis, 0, 0, tiled=True)  19.7 us
    all_to_all x2, starting transfers between devices, from_everyone(): lax.all_to_all(jnp.broadcast_to(array[None], (devices, *array.shape)), ax...  13.5 us
    another operation x8, local copies, waits for them, and re-layouts  7.42 us
  transfers between devices with their start and end apart: 3, of which 3 were waited for; matrix products, arithmetic and copies ran while one was open for 3% of the time, Pallas kernels for 0%

commit v1 on v0

v1 whole, which is shorter than its diff:
```python
import math

import jax
import jax.numpy as jnp
import numpy as np
from jax import lax
from jax.experimental import pallas as pl
from jax.experimental.pallas import tpu as pltpu
from jax.sharding import Mesh, PartitionSpec as P

NG = 48
BANDS = 32
COULOMB = 50.0
SLABS = 16
PLANES = NG // SLABS
COLS = NG * NG // 128
ROWS = 56
USED = PLANES * COLS
CHIPS = BANDS // 2
BAND, GRID = ("xl", "z", "c"), ("xh", "y")
PAIR = ("xl", "z")
f32, bf16 = jnp.float32, jnp.bfloat16


def real_basis():
    half = NG // 2
    freq = np.concatenate([np.arange(half + 1), np.arange(1, half)])
    turn = 2.0 * np.pi * ((freq[:, None] * np.arange(NG)[None, :]) % NG) / NG
    wave = np.where(np.arange(NG)[:, None] <= half, np.cos(turn), np.sin(turn))
    norm = np.where((np.arange(NG) == 0) | (np.arange(NG) == half), 1.0, 2.0) / NG
    return wave * np.sqrt(norm)[:, None], freq.astype(np.float64) ** 2


def halves(matrix):
    high = matrix.astype(np.float32).astype(bf16)
    low = (matrix - high.astype(np.float64)).astype(np.float32).astype(bf16)
    return high, low


def from_left(matrix):
    high, low = halves(matrix)
    return np.concatenate([high, high, low], 1)


BASIS, SQUARES = real_basis()
BASIS_X = BASIS[:, [PLANES * (r % SLABS) + r // SLABS for r in range(NG)]]
LEFTS = np.stack([from_left(m) for m in (BASIS_X, BASIS, BASIS.T, BASIS_X.T)])


def last_edge():
    wide = np.zeros((2, NG, 128))
    wide[0, :, :NG] = BASIS.T
    wide[1, :, 64 : 64 + NG] = BASIS.T
    return halves(wide)


LAST_HIGH, LAST_LOW = last_edge()


def split(x):
    high = x.astype(bf16)
    return high, (x - high.astype(f32)).astype(bf16)


def dot(a, b):
    return jnp.dot(a, b, preferred_element_type=f32)


def dot_t(a, b):
    return lax.dot_general(a, b, (((1,), (1,)), ((), ())), preferred_element_type=f32)


def left_mul(matrix, x):
    high, low = split(x)
    return dot(matrix, jnp.concatenate([high, low, high], 0))


def tables_kernel(high_ref, low_ref, wide_high, wide_low, coulomb):
    wide_high[...] = jnp.zeros_like(wide_high)
    wide_low[...] = jnp.zeros_like(wide_low)
    for w in range(2):
        for d in range(2):
            for i in range(4):
                rows = slice(48 * i + 64 * w, 48 * i + 64 * w + 48)
                cols = slice(128 * i, 128 * i + 128)
                wide_high[w, d, rows, cols] = high_ref[d]
                wide_low[w, d, rows, cols] = low_ref[d]

    def square(i):
        freq = jnp.where(i <= NG // 2, i, i - NG // 2).astype(f32)
        return freq * freq

    middle = lax.broadcasted_iota(jnp.int32, (NG, 128), 0)
    lane = lax.broadcasted_iota(jnp.int32, (NG, 128), 1)
    last = jnp.minimum(jnp.where(lane >= 64, lane - 64, lane), NG - 1)
    rest = square(middle) + square(last)
    for k in range(NG):
        total = rest + float(SQUARES[k])
        coulomb[k] = jnp.where(total > 0.0, -COULOMB / jnp.maximum(total, 1.0), 0.0)


def tables():
    wide = jax.ShapeDtypeStruct((2, 2, 256, 512), bf16)
    return pl.pallas_call(
        tables_kernel,
        out_shape=(wide, wide, jax.ShapeDtypeStruct((NG, NG, 128), f32)),
        name="tables",
    )(jnp.asarray(LAST_HIGH), jnp.asarray(LAST_LOW))


def exchange_kernel(
    own_ref, pair_ref, left_ref, wide_high, wide_low, coulomb, out_ref, rho_h, rho_l, za, zb, sol_h, sol_l
):
    def column(ref, first, c):
        return jnp.concatenate(
            [ref[pl.ds(first + COLS * p + c, SLABS, stride=ROWS), :] for p in range(PLANES)], 0
        )

    def place(c):
        return slice(48 * (c // 3), 48 * (c // 3) + 48), slice(128 * (c % 3), 128 * (c % 3) + 128)

    for c in range(COLS):
        own = column(own_ref, 0, c)
        rows, cols = place(c)
        for d in range(2):
            high, low = split(own * column(pair_ref, d * SLABS * ROWS, c))
            rho_h[d, rows, cols] = high
            rho_l[d, rows, cols] = low
    for w in range(2):
        window = slice(128 * w, 128 * w + 256)
        out = None
        for d in range(2):
            high, low = rho_h[d, :, window], rho_l[d, :, window]
            term = dot(high, wide_high[w, d]) + dot(low, wide_high[w, d]) + dot(high, wide_low[w, d])
            out = term if out is None else out + term
        for c in range(6):
            for i in range(4):
                y = 8 * c + 4 * w + i
                za[48 * y : 48 * y + 48, :] = out[48 * c : 48 * c + 48, 128 * i : 128 * i + 128]
    for y in range(0, NG, 2):
        both = jnp.concatenate([za[48 * y : 48 * y + 48, :], za[48 * y + 48 : 48 * y + 96, :]], 1)
        both = left_mul(left_ref[0], both)
        zb[48 * y : 48 * y + 48, :] = both[:, :128]
        zb[48 * y + 48 : 48 * y + 96, :] = both[:, 128:]
    for k in range(0, NG, 2):
        both = jnp.concatenate([zb[pl.ds(k, 48, stride=48), :], zb[pl.ds(k + 1, 48, stride=48), :]], 1)
        both = left_mul(left_ref[1], both) * jnp.concatenate([coulomb[k], coulomb[k + 1]], 1)
        both = left_mul(left_ref[2], both)
        za[pl.ds(k, 48, stride=48), :] = both[:, :128]
        za[pl.ds(k + 1, 48, stride=48), :] = both[:, 128:]
    for y in range(0, NG, 2):
        both = jnp.concatenate([za[48 * y : 48 * y + 48, :], za[48 * y + 48 : 48 * y + 96, :]], 1)
        both = left_mul(left_ref[3], both)
        for e in range(2):
            c, w, i = (y + e) // 8, ((y + e) % 8) // 4, (y + e) % 4
            high, low = split(both[:, 128 * e : 128 * e + 128])
            sol_h[w, 48 * c : 48 * c + 48, 128 * i : 128 * i + 128] = high
            sol_l[w, 48 * c : 48 * c + 48, 128 * i : 128 * i + 128] = low
    thirds = []
    for d in range(2):
        a, b = [
            dot_t(sol_h[w], wide_high[w, d]) + dot_t(sol_l[w], wide_high[w, d]) + dot_t(sol_h[w], wide_low[w, d])
            for w in range(2)
        ]
        thirds.append((a[:, :128], a[:, 128:] + b[:, :128], b[:, 128:]))
    for c in range(COLS):
        rows, _ = place(c)
        out = thirds[0][c % 3][rows] * column(pair_ref, 0, c)
        out = out + thirds[1][c % 3][rows] * column(pair_ref, SLABS * ROWS, c)
        for p in range(PLANES):
            out_ref[pl.ds(COLS * p + c, SLABS, stride=ROWS), :] = out[16 * p : 16 * p + 16]
    for r in range(USED, ROWS):
        out_ref[pl.ds(r, SLABS, stride=ROWS), :] = jnp.zeros((SLABS, 128), f32)


def partial_exchange(own, pair, made):
    big = pltpu.VMEM((NG * NG, 128), f32)
    rho, solved = pltpu.VMEM((2, 288, 384), bf16), pltpu.VMEM((2, 288, 512), bf16)
    return pl.pallas_call(
        exchange_kernel,
        out_shape=jax.ShapeDtypeStruct((SLABS * ROWS, 128), f32),
        scratch_shapes=[rho, rho, big, big, solved, solved],
        name="exchange",
    )(own, pair, jnp.asarray(LEFTS), *made)


def projected_kernel(orbital_ref, field_ref, out_ref):
    def flat(ref):
        return jnp.concatenate([ref[pl.ds(r, BANDS, stride=ROWS), :] for r in range(USED)], 1)

    left_h, left_l = split(flat(orbital_ref))
    right_h, right_l = split(flat(field_ref))
    out = dot_t(left_h, right_h) + dot_t(left_l, right_h) + dot_t(left_h, right_l)
    out_ref[...] = jnp.concatenate([out[8 * q : 8 * q + 8, :] for q in range(4)], 1)


def projected_part(orbitals, fields):
    return pl.pallas_call(
        projected_kernel, out_shape=jax.ShapeDtypeStruct((8, 128), f32), name="projected"
    )(orbitals, fields)


BLOCK = 4


def place_of(band):
    return (band % 2) * CHIPS + band // 2


def finish_kernel(band_ref, parts_ref, field_ref, out_ref, flat):
    band = band_ref[0]
    packed = jnp.sum(parts_ref[...], axis=0)
    matrix = jnp.concatenate([packed[:, 32 * q : 32 * q + 32] for q in range(4)], 0)
    definite = (matrix + matrix.T) * (-0.5 / float(NG**3))
    row = lax.broadcasted_iota(jnp.int32, (BANDS, 2 * BANDS), 0)
    lane = lax.broadcasted_iota(jnp.int32, (BANDS, 2 * BANDS), 1)
    order = 2 * (row % CHIPS) + row // CHIPS
    unit = jnp.where(row[:, :BANDS] == lane[:, :BANDS], 1.0, 0.0).astype(f32)
    state = jnp.concatenate([definite, unit], 1)
    for first in range(0, BANDS, BLOCK):
        at = [place_of(first + i) for i in range(BLOCK)]
        columns = [jnp.broadcast_to(state[:, a : a + 1], (BANDS, 2 * BANDS)) for a in at]
        pivots = [state[a : a + 1, :] for a in at]
        for i in range(BLOCK):
            factor = jnp.where(order > first + i, columns[i] / columns[i][at[i] : at[i] + 1, :], 0.0)
            for j in range(i + 1, BLOCK):
                columns[j] = columns[j] - factor * columns[j][at[i] : at[i] + 1, :]
                pivots[j] = pivots[j] - factor[at[j] : at[j] + 1, :] * pivots[i]
            state = state - factor * pivots[i]
    mine = (band % 2) * CHIPS + band // 2
    picked = jnp.sum(jnp.where(row == mine, state, 0.0), axis=0, keepdims=True)
    pivot = jnp.sum(jnp.where(lane[:1] == mine, picked, 0.0), axis=1, keepdims=True)
    weights = picked * lax.rsqrt(pivot)
    total = None
    for k in range(BANDS):
        weight = weights[:, BANDS + k : BANDS + k + 1]
        term = weight * field_ref[ROWS * k : ROWS * k + ROWS, :]
        total = term if total is None else total + term
    flat[...] = total
    for c in range(COLS):
        out_ref[:, 128 * c : 128 * c + 128] = flat[pl.ds(c, PLANES, stride=COLS), :]


def finish(band, parts, fields):
    vmem = pl.BlockSpec(memory_space=pltpu.VMEM)
    return pl.pallas_call(
        finish_kernel,
        out_shape=jax.ShapeDtypeStruct((PLANES, NG * NG), f32),
        in_specs=[pl.BlockSpec(memory_space=pltpu.SMEM), vmem, vmem],
        scratch_shapes=[pltpu.VMEM((ROWS, 128), f32)],
        name="finish",
    )(band, parts, fields)


def to_everyone(tile, devices, axis):
    return lax.all_to_all(jnp.broadcast_to(tile[None], (devices, *tile.shape)), axis, 0, 0, tiled=True)


def of_every_band(tile):
    chips = to_everyone(tile, CHIPS, PAIR)
    return lax.all_gather(chips, "c", axis=0, tiled=False).reshape(BANDS * ROWS, 128)


def per_device(orbitals):
    tile = jnp.pad(orbitals.reshape(USED, 128), ((0, ROWS - USED), (0, 0)))
    made = tables()
    moves = [
        (b * SLABS + s, (2 * s + b % 2) * SLABS + b // 2) for b in range(BANDS) for s in range(SLABS)
    ]
    partner = lax.ppermute(tile, BAND + GRID, moves)
    own = to_everyone(tile, SLABS, GRID).reshape(SLABS * ROWS, 128)
    pair = of_every_band(partner)
    partial = partial_exchange(own, pair, made)
    all_orbitals = of_every_band(tile)
    shares = lax.all_to_all(partial.reshape(SLABS, ROWS, 128), GRID, 0, 0, tiled=True)
    field = jnp.sum(shares, axis=0)
    all_fields = of_every_band(field)
    parts = to_everyone(projected_part(all_orbitals, all_fields), SLABS, GRID)
    band = lax.axis_index(BAND).astype(jnp.int32).reshape(1)
    return finish(band, parts, all_fields).reshape(1, PLANES, NG * NG)


def solution(mesh):
    parted = Mesh(mesh.devices.reshape(2, 8, 2, 2, 8), BAND + GRID)
    spec = P(BAND, GRID, None)
    return jax.shard_map(per_device, mesh=parted, in_specs=(spec,), out_specs=spec, check_vma=False)
```

time: 297 us -> 153 us (0.52); the launches traced: 293 us -> 152 us
  matrix products: 63.5 us -> 0 us
  waiting for transfers between devices: 53.3 us -> 27 us
  loops' own time: 25.6 us -> 0 us
  local copies, waits for them, and re-layouts: 30 us -> 5.8 us
  Pallas kernels: 0 us -> 15.8 us
  blocking collectives: 87.9 us -> 73.6 us
  other arithmetic: 11.4 us -> 0.85 us
  starting transfers between devices: 20.8 us -> 29.3 us
    dot_general x42 -> x0, matrix products: 63.3 us -> none  [the longest x40 62 us: contract(): return jnp.einsum(pattern, operand, matrix, precision=full_precision)]
    all_to_all x4 -> x2, blocking collectives: 87.9 us -> 55.2 us  [the longest x1 36.9 us: to_everyone(): lax.all_to_all(jnp.broadcast_to(tile[None], (devices, *tile.shape)), axis...]
    all_to_all x3 -> x4, waiting for transfers between devices: 53.3 us -> 27 us  [to_everyone(): lax.all_to_all(jnp.broadcast_to(tile[None], (devices, *tile.shape)), axis...]
    another operation x1 -> x0, loops' own time: 25.6 us -> none  [per_device(): lax.fori_loop(0, blocks * partner_count, pair_step, jnp.zeros_like(own_wh...]
    all_gather x0 -> x3, blocking collectives: none -> 18.4 us  [of_every_band(): lax.all_gather(chips, 'c', axis=0, tiled=False).reshape(BANDS * ROWS, 128)]
    pallas_call x0 -> x4, Pallas kernels: none -> 15.8 us  [the longest x1 6.91 us: partial_exchange(): pl.pallas_call(exchange_kernel, out_shape=jax.ShapeDtypeStruct((SLABS * R...]
    another operation x11 -> x0, local copies, waits for them, and re-layouts: 9.98 us -> none
    all_to_all x3 -> x4, starting transfers between devices: 20.8 us -> 28.7 us  [to_everyone(): lax.all_to_all(jnp.broadcast_to(tile[None], (devices, *tile.shape)), axis...]
  transfers between devices with their start and end apart: 3 -> 5, of which waited for: 3 -> 4; matrix products, arithmetic and copies ran while one was open for 3% -> 0% of each run, Pallas kernels for 0% -> 2%
where the time goes in v1:
time: 153 us; the launch traced here: 152 us
  blocking collectives  73.6 us (48%)
  starting transfers between devices  29.3 us (19%)
  waiting for transfers between devices  27 us (18%)
  Pallas kernels  15.8 us (10%)
  local copies, waits for them, and re-layouts  5.8 us (4%)
    all_to_all x1, blocking collectives, to_everyone(): lax.all_to_all(jnp.broadcast_to(tile[None], (devices, *tile.shape)), axis...  36.9 us
    all_to_all x4, starting transfers between devices, to_everyone(): lax.all_to_all(jnp.broadcast_to(tile[None], (devices, *tile.shape)), axis...  28.7 us
    all_to_all x4, waiting for transfers between devices, to_everyone(): lax.all_to_all(jnp.broadcast_to(tile[None], (devices, *tile.shape)), axis...  27 us
    all_gather x3, blocking collectives, of_every_band(): lax.all_gather(chips, 'c', axis=0, tiled=False).reshape(BANDS * ROWS, 128)  18.4 us
    all_to_all x1, blocking collectives, per_device(): lax.all_to_all(partial.reshape(SLABS, ROWS, 128), GRID, 0, 0, tiled=True)  18.3 us
    pallas_call x1, Pallas kernels, partial_exchange(): pl.pallas_call(exchange_kernel, out_shape=jax.ShapeDtypeStruct((SLABS * R...  6.91 us
    pallas_call x1, Pallas kernels, finish(): pl.pallas_call(finish_kernel, out_shape=jax.ShapeDtypeStruct((PLANES, NG...  3.5 us
  transfers between devices with their start and end apart: 5, of which 4 were waited for; matrix products, arithmetic and copies ran while one was open for 0% of the time, Pallas kernels for 2%

profile of v1, /device:TPU:1, one launch (start us, length us, event | category | flops | bytes accessed | tf_op | source)
XLA Modules:
  0.0 152.5 jit_solution(16082107826005567755)
XLA Ops:
  0.0 0.8 reduce
  0.9 0.7 collective-permute-start
  1.5 0.0 collective-permute-done
  1.6 36.9 %all_to_all.30 = f32[16,56,128]{2,1,0:T(8,128)S(1)} all-to-all(f32[16,56,128]{2,1,0:T(8,128)S(1)} %broadcast_in_dim.9), channel_id=1, replica_groups=mesh['xl'=2,'z'=8,'c'=2,'xh'=2,'y'=8] {'xl','z'}, dimensions={0} | all-to-all | bytes 917504 | tf_op jit(solution)/shard_map/all_to_all | solution.py:256
  38.5 0.8 broadcast_in_dim.8
  39.3 6.3 %all-to-all-start.1 = ((f32[16,56,128]{2,1,0:T(8,128)}), f32[16,56,128]{2,1,0:T(8,128)S(1)}, u32[]{:S(2)}, u32[]{:S(2)}) async-start(f32[16,56,128]{2,1,0:T(8,128)} %broadcast_in_dim.8), calls=%async_computation.1 | async-start | bytes 917504 | tf_op jit(solution)/shard_map/all_to_all | solution.py:256
  45.5 2.6 %tables.1 = (bf16[2,2,256,512]{3,2,1,0:T(8,128)(2,1)}, bf16[2,2,256,512]{3,2,1,0:T(8,128)(2,1)}, f32[48,48,128]{2,1,0:T(8,128)}) custom-call(bf16[2,48,128]{2,1,0:T(8,128)(2,1)} %constant.30.clone.high_ref, bf16[2,48,128]{2,1,0:T(8,128)(2,1)} %constant.31.clone.low_ref), custom_call_target="tpu_custom_call" | custom-call | tf_op jit(solution)/shard_map/tables/pallas_call | solution.py:104
  48.2 5.6 %all-gather.1 = f32[32,56,128]{2,1,0:T(8,128)} all-gather(f32[16,56,128]{2,1,0:T(8,128)S(1)} %all_to_all.30), channel_id=3, replica_groups=mesh['xl'=2,'z'=8,'c'=2,'xh'=2,'y'=8] {'c'}, dimensions={0}, use_global_device_ids=true | all-gather | bytes 1376256 | tf_op jit(solution)/shard_map/all_gather | solution.py:261
  53.8 3.2 %all-to-all-done.1 = f32[16,56,128]{2,1,0:T(8,128)S(1)} async-done(((f32[16,56,128]{2,1,0:T(8,128)}), f32[16,56,128]{2,1,0:T(8,128)S(1)}, u32[]{:S(2)}, u32[]{:S(2)}) %all-to-all-start.1) | async-done | bytes 458784 | tf_op jit(solution)/shard_map/all_to_all | solution.py:256
  57.0 0.0 copy-start
  57.0 0.8 copy-done
  57.8 6.9 %exchange.1 = f32[896,128]{1,0:T(8,128)} custom-call(f32[896,128]{1,0:T(8,128)} %bitcast.11, f32[1792,128]{1,0:T(8,128)} %bitcast.9, bf16[4,48,144]{2,1,0:T(8,128)(2,1)} %constant.32.clone.left_ref, bf16[2,2,256,512]{3,2,1,0:T(8,128)(2,1)} %get-tuple-element.8.wide_high, bf16[2,2,256,512]{3,2,1,0:T(8,128)(2,1)} %get-tuple-element.9.wide_low, ...), custom_call_target="tpu_custom_call" | custom-call | tf_op jit(solution)/shard_map/exchange/pallas_call | solution.py:179
  64.7 18.3 %all_to_all.31 = f32[16,56,128]{2,1,0:T(8,128)S(1)} all-to-all(f32[16,56,128]{2,1,0:T(8,128)} %bitcast.12), channel_id=1, replica_groups=mesh['xl'=2,'z'=8,'c'=2,'xh'=2,'y'=8] {'xh','y'}, dimensions={0} | all-to-all | bytes 917504 | tf_op jit(solution)/shard_map/all_to_all | solution.py:275
  83.0 8.5 %all-to-all-start = ((f32[16,56,128]{2,1,0:T(8,128)}), f32[16,56,128]{2,1,0:T(8,128)S(1)}, u32[]{:S(2)}, u32[]{:S(2)}) async-start(f32[16,56,128]{2,1,0:T(8,128)} %broadcast_in_dim.8), calls=%async_computation | async-start | bytes 917504 | tf_op jit(solution)/shard_map/all_to_all | solution.py:256
  91.6 10.0 %all-to-all-done = f32[16,56,128]{2,1,0:T(8,128)S(1)} async-done(((f32[16,56,128]{2,1,0:T(8,128)}), f32[16,56,128]{2,1,0:T(8,128)S(1)}, u32[]{:S(2)}, u32[]{:S(2)}) %all-to-all-start) | async-done | bytes 458784 | tf_op jit(solution)/shard_map/all_to_all | solution.py:256
  101.6 0.8 broadcast_in_dim.10
  102.4 6.8 %all-to-all-start.4 = ((f32[16,56,128]{2,1,0:T(8,128)}), f32[16,56,128]{2,1,0:T(8,128)S(1)}, u32[]{:S(2)}, u32[]{:S(2)}) async-start(f32[16,56,128]{2,1,0:T(8,128)} %broadcast_in_dim.10), calls=%async_computation.4 | async-start | bytes 917504 | tf_op jit(solution)/shard_map/all_to_all | solution.py:256
  109.2 5.2 %all-gather = f32[32,56,128]{2,1,0:T(8,128)} all-gather(f32[16,56,128]{2,1,0:T(8,128)S(1)} %all-to-all-done), channel_id=2, replica_groups=mesh['xl'=2,'z'=8,'c'=2,'xh'=2,'y'=8] {'c'}, dimensions={0}, use_global_device_ids=true | all-gather | bytes 1376256 | tf_op jit(solution)/shard_map/all_gather | solution.py:261
  114.4 4.9 %all-to-all-done.4 = f32[16,56,128]{2,1,0:T(8,128)S(1)} async-done(((f32[16,56,128]{2,1,0:T(8,128)}), f32[16,56,128]{2,1,0:T(8,128)S(1)}, u32[]{:S(2)}, u32[]{:S(2)}) %all-to-all-start.4) | async-done | bytes 458784 | tf_op jit(solution)/shard_map/all_to_all | solution.py:256
  119.3 7.6 %all-gather.2 = f32[32,56,128]{2,1,0:T(8,128)} all-gather(f32[16,56,128]{2,1,0:T(8,128)S(1)} %all-to-all-done.4), channel_id=4, replica_groups=mesh['xl'=2,'z'=8,'c'=2,'xh'=2,'y'=8] {'c'}, dimensions={0}, use_global_device_ids=true | all-gather | bytes 1376256 | tf_op jit(solution)/shard_map/all_gather | solution.py:261
  126.8 2.8 %projected.1 = f32[8,128]{1,0:T(8,128)} custom-call(f32[1792,128]{1,0:T(8,128)} %bitcast.10, f32[1792,128]{1,0:T(8,128)} %bitcast.7), custom_call_target="tpu_custom_call" | custom-call | tf_op jit(solution)/shard_map/projected/pallas_call | solution.py:198
  129.6 1.3 broadcast_in_dim.11
  131.0 7.1 %all-to-all-start.5 = ((f32[16,8,128]{2,1,0:T(8,128)}), f32[16,8,128]{2,1,0:T(8,128)S(1)}, u32[]{:S(2)}, u32[]{:S(2)}) async-start(f32[16,8,128]{2,1,0:T(8,128)} %broadcast_in_dim.11), calls=%async_computation.5 | async-start | bytes 131072 | tf_op jit(solution)/shard_map/all_to_all | solution.py:256
  138.1 8.9 %all-to-all-done.5.parts_ref = f32[16,8,128]{2,1,0:T(8,128)S(1)} async-done(((f32[16,8,128]{2,1,0:T(8,128)}), f32[16,8,128]{2,1,0:T(8,128)S(1)}, u32[]{:S(2)}, u32[]{:S(2)}) %all-to-all-start.5) | async-done | bytes 65568 | tf_op jit(solution)/shard_map/all_to_all | solution.py:256
  147.0 0.0 copy-start.1
  147.0 0.6 copy-done.1
  147.6 3.5 %finish.1 = f32[3,2304]{1,0:T(4,128)} custom-call(s32[1]{0:T(128)} %bitcast.band_ref, f32[16,8,128]{2,1,0:T(8,128)} %copy-done.1, f32[1792,128]{1,0:T(8,128)} %bitcast.8), custom_call_target="tpu_custom_call" | custom-call | tf_op jit(solution)/shard_map/finish/pallas_call | solution.py:246
  151.1 1.4 copy.6
  (4 shorter events, 0.1 us)
Async XLA Ops:
  0.9 0.7 collective-permute-start
  39.3 17.8 %all-to-all-start.1 = ((f32[16,56,128]{2,1,0:T(8,128)}), f32[16,56,128]{2,1,0:T(8,128)S(1)}, u32[]{:S(2)}, u32[]{:S(2)}) async-start(f32[16,56,128]{2,1,0:T(8,128)} %broadcast_in_dim.8), calls=%async_computation.1 | async-start | bytes 917504 | tf_op jit(solution)/shard_map/all_to_all | solution.py:256
  57.0 0.8 copy-start
  83.0 18.6 %all-to-all-start = ((f32[16,56,128]{2,1,0:T(8,128)}), f32[16,56,128]{2,1,0:T(8,128)S(1)}, u32[]{:S(2)}, u32[]{:S(2)}) async-start(f32[16,56,128]{2,1,0:T(8,128)} %broadcast_in_dim.8), calls=%async_computation | async-start | bytes 917504 | tf_op jit(solution)/shard_map/all_to_all | solution.py:256
  102.4 16.9 %all-to-all-start.4 = ((f32[16,56,128]{2,1,0:T(8,128)}), f32[16,56,128]{2,1,0:T(8,128)S(1)}, u32[]{:S(2)}, u32[]{:S(2)}) async-start(f32[16,56,128]{2,1,0:T(8,128)} %broadcast_in_dim.10), calls=%async_computation.4 | async-start | bytes 917504 | tf_op jit(solution)/shard_map/all_to_all | solution.py:256
  131.0 16.0 %all-to-all-start.5 = ((f32[16,8,128]{2,1,0:T(8,128)}), f32[16,8,128]{2,1,0:T(8,128)S(1)}, u32[]{:S(2)}, u32[]{:S(2)}) async-start(f32[16,8,128]{2,1,0:T(8,128)} %broadcast_in_dim.11), calls=%async_computation.5 | async-start | bytes 131072 | tf_op jit(solution)/shard_map/all_to_all | solution.py:256
  147.0 0.6 copy-start.1

commit v2 on v1

--- a/solution.py
+++ b/solution.py
@@ -184,20 +184,53 @@
     )(own, pair, jnp.asarray(LEFTS), *made)
 
 
-def projected_kernel(orbital_ref, field_ref, out_ref):
-    def flat(ref):
-        return jnp.concatenate([ref[pl.ds(r, BANDS, stride=ROWS), :] for r in range(USED)], 1)
-
-    left_h, left_l = split(flat(orbital_ref))
-    right_h, right_l = split(flat(field_ref))
-    out = dot_t(left_h, right_h) + dot_t(left_l, right_h) + dot_t(left_h, right_l)
-    out_ref[...] = jnp.concatenate([out[8 * q : 8 * q + 8, :] for q in range(4)], 1)
-
-
-def projected_part(orbitals, fields):
-    return pl.pallas_call(
-        projected_kernel, out_shape=jax.ShapeDtypeStruct((8, 128), f32), name="projected"
-    )(orbitals, fields)
+def prepare_kernel(slab_ref, tile_ref, copies_ref):
+    tile_ref[USED:ROWS, :] = jnp.zeros((ROWS - USED, 128), f32)
+    for p in range(PLANES):
+        for c in range(COLS):
+            r = COLS * p + c
+            tile_ref[r : r + 1, :] = slab_ref[p, :, 128 * c : 128 * c + 128]
+    tile = tile_ref[...]
+    for k in range(SLABS):
+        copies_ref[k] = tile
+
+
+def prepare(slab):
+    tile = jax.ShapeDtypeStruct((ROWS, 128), f32)
+    copies = jax.ShapeDtypeStruct((SLABS, ROWS, 128), f32)
+    return pl.pallas_call(prepare_kernel, out_shape=(tile, copies), name="prepare")(slab)
+
+
+def column_kernel(share_ref, orbital_ref, field_ref, copies_ref):
+    field = jnp.sum(share_ref[...], axis=0)
+    field_ref[...] = field
+    sums = [
+        jnp.sum(field * orbital_ref[ROWS * k : ROWS * k + ROWS, :], axis=0, keepdims=True) for k in range(BANDS)
+    ]
+    high, low = split(jnp.concatenate(sums + [jnp.zeros((128 - BANDS, 128), f32)], 0))
+    ones = jnp.ones((8, 128), bf16)
+    line = dot_t(ones, high) + dot_t(ones, low)
+    for k in range(SLABS):
+        copies_ref[k] = line
+
+
+def column_part(shares, orbitals):
+    field = jax.ShapeDtypeStruct((ROWS, 128), f32)
+    copies = jax.ShapeDtypeStruct((SLABS, 8, 128), f32)
+    return pl.pallas_call(column_kernel, out_shape=(field, copies), name="column")(shares, orbitals)
+
+
+def attach_kernel(field_ref, parts_ref, copies_ref):
+    column = jnp.sum(parts_ref[...], axis=0)[:1]
+    row = lax.broadcasted_iota(jnp.int32, (ROWS, 128), 0)
+    tile = jnp.where(row == USED, column, field_ref[...])
+    for k in range(CHIPS):
+        copies_ref[k] = tile
+
+
+def attach(field, parts):
+    copies = jax.ShapeDtypeStruct((CHIPS, ROWS, 128), f32)
+    return pl.pallas_call(attach_kernel, out_shape=copies, name="attach")(field, parts)
 
 
 BLOCK = 4
@@ -207,10 +240,9 @@
     return (band % 2) * CHIPS + band // 2
 
 
-def finish_kernel(band_ref, parts_ref, field_ref, out_ref, flat):
+def finish_kernel(band_ref, field_ref, out_ref, flat):
     band = band_ref[0]
-    packed = jnp.sum(parts_ref[...], axis=0)
-    matrix = jnp.concatenate([packed[:, 32 * q : 32 * q + 32] for q in range(4)], 0)
+    matrix = field_ref[pl.ds(USED, BANDS, stride=ROWS), :][:, :BANDS]
     definite = (matrix + matrix.T) * (-0.5 / float(NG**3))
     row = lax.broadcasted_iota(jnp.int32, (BANDS, 2 * BANDS), 0)
     lane = lax.broadcasted_iota(jnp.int32, (BANDS, 2 * BANDS), 1)
@@ -237,47 +269,50 @@
         term = weight * field_ref[ROWS * k : ROWS * k + ROWS, :]
         total = term if total is None else total + term
     flat[...] = total
-    for c in range(COLS):
-        out_ref[:, 128 * c : 128 * c + 128] = flat[pl.ds(c, PLANES, stride=COLS), :]
-
-
-def finish(band, parts, fields):
-    vmem = pl.BlockSpec(memory_space=pltpu.VMEM)
+    for p in range(PLANES):
+        for c in range(COLS):
+            r = COLS * p + c
+            out_ref[p, :, 128 * c : 128 * c + 128] = flat[r : r + 1, :]
+
+
+def finish(band, fields):
     return pl.pallas_call(
         finish_kernel,
-        out_shape=jax.ShapeDtypeStruct((PLANES, NG * NG), f32),
-        in_specs=[pl.BlockSpec(memory_space=pltpu.SMEM), vmem, vmem],
+        out_shape=jax.ShapeDtypeStruct((PLANES, 1, NG * NG), f32),
+        in_specs=[pl.BlockSpec(memory_space=pltpu.SMEM), pl.BlockSpec(memory_space=pltpu.VMEM)],
         scratch_shapes=[pltpu.VMEM((ROWS, 128), f32)],
         name="finish",
-    )(band, parts, fields)
-
-
-def to_everyone(tile, devices, axis):
-    return lax.all_to_all(jnp.broadcast_to(tile[None], (devices, *tile.shape)), axis, 0, 0, tiled=True)
-
-
-def of_every_band(tile):
-    chips = to_everyone(tile, CHIPS, PAIR)
+    )(band, fields)
+
+
+def exchange_tiles(tiles, axis):
+    return lax.all_to_all(tiles, axis, 0, 0, tiled=True)
+
+
+def both_cores(chips):
     return lax.all_gather(chips, "c", axis=0, tiled=False).reshape(BANDS * ROWS, 128)
 
 
 def per_device(orbitals):
-    tile = jnp.pad(orbitals.reshape(USED, 128), ((0, ROWS - USED), (0, 0)))
+    tile, copies = prepare(jnp.transpose(orbitals, (1, 0, 2)))
     made = tables()
     moves = [
         (b * SLABS + s, (2 * s + b % 2) * SLABS + b // 2) for b in range(BANDS) for s in range(SLABS)
     ]
     partner = lax.ppermute(tile, BAND + GRID, moves)
-    own = to_everyone(tile, SLABS, GRID).reshape(SLABS * ROWS, 128)
-    pair = of_every_band(partner)
-    partial = partial_exchange(own, pair, made)
-    all_orbitals = of_every_band(tile)
-    shares = lax.all_to_all(partial.reshape(SLABS, ROWS, 128), GRID, 0, 0, tiled=True)
-    field = jnp.sum(shares, axis=0)
-    all_fields = of_every_band(field)
-    parts = to_everyone(projected_part(all_orbitals, all_fields), SLABS, GRID)
+    own = exchange_tiles(copies, GRID)
+    own, partner = lax.optimization_barrier((own, partner))
+    pair = exchange_tiles(jnp.broadcast_to(partner[None], copies.shape), PAIR)
+    pair, copies = lax.optimization_barrier((pair, copies))
+    slab_orbitals = exchange_tiles(copies, PAIR)
+    partial = partial_exchange(own.reshape(SLABS * ROWS, 128), both_cores(pair), made)
+    partial, slab_orbitals = lax.optimization_barrier((partial, slab_orbitals))
+    shares = exchange_tiles(partial.reshape(SLABS, ROWS, 128), GRID)
+    field, lines = column_part(shares, both_cores(slab_orbitals))
+    parts = exchange_tiles(lines, GRID)
+    fields = both_cores(exchange_tiles(attach(field, parts), PAIR))
     band = lax.axis_index(BAND).astype(jnp.int32).reshape(1)
-    return finish(band, parts, all_fields).reshape(1, PLANES, NG * NG)
+    return jnp.transpose(finish(band, fields), (1, 0, 2))
 
 
 def solution(mesh):

time: 153 us -> 139 us (0.908)
  blocking collectives: 73.6 us -> 51.4 us
  starting transfers between devices: 29.3 us -> 35.3 us
  waiting for transfers between devices: 27 us -> 32.4 us
  local copies, waits for them, and re-layouts: 5.8 us -> 0.82 us
  Pallas kernels: 15.8 us -> 18.3 us
    all_to_all x2, blocking collectives: 55.2 us -> 36.4 us  [exchange_tiles(): return lax.all_to_all(tiles, axis, 0, 0, tiled=True)]
    all_to_all x4, waiting for transfers between devices: 27 us -> 32.4 us  [exchange_tiles(): return lax.all_to_all(tiles, axis, 0, 0, tiled=True)]
    all_to_all x4, starting transfers between devices: 28.7 us -> 33.9 us  [exchange_tiles(): return lax.all_to_all(tiles, axis, 0, 0, tiled=True)]
    all_gather x3, blocking collectives: 18.4 us -> 15 us  [both_cores(): lax.all_gather(chips, 'c', axis=0, tiled=False).reshape(BANDS * ROWS, 128)]
    broadcast_in_dim x4 -> x1, local copies, waits for them, and re-layouts: 2.95 us -> 0.03 us  [per_device(): pair = exchange_tiles(jnp.broadcast_to(partner[None], copies.shape), PAIR)]
    pallas_call x2 -> x4, Pallas kernels: 6.31 us -> 8.82 us  [the longest x1 3.39 us: finish(): pl.pallas_call(finish_kernel, out_shape=jax.ShapeDtypeStruct((PLANES, 1,...]
  transfers between devices with their start and end apart: 5 -> 5, of which waited for: 4 -> 3; matrix products, arithmetic and copies ran while one was open for 0% -> 0% of each run, Pallas kernels for 2% -> 7%
where the time goes in v2:
time: 139 us; the launch traced here: 138 us
  blocking collectives  51.4 us (37%)
  starting transfers between devices  35.3 us (25%)
  waiting for transfers between devices  32.4 us (23%)
  Pallas kernels  18.3 us (13%)
    all_to_all x2, blocking collectives, exchange_tiles(): return lax.all_to_all(tiles, axis, 0, 0, tiled=True)  36.4 us
    all_to_all x4, starting transfers between devices, exchange_tiles(): return lax.all_to_all(tiles, axis, 0, 0, tiled=True)  33.9 us
    all_to_all x4, waiting for transfers between devices, exchange_tiles(): return lax.all_to_all(tiles, axis, 0, 0, tiled=True)  32.4 us
    all_gather x3, blocking collectives, both_cores(): lax.all_gather(chips, 'c', axis=0, tiled=False).reshape(BANDS * ROWS, 128)  15 us
    pallas_call x1, Pallas kernels, partial_exchange(): pl.pallas_call(exchange_kernel, out_shape=jax.ShapeDtypeStruct((SLABS * R...  6.9 us
    pallas_call x1, Pallas kernels, finish(): pl.pallas_call(finish_kernel, out_shape=jax.ShapeDtypeStruct((PLANES, 1,...  3.39 us
  transfers between devices with their start and end apart: 5, of which 3 were waited for; matrix products, arithmetic and copies ran while one was open for 0% of the time, Pallas kernels for 7%

profile of v2, /device:TPU:1, one launch (start us, length us, event | category | flops | bytes accessed | tf_op | source)
XLA Modules:
  0.0 138.3 jit_solution(16034587056568578533)
XLA Ops:
  0.0 1.6 %prepare.1 = (f32[56,128]{1,0:T(8,128)}, f32[16,56,128]{2,1,0:T(8,128)}) custom-call(f32[3,1,2304]{2,1,0:T(1,128)} %bitcast.13), custom_call_target="tpu_custom_call" | custom-call | tf_op jit(solution)/shard_map/prepare/pallas_call | solution.py:201
  1.6 10.2 %all-to-all-start = ((f32[16,56,128]{2,1,0:T(8,128)}), f32[16,56,128]{2,1,0:T(8,128)S(1)}, u32[]{:S(2)}, u32[]{:S(2)}) async-start(f32[16,56,128]{2,1,0:T(8,128)} %get-tuple-element.26), calls=%async_computation | async-start | bytes 917504 | tf_op jit(solution)/shard_map/all_to_all | solution.py:289
  11.8 1.4 %collective-permute-start = (f32[56,128]{1,0:T(8,128)}, f32[56,128]{1,0:T(8,128)S(1)}, u32[]{:S(2)}, u32[]{:S(2)}) collective-permute-start(f32[56,128]{1,0:T(8,128)} %get-tuple-element.19), channel_id=1, source_target_pairs={{0,0},{1,32},{2,64},{3,96},{4,128},{5,160},{6,192},{7,224},{8,256}... | collective-permute-start | bytes 86024 | tf_op jit(solution)/shard_map/ppermute | solution.py:302
  13.2 0.0 collective-permute-done
  13.2 12.0 %all-to-all-done = f32[16,56,128]{2,1,0:T(8,128)S(1)} async-done(((f32[16,56,128]{2,1,0:T(8,128)}), f32[16,56,128]{2,1,0:T(8,128)S(1)}, u32[]{:S(2)}, u32[]{:S(2)}) %all-to-all-start) | async-done | bytes 458784 | tf_op jit(solution)/shard_map/all_to_all | solution.py:289
  25.2 0.0 copy-start
  25.2 21.3 %all_to_all.30 = f32[16,56,128]{2,1,0:T(8,128)S(1)} all-to-all(f32[16,56,128]{2,1,0:T(8,128)S(1)} %broadcast_in_dim.2), channel_id=1, replica_groups=mesh['xl'=2,'z'=8,'c'=2,'xh'=2,'y'=8] {'xl','z'}, dimensions={0} | all-to-all | bytes 917504 | tf_op jit(solution)/shard_map/all_to_all | solution.py:289
  46.5 6.8 %all-to-all-start.2 = ((f32[16,56,128]{2,1,0:T(8,128)}), f32[16,56,128]{2,1,0:T(8,128)S(1)}, u32[]{:S(2)}, u32[]{:S(2)}) async-start(f32[16,56,128]{2,1,0:T(8,128)} %get-tuple-element.26), calls=%async_computation.2 | async-start | bytes 917504 | tf_op jit(solution)/shard_map/all_to_all | solution.py:289
  53.4 2.6 %tables.1 = (bf16[2,2,256,512]{3,2,1,0:T(8,128)(2,1)}, bf16[2,2,256,512]{3,2,1,0:T(8,128)(2,1)}, f32[48,48,128]{2,1,0:T(8,128)}) custom-call(bf16[2,48,128]{2,1,0:T(8,128)(2,1)} %constant.26.clone.high_ref, bf16[2,48,128]{2,1,0:T(8,128)(2,1)} %constant.27.clone.low_ref), custom_call_target="tpu_custom_call" | custom-call | tf_op jit(solution)/shard_map/tables/pallas_call | solution.py:104
  56.0 0.0 copy-done
  56.0 5.1 %all-gather = f32[32,56,128]{2,1,0:T(8,128)} all-gather(f32[16,56,128]{2,1,0:T(8,128)S(1)} %all_to_all.30), channel_id=2, replica_groups=mesh['xl'=2,'z'=8,'c'=2,'xh'=2,'y'=8] {'c'}, dimensions={0}, use_global_device_ids=true | all-gather | bytes 1376256 | tf_op jit(solution)/shard_map/all_gather | solution.py:293
  61.1 6.9 %exchange.1 = f32[896,128]{1,0:T(8,128)} custom-call(f32[896,128]{1,0:T(8,128)} %bitcast.11, f32[1792,128]{1,0:T(8,128)} %bitcast.8, bf16[4,48,144]{2,1,0:T(8,128)(2,1)} %constant.28.clone.left_ref, bf16[2,2,256,512]{3,2,1,0:T(8,128)(2,1)} %get-tuple-element.23.wide_high, bf16[2,2,256,512]{3,2,1,0:T(8,128)(2,1)} %get-tuple-element.24.wide_low, ...), custom_call_target="tpu_custom_call" | custom-call | tf_op jit(solution)/shard_map/exchange/pallas_call | solution.py:179
  68.0 0.0 all-to-all-done.2
  68.0 8.8 %all-to-all-start.3 = ((f32[16,56,128]{2,1,0:T(8,128)}), f32[16,56,128]{2,1,0:T(8,128)S(1)}, u32[]{:S(2)}, u32[]{:S(2)}) async-start(f32[16,56,128]{2,1,0:T(8,128)} %bitcast.12), calls=%async_computation.3 | async-start | bytes 917504 | tf_op jit(solution)/shard_map/all_to_all | solution.py:289
  76.8 3.7 %all-gather.1 = f32[32,56,128]{2,1,0:T(8,128)} all-gather(f32[16,56,128]{2,1,0:T(8,128)S(1)} %all-to-all-done.2), channel_id=3, replica_groups=mesh['xl'=2,'z'=8,'c'=2,'xh'=2,'y'=8] {'c'}, dimensions={0}, use_global_device_ids=true | all-gather | bytes 1376256 | tf_op jit(solution)/shard_map/all_gather | solution.py:293
  80.5 9.5 %all-to-all-done.3.share_ref = f32[16,56,128]{2,1,0:T(8,128)S(1)} async-done(((f32[16,56,128]{2,1,0:T(8,128)}), f32[16,56,128]{2,1,0:T(8,128)S(1)}, u32[]{:S(2)}, u32[]{:S(2)}) %all-to-all-start.3) | async-done | bytes 458784 | tf_op jit(solution)/shard_map/all_to_all | solution.py:289
  90.0 0.0 copy-start.1
  90.0 0.8 copy-done.1
  90.8 2.2 %column.1 = (f32[56,128]{1,0:T(8,128)}, f32[16,8,128]{2,1,0:T(8,128)}) custom-call(f32[16,56,128]{2,1,0:T(8,128)} %copy-done.1, f32[1792,128]{1,0:T(8,128)} %bitcast.9), custom_call_target="tpu_custom_call" | custom-call | tf_op jit(solution)/shard_map/column/pallas_call | solution.py:220
  93.0 15.1 %all_to_all.31.parts_ref = f32[16,8,128]{2,1,0:T(8,128)} all-to-all(f32[16,8,128]{2,1,0:T(8,128)} %get-tuple-element.30), channel_id=1, replica_groups=mesh['xl'=2,'z'=8,'c'=2,'xh'=2,'y'=8] {'xh','y'}, dimensions={0} | all-to-all | bytes 131072 | tf_op jit(solution)/shard_map/all_to_all | solution.py:289
  108.1 1.7 %attach.1 = f32[16,56,128]{2,1,0:T(8,128)} custom-call(f32[56,128]{1,0:T(8,128)} %get-tuple-element.29.field_ref, f32[16,8,128]{2,1,0:T(8,128)} %all_to_all.31.parts_ref), custom_call_target="tpu_custom_call" | custom-call | tf_op jit(solution)/shard_map/attach/pallas_call | solution.py:233
  109.8 8.1 %all-to-all-start.5 = ((f32[16,56,128]{2,1,0:T(8,128)}), f32[16,56,128]{2,1,0:T(8,128)S(1)}, u32[]{:S(2)}, u32[]{:S(2)}) async-start(f32[16,56,128]{2,1,0:T(8,128)} %attach.1), calls=%async_computation.5 | async-start | bytes 917504 | tf_op jit(solution)/shard_map/all_to_all | solution.py:289
  117.9 10.8 %all-to-all-done.5 = f32[16,56,128]{2,1,0:T(8,128)S(1)} async-done(((f32[16,56,128]{2,1,0:T(8,128)}), f32[16,56,128]{2,1,0:T(8,128)S(1)}, u32[]{:S(2)}, u32[]{:S(2)}) %all-to-all-start.5) | async-done | bytes 458784 | tf_op jit(solution)/shard_map/all_to_all | solution.py:289
  128.7 6.2 %all-gather.2 = f32[32,56,128]{2,1,0:T(8,128)} all-gather(f32[16,56,128]{2,1,0:T(8,128)S(1)} %all-to-all-done.5), channel_id=4, replica_groups=mesh['xl'=2,'z'=8,'c'=2,'xh'=2,'y'=8] {'c'}, dimensions={0}, use_global_device_ids=true | all-gather | bytes 1376256 | tf_op jit(solution)/shard_map/all_gather | solution.py:293
  135.0 3.4 %finish.1 = f32[3,1,2304]{2,1,0:T(1,128)} custom-call(s32[1]{0:T(128)} %bitcast.band_ref, f32[1792,128]{1,0:T(8,128)} %bitcast.10), custom_call_target="tpu_custom_call" | custom-call | tf_op jit(solution)/shard_map/finish/pallas_call | solution.py:279
  (1 shorter events, 0.0 us)
Async XLA Ops:
  1.6 23.6 %all-to-all-start = ((f32[16,56,128]{2,1,0:T(8,128)}), f32[16,56,128]{2,1,0:T(8,128)S(1)}, u32[]{:S(2)}, u32[]{:S(2)}) async-start(f32[16,56,128]{2,1,0:T(8,128)} %get-tuple-element.26), calls=%async_computation | async-start | bytes 917504 | tf_op jit(solution)/shard_map/all_to_all | solution.py:289
  11.8 1.4 %collective-permute-start = (f32[56,128]{1,0:T(8,128)}, f32[56,128]{1,0:T(8,128)S(1)}, u32[]{:S(2)}, u32[]{:S(2)}) collective-permute-start(f32[56,128]{1,0:T(8,128)} %get-tuple-element.19), channel_id=1, source_target_pairs={{0,0},{1,32},{2,64},{3,96},{4,128},{5,160},{6,192},{7,224},{8,256}... | collective-permute-start | bytes 86024 | tf_op jit(solution)/shard_map/ppermute | solution.py:302
  25.2 30.8 %copy-start = (f32[16,56,128]{2,1,0:T(8,128)}, f32[16,56,128]{2,1,0:T(8,128)S(1)}, u32[]{:S(2)}) copy-start(f32[16,56,128]{2,1,0:T(8,128)S(1)} %all-to-all-done) | copy-start | bytes 1376260
  46.5 21.5 %all-to-all-start.2 = ((f32[16,56,128]{2,1,0:T(8,128)}), f32[16,56,128]{2,1,0:T(8,128)S(1)}, u32[]{:S(2)}, u32[]{:S(2)}) async-start(f32[16,56,128]{2,1,0:T(8,128)} %get-tuple-element.26), calls=%async_computation.2 | async-start | bytes 917504 | tf_op jit(solution)/shard_map/all_to_all | solution.py:289
  68.0 22.0 %all-to-all-start.3 = ((f32[16,56,128]{2,1,0:T(8,128)}), f32[16,56,128]{2,1,0:T(8,128)S(1)}, u32[]{:S(2)}, u32[]{:S(2)}) async-start(f32[16,56,128]{2,1,0:T(8,128)} %bitcast.12), calls=%async_computation.3 | async-start | bytes 917504 | tf_op jit(solution)/shard_map/all_to_all | solution.py:289
  90.0 0.8 copy-start.1
  109.8 19.0 %all-to-all-start.5 = ((f32[16,56,128]{2,1,0:T(8,128)}), f32[16,56,128]{2,1,0:T(8,128)S(1)}, u32[]{:S(2)}, u32[]{:S(2)}) async-start(f32[16,56,128]{2,1,0:T(8,128)} %attach.1), calls=%async_computation.5 | async-start | bytes 917504 | tf_op jit(solution)/shard_map/all_to_all | solution.py:289

commit v3 on v2

--- a/solution.py
+++ b/solution.py
@@ -17,9 +17,11 @@
 ROWS = 56
 USED = PLANES * COLS
 CHIPS = BANDS // 2
-BAND, GRID = ("xl", "z", "c"), ("xh", "y")
-PAIR = ("xl", "z")
+PAIR, CORE, GRID = ("xl", "z4", "z2", "z1"), ("c",), ("xh", "y4", "y2", "y1")
+BAND = PAIR + CORE
 f32, bf16 = jnp.float32, jnp.bfloat16
+SMALL = pltpu.CompilerParams(vmem_limit_bytes=12 << 20)
+LARGE = pltpu.CompilerParams(vmem_limit_bytes=24 << 20)
 
 
 def real_basis():
@@ -105,6 +107,7 @@
         tables_kernel,
         out_shape=(wide, wide, jax.ShapeDtypeStruct((NG, NG, 128), f32)),
         name="tables",
+        compiler_params=SMALL,
     )(jnp.asarray(LAST_HIGH), jnp.asarray(LAST_LOW))
 
 
@@ -116,6 +119,9 @@
             [ref[pl.ds(first + COLS * p + c, SLABS, stride=ROWS), :] for p in range(PLANES)], 0
         )
 
+    def partner(d, c):
+        return column(pair_ref, d * SLABS * ROWS, c)
+
     def place(c):
         return slice(48 * (c // 3), 48 * (c // 3) + 48), slice(128 * (c % 3), 128 * (c % 3) + 128)
 
@@ -123,7 +129,7 @@
         own = column(own_ref, 0, c)
         rows, cols = place(c)
         for d in range(2):
-            high, low = split(own * column(pair_ref, d * SLABS * ROWS, c))
+            high, low = split(own * partner(d, c))
             rho_h[d, rows, cols] = high
             rho_l[d, rows, cols] = low
     for w in range(2):
@@ -165,8 +171,8 @@
         thirds.append((a[:, :128], a[:, 128:] + b[:, :128], b[:, 128:]))
     for c in range(COLS):
         rows, _ = place(c)
-        out = thirds[0][c % 3][rows] * column(pair_ref, 0, c)
-        out = out + thirds[1][c % 3][rows] * column(pair_ref, SLABS * ROWS, c)
+        out = thirds[0][c % 3][rows] * partner(0, c)
+        out = out + thirds[1][c % 3][rows] * partner(1, c)
         for p in range(PLANES):
             out_ref[pl.ds(COLS * p + c, SLABS, stride=ROWS), :] = out[16 * p : 16 * p + 16]
     for r in range(USED, ROWS):
@@ -181,6 +187,7 @@
         out_shape=jax.ShapeDtypeStruct((SLABS * ROWS, 128), f32),
         scratch_shapes=[rho, rho, big, big, solved, solved],
         name="exchange",
+        compiler_params=LARGE,
     )(own, pair, jnp.asarray(LEFTS), *made)
 
 
@@ -198,39 +205,38 @@
 def prepare(slab):
     tile = jax.ShapeDtypeStruct((ROWS, 128), f32)
     copies = jax.ShapeDtypeStruct((SLABS, ROWS, 128), f32)
-    return pl.pallas_call(prepare_kernel, out_shape=(tile, copies), name="prepare")(slab)
-
-
-def column_kernel(share_ref, orbital_ref, field_ref, copies_ref):
+    return pl.pallas_call(prepare_kernel, out_shape=(tile, copies), name="prepare", compiler_params=SMALL)(slab)
+
+
+def column_kernel(share_ref, orbital_ref, line_ref, copies_ref):
     field = jnp.sum(share_ref[...], axis=0)
-    field_ref[...] = field
+    for k in range(CHIPS):
+        copies_ref[k] = field
     sums = [
         jnp.sum(field * orbital_ref[ROWS * k : ROWS * k + ROWS, :], axis=0, keepdims=True) for k in range(BANDS)
     ]
     high, low = split(jnp.concatenate(sums + [jnp.zeros((128 - BANDS, 128), f32)], 0))
     ones = jnp.ones((8, 128), bf16)
-    line = dot_t(ones, high) + dot_t(ones, low)
+    line_ref[...] = (dot_t(ones, high) + dot_t(ones, low))[:1]
+
+
+def column_part(shares, orbitals):
+    line = jax.ShapeDtypeStruct((1, 128), f32)
+    copies = jax.ShapeDtypeStruct((CHIPS, ROWS, 128), f32)
+    return pl.pallas_call(
+        column_kernel, out_shape=(line, copies), name="column", compiler_params=SMALL
+    )(shares, orbitals)
+
+
+def pack_kernel(column_ref, copies_ref):
+    packed = jnp.concatenate([column_ref[8 * q : 8 * q + 8, :BANDS] for q in range(4)], 1)
     for k in range(SLABS):
-        copies_ref[k] = line
-
-
-def column_part(shares, orbitals):
-    field = jax.ShapeDtypeStruct((ROWS, 128), f32)
+        copies_ref[k] = packed
+
+
+def pack(columns):
     copies = jax.ShapeDtypeStruct((SLABS, 8, 128), f32)
-    return pl.pallas_call(column_kernel, out_shape=(field, copies), name="column")(shares, orbitals)
-
-
-def attach_kernel(field_ref, parts_ref, copies_ref):
-    column = jnp.sum(parts_ref[...], axis=0)[:1]
-    row = lax.broadcasted_iota(jnp.int32, (ROWS, 128), 0)
-    tile = jnp.where(row == USED, column, field_ref[...])
-    for k in range(CHIPS):
-        copies_ref[k] = tile
-
-
-def attach(field, parts):
-    copies = jax.ShapeDtypeStruct((CHIPS, ROWS, 128), f32)
-    return pl.pallas_call(attach_kernel, out_shape=copies, name="attach")(field, parts)
+    return pl.pallas_call(pack_kernel, out_shape=copies, name="pack", compiler_params=SMALL)(columns)
 
 
 BLOCK = 4
@@ -240,9 +246,10 @@
     return (band % 2) * CHIPS + band // 2
 
 
-def finish_kernel(band_ref, field_ref, out_ref, flat):
+def finish_kernel(band_ref, part_ref, field_ref, out_ref, flat):
     band = band_ref[0]
-    matrix = field_ref[pl.ds(USED, BANDS, stride=ROWS), :][:, :BANDS]
+    packed = jnp.sum(part_ref[...], axis=0)
+    matrix = jnp.concatenate([packed[:, 32 * q : 32 * q + 32] for q in range(4)], 0)
     definite = (matrix + matrix.T) * (-0.5 / float(NG**3))
     row = lax.broadcasted_iota(jnp.int32, (BANDS, 2 * BANDS), 0)
     lane = lax.broadcasted_iota(jnp.int32, (BANDS, 2 * BANDS), 1)
@@ -275,14 +282,16 @@
             out_ref[p, :, 128 * c : 128 * c + 128] = flat[r : r + 1, :]
 
 
-def finish(band, fields):
+def finish(band, parts, fields):
+    vmem = pl.BlockSpec(memory_space=pltpu.VMEM)
     return pl.pallas_call(
         finish_kernel,
         out_shape=jax.ShapeDtypeStruct((PLANES, 1, NG * NG), f32),
-        in_specs=[pl.BlockSpec(memory_space=pltpu.SMEM), pl.BlockSpec(memory_space=pltpu.VMEM)],
+        in_specs=[pl.BlockSpec(memory_space=pltpu.SMEM), vmem, vmem],
         scratch_shapes=[pltpu.VMEM((ROWS, 128), f32)],
         name="finish",
-    )(band, fields)
+        compiler_params=SMALL,
+    )(band, parts, fields)
 
 
 def exchange_tiles(tiles, axis):
@@ -290,7 +299,7 @@
 
 
 def both_cores(chips):
-    return lax.all_gather(chips, "c", axis=0, tiled=False).reshape(BANDS * ROWS, 128)
+    return lax.all_gather(chips, CORE, axis=0, tiled=False).reshape(-1, 128)
 
 
 def per_device(orbitals):
@@ -301,21 +310,25 @@
     ]
     partner = lax.ppermute(tile, BAND + GRID, moves)
     own = exchange_tiles(copies, GRID)
-    own, partner = lax.optimization_barrier((own, partner))
-    pair = exchange_tiles(jnp.broadcast_to(partner[None], copies.shape), PAIR)
-    pair, copies = lax.optimization_barrier((pair, copies))
-    slab_orbitals = exchange_tiles(copies, PAIR)
-    partial = partial_exchange(own.reshape(SLABS * ROWS, 128), both_cores(pair), made)
-    partial, slab_orbitals = lax.optimization_barrier((partial, slab_orbitals))
+    own, partner, *made = lax.optimization_barrier((own, partner, *made))
+    both = jnp.concatenate([partner, tile], 0)
+    both = exchange_tiles(jnp.broadcast_to(both[None], (CHIPS, 2 * ROWS, 128)), PAIR)
+    pair = both_cores(both[:, :ROWS])
+    partial = partial_exchange(own.reshape(SLABS * ROWS, 128), pair, made)
+    partial, others = lax.optimization_barrier((partial, both[:, ROWS:]))
     shares = exchange_tiles(partial.reshape(SLABS, ROWS, 128), GRID)
-    field, lines = column_part(shares, both_cores(slab_orbitals))
-    parts = exchange_tiles(lines, GRID)
-    fields = both_cores(exchange_tiles(attach(field, parts), PAIR))
+    columns, copies = column_part(shares, both_cores(others))
+    fields = exchange_tiles(copies, PAIR)
+    for axes in (("z2", "z1"), "z4", "xl", "c"):
+        columns = lax.all_gather(columns, axes, axis=0, tiled=True)
+    parts = pack(columns)
+    parts, fields = lax.optimization_barrier((parts, fields))
+    parts = exchange_tiles(parts, GRID)
     band = lax.axis_index(BAND).astype(jnp.int32).reshape(1)
-    return jnp.transpose(finish(band, fields), (1, 0, 2))
+    return jnp.transpose(finish(band, parts, both_cores(fields)), (1, 0, 2))
 
 
 def solution(mesh):
-    parted = Mesh(mesh.devices.reshape(2, 8, 2, 2, 8), BAND + GRID)
+    parted = Mesh(mesh.devices.reshape((2,) * 9), BAND + GRID)
     spec = P(BAND, GRID, None)
     return jax.shard_map(per_device, mesh=parted, in_specs=(spec,), out_specs=spec, check_vma=False)

time: 139 us -> 146 us (1.050)
  blocking collectives: 51.4 us -> 74.8 us
  Pallas kernels: 18.3 us -> 9.58 us
  waiting for transfers between devices: 32.4 us -> 27.1 us
  starting transfers between devices: 35.3 us -> 30.2 us
  local copies, waits for them, and re-layouts: 0.82 us -> 3.32 us
    all_gather x3 -> x7, blocking collectives: 15 us -> 44.1 us  [the longest x4 30.8 us: per_device(): columns = lax.all_gather(columns, axes, axis=0, tiled=True)]
    all_to_all x2 -> x1, blocking collectives: 36.4 us -> 30.8 us  [exchange_tiles(): return lax.all_to_all(tiles, axis, 0, 0, tiled=True)]
    all_to_all x4, waiting for transfers between devices: 32.4 us -> 27.1 us  [exchange_tiles(): return lax.all_to_all(tiles, axis, 0, 0, tiled=True)]
    all_to_all x4, starting transfers between devices: 33.9 us -> 29.6 us  [exchange_tiles(): return lax.all_to_all(tiles, axis, 0, 0, tiled=True)]
    pallas_call x3, Pallas kernels: 5.43 us -> 2.42 us  [the longest x1 0.87 us: column_part(): pl.pallas_call(column_kernel, out_shape=(line, copies), name='column', co...]
    unnamed x4 -> x12, local copies, waits for them, and re-layouts: 0.79 us -> 3.2 us
    pallas_call x1, Pallas kernels: 2.63 us -> 0.3 us  [tables(): pl.pallas_call(tables_kernel, out_shape=(wide, wide, jax.ShapeDtypeStruct...]
    pallas_call x1, Pallas kernels: 6.9 us -> 4.59 us  [partial_exchange(): pl.pallas_call(exchange_kernel, out_shape=jax.ShapeDtypeStruct((SLABS * R...]
  transfers between devices with their start and end apart: 5 -> 5, of which waited for: 3 -> 3; matrix products, arithmetic and copies ran while one was open for 0% -> 0% of each run, Pallas kernels for 7% -> 1%
where the time goes in v3:
time: 146 us; the launch traced here: 145 us
  blocking collectives  74.8 us (51%)
  starting transfers between devices  30.2 us (21%)
  waiting for transfers between devices  27.1 us (19%)
  Pallas kernels  9.58 us (7%)
  local copies, waits for them, and re-layouts  3.32 us (2%)
    all_to_all x1, blocking collectives, exchange_tiles(): return lax.all_to_all(tiles, axis, 0, 0, tiled=True)  30.8 us
    all_gather x4, blocking collectives, per_device(): columns = lax.all_gather(columns, axes, axis=0, tiled=True)  30.8 us
    all_to_all x4, starting transfers between devices, exchange_tiles(): return lax.all_to_all(tiles, axis, 0, 0, tiled=True)  29.6 us
    all_to_all x4, waiting for transfers between devices, exchange_tiles(): return lax.all_to_all(tiles, axis, 0, 0, tiled=True)  27.1 us
    all_gather x3, blocking collectives, both_cores(): return lax.all_gather(chips, CORE, axis=0, tiled=False).reshape(-1, 128)  13.3 us
    pallas_call x1, Pallas kernels, partial_exchange(): pl.pallas_call(exchange_kernel, out_shape=jax.ShapeDtypeStruct((SLABS * R...  4.59 us
    unnamed x12, local copies, waits for them, and re-layouts  3.2 us
  transfers between devices with their start and end apart: 5, of which 3 were waited for; matrix products, arithmetic and copies ran while one was open for 0% of the time, Pallas kernels for 1%

profile of v3, /device:TPU:1, one launch (start us, length us, event | category | flops | bytes accessed | tf_op | source)
XLA Modules:
  0.0 145.2 jit_solution(16521492640961296316)
XLA Ops:
  0.0 0.7 copy-done.3
  0.7 0.9 prepare.1
  1.6 10.2 %all-to-all-start = ((f32[16,56,128]{2,1,0:T(8,128)}), f32[16,56,128]{2,1,0:T(8,128)S(1)}, u32[]{:S(2)}, u32[]{:S(2)}) async-start(f32[16,56,128]{2,1,0:T(8,128)} %get-tuple-element.21), calls=%async_computation | async-start | bytes 917504 | tf_op jit(solution)/shard_map/all_to_all | solution.py:298
  11.8 0.7 collective-permute-start
  12.5 0.0 copy-start.4
  12.5 0.7 copy-done.4
  13.2 0.7 copy-done.5
  14.0 0.3 tables.1
  14.3 1.0 copy-done
  15.2 0.0 collective-permute-done
  15.2 10.0 %all-to-all-done = f32[16,56,128]{2,1,0:T(8,128)S(1)} async-done(((f32[16,56,128]{2,1,0:T(8,128)}), f32[16,56,128]{2,1,0:T(8,128)S(1)}, u32[]{:S(2)}, u32[]{:S(2)}) %all-to-all-start) | async-done | bytes 458784 | tf_op jit(solution)/shard_map/all_to_all | solution.py:298
  25.3 0.1 broadcast_in_dim.2
  25.3 30.8 %all_to_all.25 = f32[16,112,128]{2,1,0:T(8,128)S(1)} all-to-all(f32[16,112,128]{2,1,0:T(8,128)S(1)} %broadcast_in_dim.2), channel_id=1, replica_groups=mesh['xl'=2,'z4'=2,'z2'=2,'z1'=2,'c'=2,'xh'=2,'y4'=2,'y2'=2,'y1'=2] {'xl..., dimensions={0} | all-to-all | bytes 1835008 | tf_op jit(solution)/shard_map/all_to_all | solution.py:298
  56.1 0.1 fusion
  56.2 7.8 %all-gather = f32[32,56,128]{2,1,0:T(8,128)S(1)} all-gather(f32[16,56,128]{2,1,0:T(8,128)S(1)} %get-tuple-element.38), channel_id=2, replica_groups=mesh['xl'=2,'z4'=2,'z2'=2,'z1'=2,'c'=2,'xh'=2,'y4'=2,'y2'=2,'y1'=2] {'c'}, dimensions={0}, use_global_device_ids=true | all-gather | bytes 1376256 | tf_op jit(solution)/shard_map/all_gather | solution.py:302
  64.0 0.0 copy-done.2
  64.0 4.6 %exchange.1 = f32[896,128]{1,0:T(8,128)} custom-call(f32[896,128]{1,0:T(8,128)S(1)} %bitcast.14, f32[1792,128]{1,0:T(8,128)S(1)} %bitcast.11, bf16[4,48,144]{2,1,0:T(8,128)(2,1)S(1)} %copy-done.2, bf16[2,2,256,512]{3,2,1,0:T(8,128)(2,1)S(1)} %get-tuple-element.28.wide_high, bf16[2,2,256,512]{3,2,1,0:T(8,128)(2,1)S(1)} %copy-done.1, ...), custom_call_target="tpu_custom_call" | custom-call | tf_op jit(solution)/shard_map/exchange/pallas_call | solution.py:185
  68.6 8.4 %all-to-all-start.2 = ((f32[16,56,128]{2,1,0:T(8,128)}), f32[16,56,128]{2,1,0:T(8,128)S(1)}, u32[]{:S(2)}, u32[]{:S(2)}) async-start(f32[16,56,128]{2,1,0:T(8,128)} %bitcast.4), calls=%async_computation.2 | async-start | bytes 917504 | tf_op jit(solution)/shard_map/all_to_all | solution.py:298
  77.0 2.7 %all-gather.1 = f32[32,56,128]{2,1,0:T(8,128)S(1)} all-gather(f32[16,56,128]{2,1,0:T(8,128)S(1)} %get-tuple-element.32), channel_id=3, replica_groups=mesh['xl'=2,'z4'=2,'z2'=2,'z1'=2,'c'=2,'xh'=2,'y4'=2,'y2'=2,'y1'=2] {'c'}, dimensions={0}, use_global_device_ids=true | all-gather | bytes 1376256 | tf_op jit(solution)/shard_map/all_gather | solution.py:302
  79.8 10.9 %all-to-all-done.2.share_ref = f32[16,56,128]{2,1,0:T(8,128)S(1)} async-done(((f32[16,56,128]{2,1,0:T(8,128)}), f32[16,56,128]{2,1,0:T(8,128)S(1)}, u32[]{:S(2)}, u32[]{:S(2)}) %all-to-all-start.2) | async-done | bytes 458784 | tf_op jit(solution)/shard_map/all_to_all | solution.py:298
  90.7 0.9 column.1
  91.6 4.2 %all-to-all-start.3 = ((f32[16,56,128]{2,1,0:T(8,128)}), f32[16,56,128]{2,1,0:T(8,128)S(1)}, u32[]{:S(2)}, u32[]{:S(2)}) async-start(f32[16,56,128]{2,1,0:T(8,128)} %get-tuple-element.34), calls=%async_computation.3 | async-start | bytes 917504 | tf_op jit(solution)/shard_map/all_to_all | solution.py:298
  95.9 12.7 %all-gather.3 = f32[4,1,128]{2,1,0:T(1,128)S(1)} all-gather(f32[1,1,128]{2,1,0:T(1,128)S(1)} %bitcast.16), channel_id=1, replica_groups=mesh['xl'=2,'z4'=2,'z2'=2,'z1'=2,'c'=2,'xh'=2,'y4'=2,'y2'=2,'y1'=2] {'z2..., dimensions={0}, use_global_device_ids=true | all-gather | bytes 2560 | tf_op jit(solution)/shard_map/all_gather | solution.py:323
  108.6 7.1 %all-gather.4 = f32[2,4,128]{2,1,0:T(4,128)S(1)} all-gather(f32[1,4,128]{2,1,0:T(4,128)S(1)} %bitcast.18), channel_id=1, replica_groups=mesh['xl'=2,'z4'=2,'z2'=2,'z1'=2,'c'=2,'xh'=2,'y4'=2,'y2'=2,'y1'=2] {'z4'}, dimensions={0}, use_global_device_ids=true | all-gather | bytes 6144 | tf_op jit(solution)/shard_map/all_gather | solution.py:323
  115.7 3.2 %all_gather.36 = f32[16,128]{1,0:T(8,128)S(1)} all-gather(f32[8,128]{1,0:T(8,128)S(1)} %bitcast.17), channel_id=1, replica_groups=mesh['xl'=2,'z4'=2,'z2'=2,'z1'=2,'c'=2,'xh'=2,'y4'=2,'y2'=2,'y1'=2] {'xl'}, dimensions={0}, use_global_device_ids=true | all-gather | bytes 12288 | tf_op jit(solution)/shard_map/all_gather | solution.py:323
  118.9 7.7 %all_gather.37.column_ref = f32[32,128]{1,0:T(8,128)S(1)} all-gather(f32[16,128]{1,0:T(8,128)S(1)} %all_gather.36), channel_id=1, replica_groups=mesh['xl'=2,'z4'=2,'z2'=2,'z1'=2,'c'=2,'xh'=2,'y4'=2,'y2'=2,'y1'=2] {'c'}, dimensions={0}, use_global_device_ids=true | all-gather | bytes 24576 | tf_op jit(solution)/shard_map/all_gather | solution.py:323
  126.6 0.7 pack.1
  127.3 0.0 all-to-all-done.3
  127.3 6.7 %all-to-all-start.4 = ((f32[16,8,128]{2,1,0:T(8,128)}), f32[16,8,128]{2,1,0:T(8,128)S(1)}, u32[]{:S(2)}, u32[]{:S(2)}) async-start(f32[16,8,128]{2,1,0:T(8,128)} %pack.1), calls=%async_computation.4 | async-start | bytes 131072 | tf_op jit(solution)/shard_map/all_to_all | solution.py:298
  134.0 2.7 %all-gather.2 = f32[32,56,128]{2,1,0:T(8,128)S(1)} all-gather(f32[16,56,128]{2,1,0:T(8,128)S(1)} %all-to-all-done.3), channel_id=4, replica_groups=mesh['xl'=2,'z4'=2,'z2'=2,'z1'=2,'c'=2,'xh'=2,'y4'=2,'y2'=2,'y1'=2] {'c'}, dimensions={0}, use_global_device_ids=true | all-gather | bytes 1376256 | tf_op jit(solution)/shard_map/all_gather | solution.py:302
  136.7 6.2 %all-to-all-done.4.part_ref = f32[16,8,128]{2,1,0:T(8,128)S(1)} async-done(((f32[16,8,128]{2,1,0:T(8,128)}), f32[16,8,128]{2,1,0:T(8,128)S(1)}, u32[]{:S(2)}, u32[]{:S(2)}) %all-to-all-start.4) | async-done | bytes 65568 | tf_op jit(solution)/shard_map/all_to_all | solution.py:298
  142.9 2.3 %finish.1 = f32[3,1,2304]{2,1,0:T(1,128)} custom-call(s32[1]{0:T(128)} %bitcast.band_ref, f32[16,8,128]{2,1,0:T(8,128)S(1)} %all-to-all-done.4.part_ref, f32[1792,128]{1,0:T(8,128)S(1)} %bitcast.13), custom_call_target="tpu_custom_call" | custom-call | tf_op jit(solution)/shard_map/finish/pallas_call | solution.py:287
  (7 shorter events, 0.0 us)
Async XLA Ops:
  0.0 0.7 copy-start.3
  1.6 23.6 %all-to-all-start = ((f32[16,56,128]{2,1,0:T(8,128)}), f32[16,56,128]{2,1,0:T(8,128)S(1)}, u32[]{:S(2)}, u32[]{:S(2)}) async-start(f32[16,56,128]{2,1,0:T(8,128)} %get-tuple-element.21), calls=%async_computation | async-start | bytes 917504 | tf_op jit(solution)/shard_map/all_to_all | solution.py:298
  11.8 3.4 %collective-permute-start = (f32[56,128]{1,0:T(8,128)S(1)}, f32[56,128]{1,0:T(8,128)S(1)}, u32[]{:S(2)}, u32[]{:S(2)}) collective-permute-start(f32[56,128]{1,0:T(8,128)S(1)} %get-tuple-element.22), channel_id=1, source_target_pairs={{0,0},{1,32},{2,64},{3,96},{4,128},{5,160},{6,192},{7,224},{8,256}... | collective-permute-start | bytes 86024 | tf_op jit(solution)/shard_map/ppermute | solution.py:311
  12.5 0.7 copy-start.4
  13.2 0.7 copy-start.5
  14.3 1.0 copy-start
  56.1 7.9 %copy-start.1 = (bf16[2,2,256,512]{3,2,1,0:T(8,128)(2,1)S(1)}, bf16[2,2,256,512]{3,2,1,0:T(8,128)(2,1)}, u32[]{:S(2)}) copy-start(bf16[2,2,256,512]{3,2,1,0:T(8,128)(2,1)} %copy-done) | copy-start | bytes 3145732
  56.1 7.9 %copy-start.2 = (bf16[4,48,144]{2,1,0:T(8,128)(2,1)S(1)}, bf16[4,48,144]{2,1,0:T(8,128)(2,1)}, u32[]{:S(2)}) copy-start(bf16[4,48,144]{2,1,0:T(8,128)(2,1)} %constant.38.clone.left_ref) | copy-start | bytes 165892
  68.6 22.1 %all-to-all-start.2 = ((f32[16,56,128]{2,1,0:T(8,128)}), f32[16,56,128]{2,1,0:T(8,128)S(1)}, u32[]{:S(2)}, u32[]{:S(2)}) async-start(f32[16,56,128]{2,1,0:T(8,128)} %bitcast.4), calls=%async_computation.2 | async-start | bytes 917504 | tf_op jit(solution)/shard_map/all_to_all | solution.py:298
  91.6 35.7 %all-to-all-start.3 = ((f32[16,56,128]{2,1,0:T(8,128)}), f32[16,56,128]{2,1,0:T(8,128)S(1)}, u32[]{:S(2)}, u32[]{:S(2)}) async-start(f32[16,56,128]{2,1,0:T(8,128)} %get-tuple-element.34), calls=%async_computation.3 | async-start | bytes 917504 | tf_op jit(solution)/shard_map/all_to_all | solution.py:298
  127.3 15.6 %all-to-all-start.4 = ((f32[16,8,128]{2,1,0:T(8,128)}), f32[16,8,128]{2,1,0:T(8,128)S(1)}, u32[]{:S(2)}, u32[]{:S(2)}) async-start(f32[16,8,128]{2,1,0:T(8,128)} %pack.1), calls=%async_computation.4 | async-start | bytes 131072 | tf_op jit(solution)/shard_map/all_to_all | solution.py:298

commit v4 on v2

--- a/solution.py
+++ b/solution.py
@@ -17,9 +17,11 @@
 ROWS = 56
 USED = PLANES * COLS
 CHIPS = BANDS // 2
-BAND, GRID = ("xl", "z", "c"), ("xh", "y")
-PAIR = ("xl", "z")
+PAIR, CORE, GRID = ("xl", "z4", "z2", "z1"), ("c",), ("xh", "y4", "y2", "y1")
+BAND = PAIR + CORE
 f32, bf16 = jnp.float32, jnp.bfloat16
+SMALL = pltpu.CompilerParams(vmem_limit_bytes=12 << 20)
+LARGE = pltpu.CompilerParams(vmem_limit_bytes=24 << 20)
 
 
 def real_basis():
@@ -105,6 +107,7 @@
         tables_kernel,
         out_shape=(wide, wide, jax.ShapeDtypeStruct((NG, NG, 128), f32)),
         name="tables",
+        compiler_params=SMALL,
     )(jnp.asarray(LAST_HIGH), jnp.asarray(LAST_LOW))
 
 
@@ -116,6 +119,9 @@
             [ref[pl.ds(first + COLS * p + c, SLABS, stride=ROWS), :] for p in range(PLANES)], 0
         )
 
+    def partner(d, c):
+        return column(pair_ref, d * SLABS * ROWS, c)
+
     def place(c):
         return slice(48 * (c // 3), 48 * (c // 3) + 48), slice(128 * (c % 3), 128 * (c % 3) + 128)
 
@@ -123,7 +129,7 @@
         own = column(own_ref, 0, c)
         rows, cols = place(c)
         for d in range(2):
-            high, low = split(own * column(pair_ref, d * SLABS * ROWS, c))
+            high, low = split(own * partner(d, c))
             rho_h[d, rows, cols] = high
             rho_l[d, rows, cols] = low
     for w in range(2):
@@ -165,8 +171,8 @@
         thirds.append((a[:, :128], a[:, 128:] + b[:, :128], b[:, 128:]))
     for c in range(COLS):
         rows, _ = place(c)
-        out = thirds[0][c % 3][rows] * column(pair_ref, 0, c)
-        out = out + thirds[1][c % 3][rows] * column(pair_ref, SLABS * ROWS, c)
+        out = thirds[0][c % 3][rows] * partner(0, c)
+        out = out + thirds[1][c % 3][rows] * partner(1, c)
         for p in range(PLANES):
             out_ref[pl.ds(COLS * p + c, SLABS, stride=ROWS), :] = out[16 * p : 16 * p + 16]
     for r in range(USED, ROWS):
@@ -181,10 +187,11 @@
         out_shape=jax.ShapeDtypeStruct((SLABS * ROWS, 128), f32),
         scratch_shapes=[rho, rho, big, big, solved, solved],
         name="exchange",
+        compiler_params=LARGE,
     )(own, pair, jnp.asarray(LEFTS), *made)
 
 
-def prepare_kernel(slab_ref, tile_ref, copies_ref):
+def prepare_kernel(slab_ref, copies_ref, tile_ref):
     tile_ref[USED:ROWS, :] = jnp.zeros((ROWS - USED, 128), f32)
     for p in range(PLANES):
         for c in range(COLS):
@@ -196,9 +203,13 @@
 
 
 def prepare(slab):
-    tile = jax.ShapeDtypeStruct((ROWS, 128), f32)
-    copies = jax.ShapeDtypeStruct((SLABS, ROWS, 128), f32)
-    return pl.pallas_call(prepare_kernel, out_shape=(tile, copies), name="prepare")(slab)
+    return pl.pallas_call(
+        prepare_kernel,
+        out_shape=jax.ShapeDtypeStruct((SLABS, ROWS, 128), f32),
+        scratch_shapes=[pltpu.VMEM((ROWS, 128), f32)],
+        name="prepare",
+        compiler_params=SMALL,
+    )(slab)
 
 
 def column_kernel(share_ref, orbital_ref, field_ref, copies_ref):
@@ -217,7 +228,9 @@
 def column_part(shares, orbitals):
     field = jax.ShapeDtypeStruct((ROWS, 128), f32)
     copies = jax.ShapeDtypeStruct((SLABS, 8, 128), f32)
-    return pl.pallas_call(column_kernel, out_shape=(field, copies), name="column")(shares, orbitals)
+    return pl.pallas_call(column_kernel, out_shape=(field, copies), name="column", compiler_params=SMALL)(
+        shares, orbitals
+    )
 
 
 def attach_kernel(field_ref, parts_ref, copies_ref):
@@ -230,7 +243,7 @@
 
 def attach(field, parts):
     copies = jax.ShapeDtypeStruct((CHIPS, ROWS, 128), f32)
-    return pl.pallas_call(attach_kernel, out_shape=copies, name="attach")(field, parts)
+    return pl.pallas_call(attach_kernel, out_shape=copies, name="attach", compiler_params=SMALL)(field, parts)
 
 
 BLOCK = 4
@@ -282,6 +295,7 @@
         in_specs=[pl.BlockSpec(memory_space=pltpu.SMEM), pl.BlockSpec(memory_space=pltpu.VMEM)],
         scratch_shapes=[pltpu.VMEM((ROWS, 128), f32)],
         name="finish",
+        compiler_params=SMALL,
     )(band, fields)
 
 
@@ -290,25 +304,18 @@
 
 
 def both_cores(chips):
-    return lax.all_gather(chips, "c", axis=0, tiled=False).reshape(BANDS * ROWS, 128)
+    return lax.all_gather(chips, CORE, axis=0, tiled=False).reshape(-1, 128)
 
 
 def per_device(orbitals):
-    tile, copies = prepare(jnp.transpose(orbitals, (1, 0, 2)))
+    copies = prepare(jnp.transpose(orbitals, (1, 0, 2)))
     made = tables()
-    moves = [
-        (b * SLABS + s, (2 * s + b % 2) * SLABS + b // 2) for b in range(BANDS) for s in range(SLABS)
-    ]
-    partner = lax.ppermute(tile, BAND + GRID, moves)
-    own = exchange_tiles(copies, GRID)
-    own, partner = lax.optimization_barrier((own, partner))
-    pair = exchange_tiles(jnp.broadcast_to(partner[None], copies.shape), PAIR)
-    pair, copies = lax.optimization_barrier((pair, copies))
-    slab_orbitals = exchange_tiles(copies, PAIR)
-    partial = partial_exchange(own.reshape(SLABS * ROWS, 128), both_cores(pair), made)
-    partial, slab_orbitals = lax.optimization_barrier((partial, slab_orbitals))
+    chips = exchange_tiles(copies, PAIR)
+    whole = exchange_tiles(jnp.concatenate([copies, chips], 1), GRID)
+    pair = both_cores(whole[:, ROWS:])
+    partial = partial_exchange(whole[:, :ROWS].reshape(SLABS * ROWS, 128), pair, made)
     shares = exchange_tiles(partial.reshape(SLABS, ROWS, 128), GRID)
-    field, lines = column_part(shares, both_cores(slab_orbitals))
+    field, lines = column_part(shares, both_cores(chips))
     parts = exchange_tiles(lines, GRID)
     fields = both_cores(exchange_tiles(attach(field, parts), PAIR))
     band = lax.axis_index(BAND).astype(jnp.int32).reshape(1)
@@ -316,6 +323,6 @@
 
 
 def solution(mesh):
-    parted = Mesh(mesh.devices.reshape(2, 8, 2, 2, 8), BAND + GRID)
+    parted = Mesh(mesh.devices.reshape((2,) * 9), BAND + GRID)
     spec = P(BAND, GRID, None)
     return jax.shard_map(per_device, mesh=parted, in_specs=(spec,), out_specs=spec, check_vma=False)

time: 139 us -> 130 us (0.935)
  starting transfers between devices: 35.3 us -> 20 us
  Pallas kernels: 18.3 us -> 8.16 us
  waiting for transfers between devices: 32.4 us -> 41.6 us
  blocking collectives: 51.4 us -> 55.8 us
  local copies, waits for them, and re-layouts: 0.82 us -> 2.76 us
    all_to_all x4 -> x3, starting transfers between devices: 33.9 us -> 20 us  [exchange_tiles(): return lax.all_to_all(tiles, axis, 0, 0, tiled=True)]
    all_to_all x4 -> x3, waiting for transfers between devices: 32.4 us -> 41.6 us  [exchange_tiles(): return lax.all_to_all(tiles, axis, 0, 0, tiled=True)]
    pallas_call x3, Pallas kernels: 5.43 us -> 1.06 us  [the longest x1 0.81 us: attach(): pl.pallas_call(attach_kernel, out_shape=copies, name='attach', compiler_p...]
    all_to_all x2, blocking collectives: 36.4 us -> 38.8 us  [exchange_tiles(): return lax.all_to_all(tiles, axis, 0, 0, tiled=True)]
    pallas_call x1, Pallas kernels: 2.63 us -> 0.3 us  [tables(): pl.pallas_call(tables_kernel, out_shape=(wide, wide, jax.ShapeDtypeStruct...]
    pallas_call x1, Pallas kernels: 6.9 us -> 4.58 us  [partial_exchange(): pl.pallas_call(exchange_kernel, out_shape=jax.ShapeDtypeStruct((SLABS * R...]
    all_gather x3, blocking collectives: 15 us -> 17 us  [both_cores(): return lax.all_gather(chips, CORE, axis=0, tiled=False).reshape(-1, 128)]
    ppermute x1 -> x0, starting transfers between devices: 1.41 us -> none  [per_device(): partner = lax.ppermute(tile, BAND + GRID, moves)]
  transfers between devices with their start and end apart: 5 -> 3, of which waited for: 3 -> 3; matrix products, arithmetic and copies ran while one was open for 0% -> 0% of each run, Pallas kernels for 7% -> 0%
where the time goes in v4:
time: 130 us
  blocking collectives  55.8 us (43%)
  waiting for transfers between devices  41.6 us (32%)
  starting transfers between devices  20 us (15%)
  Pallas kernels  8.16 us (6%)
  local copies, waits for them, and re-layouts  2.76 us (2%)
    all_to_all x3, waiting for transfers between devices, exchange_tiles(): return lax.all_to_all(tiles, axis, 0, 0, tiled=True)  41.6 us
    all_to_all x2, blocking collectives, exchange_tiles(): return lax.all_to_all(tiles, axis, 0, 0, tiled=True)  38.8 us
    all_to_all x3, starting transfers between devices, exchange_tiles(): return lax.all_to_all(tiles, axis, 0, 0, tiled=True)  20 us
    all_gather x3, blocking collectives, both_cores(): return lax.all_gather(chips, CORE, axis=0, tiled=False).reshape(-1, 128)  17 us
    pallas_call x1, Pallas kernels, partial_exchange(): pl.pallas_call(exchange_kernel, out_shape=jax.ShapeDtypeStruct((SLABS * R...  4.58 us
  transfers between devices with their start and end apart: 3, of which 3 were waited for; matrix products, arithmetic and copies ran while one was open for 0% of the time, Pallas kernels for 0%

profile of v4, /device:TPU:1, one launch (start us, length us, event | category | flops | bytes accessed | tf_op | source)
XLA Modules:
  0.0 129.6 jit_solution(14067676915902846077)
XLA Ops:
  0.0 0.0 copy-start.1
  0.0 0.7 copy-done.1
  0.8 23.6 %all_to_all.25 = f32[16,56,128]{2,1,0:T(8,128)S(1)} all-to-all(f32[16,56,128]{2,1,0:T(8,128)S(1)} %prepare.1), channel_id=1, replica_groups=mesh['xl'=2,'z4'=2,'z2'=2,'z1'=2,'c'=2,'xh'=2,'y4'=2,'y2'=2,'y1'=2] {'xl..., dimensions={0} | all-to-all | bytes 917504 | tf_op jit(solution)/shard_map/all_to_all | solution.py:303
  24.4 0.0 copy-start.4
  24.4 0.8 copy-done.4
  25.2 1.1 pad_maximum_fusion
  26.2 0.0 copy-start.2
  26.2 0.0 copy-start.3
  26.2 9.3 %all-to-all-start.1 = ((f32[16,112,128]{2,1,0:T(8,128)}), f32[16,112,128]{2,1,0:T(8,128)}, u32[]{:S(2)}, u32[]{:S(2)}) async-start(f32[16,112,128]{2,1,0:T(8,128)} %pad_maximum_fusion), calls=%async_computation.1 | async-start | bytes 1835008 | tf_op jit(solution)/shard_map/all_to_all | solution.py:303
  35.5 0.0 copy-done.2
  35.5 0.0 copy-done.3
  35.5 0.3 tables.1
  35.9 0.0 copy-start
  35.9 19.9 %all-to-all-done.1 = f32[16,112,128]{2,1,0:T(8,128)} async-done(((f32[16,112,128]{2,1,0:T(8,128)}), f32[16,112,128]{2,1,0:T(8,128)}, u32[]{:S(2)}, u32[]{:S(2)}) %all-to-all-start.1) | async-done | bytes 917536 | tf_op jit(solution)/shard_map/all_to_all | solution.py:303
  55.7 1.2 fusion
  57.0 8.1 %all-gather = f32[32,56,128]{2,1,0:T(8,128)S(1)} all-gather(f32[16,56,128]{2,1,0:T(8,128)S(1)} %get-tuple-element.15), channel_id=2, replica_groups=mesh['xl'=2,'z4'=2,'z2'=2,'z1'=2,'c'=2,'xh'=2,'y4'=2,'y2'=2,'y1'=2] {'c'}, dimensions={0}, use_global_device_ids=true | all-gather | bytes 1376256 | tf_op jit(solution)/shard_map/all_gather | solution.py:307
  65.1 0.0 copy-done
  65.1 4.6 %exchange.1 = f32[896,128]{1,0:T(8,128)} custom-call(f32[896,128]{1,0:T(8,128)S(1)} %bitcast.11, f32[1792,128]{1,0:T(8,128)S(1)} %bitcast.8, bf16[4,48,144]{2,1,0:T(8,128)(2,1)S(1)} %copy-done, bf16[2,2,256,512]{3,2,1,0:T(8,128)(2,1)S(1)} %get-tuple-element.10.wide_high, bf16[2,2,256,512]{3,2,1,0:T(8,128)(2,1)S(1)} %get-tuple-element.11.wide_low, ...), custom_call_target="tpu_custom_call" | custom-call | tf_op jit(solution)/shard_map/exchange/pallas_call | solution.py:185
  69.7 0.0 copy-start.5
  69.7 4.8 %all-to-all-start.2 = ((f32[16,56,128]{2,1,0:T(8,128)}), f32[16,56,128]{2,1,0:T(8,128)S(1)}, u32[]{:S(2)}, u32[]{:S(2)}) async-start(f32[16,56,128]{2,1,0:T(8,128)} %bitcast.4), calls=%async_computation.2 | async-start | bytes 917504 | tf_op jit(solution)/shard_map/all_to_all | solution.py:303
  74.5 0.0 copy-done.5
  74.5 2.7 %all-gather.1 = f32[32,56,128]{2,1,0:T(8,128)S(1)} all-gather(f32[16,56,128]{2,1,0:T(8,128)S(1)} %copy-done.5), channel_id=3, replica_groups=mesh['xl'=2,'z4'=2,'z2'=2,'z1'=2,'c'=2,'xh'=2,'y4'=2,'y2'=2,'y1'=2] {'c'}, dimensions={0}, use_global_device_ids=true | all-gather | bytes 1376256 | tf_op jit(solution)/shard_map/all_gather | solution.py:307
  77.2 10.9 %all-to-all-done.2.share_ref = f32[16,56,128]{2,1,0:T(8,128)S(1)} async-done(((f32[16,56,128]{2,1,0:T(8,128)}), f32[16,56,128]{2,1,0:T(8,128)S(1)}, u32[]{:S(2)}, u32[]{:S(2)}) %all-to-all-start.2) | async-done | bytes 458784 | tf_op jit(solution)/shard_map/all_to_all | solution.py:303
  88.2 0.2 column.1
  88.4 15.2 %all_to_all.26.parts_ref = f32[16,8,128]{2,1,0:T(8,128)S(1)} all-to-all(f32[16,8,128]{2,1,0:T(8,128)S(1)} %get-tuple-element.14), channel_id=1, replica_groups=mesh['xl'=2,'z4'=2,'z2'=2,'z1'=2,'c'=2,'xh'=2,'y4'=2,'y2'=2,'y1'=2] {'xh..., dimensions={0} | all-to-all | bytes 131072 | tf_op jit(solution)/shard_map/all_to_all | solution.py:303
  103.6 0.8 attach.1
  104.4 6.0 %all-to-all-start.4 = ((f32[16,56,128]{2,1,0:T(8,128)}), f32[16,56,128]{2,1,0:T(8,128)S(1)}, u32[]{:S(2)}, u32[]{:S(2)}) async-start(f32[16,56,128]{2,1,0:T(8,128)} %attach.1), calls=%async_computation.4 | async-start | bytes 917504 | tf_op jit(solution)/shard_map/all_to_all | solution.py:303
  110.4 10.8 %all-to-all-done.4 = f32[16,56,128]{2,1,0:T(8,128)S(1)} async-done(((f32[16,56,128]{2,1,0:T(8,128)}), f32[16,56,128]{2,1,0:T(8,128)S(1)}, u32[]{:S(2)}, u32[]{:S(2)}) %all-to-all-start.4) | async-done | bytes 458784 | tf_op jit(solution)/shard_map/all_to_all | solution.py:303
  121.3 6.1 %all-gather.2 = f32[32,56,128]{2,1,0:T(8,128)S(1)} all-gather(f32[16,56,128]{2,1,0:T(8,128)S(1)} %all-to-all-done.4), channel_id=4, replica_groups=mesh['xl'=2,'z4'=2,'z2'=2,'z1'=2,'c'=2,'xh'=2,'y4'=2,'y2'=2,'y1'=2] {'c'}, dimensions={0}, use_global_device_ids=true | all-gather | bytes 1376256 | tf_op jit(solution)/shard_map/all_gather | solution.py:307
  127.4 2.2 %finish.1 = f32[3,1,2304]{2,1,0:T(1,128)} custom-call(s32[1]{0:T(128)} %bitcast.band_ref, f32[1792,128]{1,0:T(8,128)S(1)} %bitcast.10), custom_call_target="tpu_custom_call" | custom-call | tf_op jit(solution)/shard_map/finish/pallas_call | solution.py:292
  (1 shorter events, 0.0 us)
Async XLA Ops:
  0.0 0.7 copy-start.1
  24.4 0.8 copy-start.4
  26.2 9.3 %copy-start.2 = (bf16[2,48,128]{2,1,0:T(8,128)(2,1)S(1)}, bf16[2,48,128]{2,1,0:T(8,128)(2,1)}, u32[]{:S(2)}) copy-start(bf16[2,48,128]{2,1,0:T(8,128)(2,1)} %constant.36.clone.high_ref) | copy-start | bytes 73732
  26.2 9.3 %copy-start.3 = (bf16[2,48,128]{2,1,0:T(8,128)(2,1)S(1)}, bf16[2,48,128]{2,1,0:T(8,128)(2,1)}, u32[]{:S(2)}) copy-start(bf16[2,48,128]{2,1,0:T(8,128)(2,1)} %constant.37.clone.low_ref) | copy-start | bytes 73732
  26.2 29.5 %all-to-all-start.1 = ((f32[16,112,128]{2,1,0:T(8,128)}), f32[16,112,128]{2,1,0:T(8,128)}, u32[]{:S(2)}, u32[]{:S(2)}) async-start(f32[16,112,128]{2,1,0:T(8,128)} %pad_maximum_fusion), calls=%async_computation.1 | async-start | bytes 1835008 | tf_op jit(solution)/shard_map/all_to_all | solution.py:303
  35.9 29.3 %copy-start = (bf16[4,48,144]{2,1,0:T(8,128)(2,1)S(1)}, bf16[4,48,144]{2,1,0:T(8,128)(2,1)}, u32[]{:S(2)}) copy-start(bf16[4,48,144]{2,1,0:T(8,128)(2,1)} %constant.38.clone.left_ref) | copy-start | bytes 165892
  69.7 4.8 %copy-start.5 = (f32[16,56,128]{2,1,0:T(8,128)S(1)}, f32[16,56,128]{2,1,0:T(8,128)}, u32[]{:S(2)}) copy-start(f32[16,56,128]{2,1,0:T(8,128)} %copy-done.4) | copy-start | bytes 1376260
  69.7 18.5 %all-to-all-start.2 = ((f32[16,56,128]{2,1,0:T(8,128)}), f32[16,56,128]{2,1,0:T(8,128)S(1)}, u32[]{:S(2)}, u32[]{:S(2)}) async-start(f32[16,56,128]{2,1,0:T(8,128)} %bitcast.4), calls=%async_computation.2 | async-start | bytes 917504 | tf_op jit(solution)/shard_map/all_to_all | solution.py:303
  104.4 16.8 %all-to-all-start.4 = ((f32[16,56,128]{2,1,0:T(8,128)}), f32[16,56,128]{2,1,0:T(8,128)S(1)}, u32[]{:S(2)}, u32[]{:S(2)}) async-start(f32[16,56,128]{2,1,0:T(8,128)} %attach.1), calls=%async_computation.4 | async-start | bytes 917504 | tf_op jit(solution)/shard_map/all_to_all | solution.py:303

commit v5 on v4

--- a/solution.py
+++ b/solution.py
@@ -101,14 +101,14 @@
         coulomb[k] = jnp.where(total > 0.0, -COULOMB / jnp.maximum(total, 1.0), 0.0)
 
 
-def tables():
+def tables(last_high, last_low):
     wide = jax.ShapeDtypeStruct((2, 2, 256, 512), bf16)
     return pl.pallas_call(
         tables_kernel,
         out_shape=(wide, wide, jax.ShapeDtypeStruct((NG, NG, 128), f32)),
         name="tables",
         compiler_params=SMALL,
-    )(jnp.asarray(LAST_HIGH), jnp.asarray(LAST_LOW))
+    )(last_high, last_low)
 
 
 def exchange_kernel(
@@ -191,7 +191,7 @@
     )(own, pair, jnp.asarray(LEFTS), *made)
 
 
-def prepare_kernel(slab_ref, copies_ref, tile_ref):
+def prepare_kernel(slab_ref, tile_ref, copies_ref):
     tile_ref[USED:ROWS, :] = jnp.zeros((ROWS - USED, 128), f32)
     for p in range(PLANES):
         for c in range(COLS):
@@ -203,13 +203,9 @@
 
 
 def prepare(slab):
-    return pl.pallas_call(
-        prepare_kernel,
-        out_shape=jax.ShapeDtypeStruct((SLABS, ROWS, 128), f32),
-        scratch_shapes=[pltpu.VMEM((ROWS, 128), f32)],
-        name="prepare",
-        compiler_params=SMALL,
-    )(slab)
+    tile = jax.ShapeDtypeStruct((ROWS, 128), f32)
+    copies = jax.ShapeDtypeStruct((SLABS, ROWS, 128), f32)
+    return pl.pallas_call(prepare_kernel, out_shape=(tile, copies), name="prepare", compiler_params=SMALL)(slab)
 
 
 def column_kernel(share_ref, orbital_ref, field_ref, copies_ref):
@@ -308,12 +304,14 @@
 
 
 def per_device(orbitals):
-    copies = prepare(jnp.transpose(orbitals, (1, 0, 2)))
-    made = tables()
-    chips = exchange_tiles(copies, PAIR)
-    whole = exchange_tiles(jnp.concatenate([copies, chips], 1), GRID)
-    pair = both_cores(whole[:, ROWS:])
-    partial = partial_exchange(whole[:, :ROWS].reshape(SLABS * ROWS, 128), pair, made)
+    tile, copies = prepare(jnp.transpose(orbitals, (1, 0, 2)))
+    own = exchange_tiles(copies, GRID)
+    chips = lax.all_gather(lax.all_gather(tile, ("z4", "z2", "z1")), "xl").reshape(CHIPS, ROWS, 128)
+    last = (jnp.asarray(LAST_HIGH), jnp.asarray(LAST_LOW))
+    own, chips, *last = lax.optimization_barrier((own, chips, *last))
+    pair, *made = lax.optimization_barrier((exchange_tiles(chips, GRID), *tables(*last)))
+    pair = both_cores(pair)
+    partial = partial_exchange(own.reshape(SLABS * ROWS, 128), pair, made)
     shares = exchange_tiles(partial.reshape(SLABS, ROWS, 128), GRID)
     field, lines = column_part(shares, both_cores(chips))
     parts = exchange_tiles(lines, GRID)

time: 130 us -> 138 us (1.062)
  blocking collectives: 55.8 us -> 67.4 us
  waiting for transfers between devices: 41.6 us -> 31.4 us
  starting transfers between devices: 20 us -> 27.3 us
    all_gather x0 -> x2, blocking collectives: none -> 31.8 us  [the longest x1 25.9 us: per_device(): lax.all_gather(tile, ('z4', 'z2', 'z1'))]
    all_to_all x2 -> x1, blocking collectives: 38.8 us -> 15.2 us  [exchange_tiles(): return lax.all_to_all(tiles, axis, 0, 0, tiled=True)]
    all_to_all x3 -> x4, waiting for transfers between devices: 41.6 us -> 31.4 us  [exchange_tiles(): return lax.all_to_all(tiles, axis, 0, 0, tiled=True)]
    all_to_all x3 -> x4, starting transfers between devices: 20 us -> 27.3 us  [exchange_tiles(): return lax.all_to_all(tiles, axis, 0, 0, tiled=True)]
    all_gather x3, blocking collectives: 17 us -> 20.4 us  [both_cores(): return lax.all_gather(chips, CORE, axis=0, tiled=False).reshape(-1, 128)]
  transfers between devices with their start and end apart: 3 -> 4, of which waited for: 3 -> 3; matrix products, arithmetic and copies ran while one was open for 0% -> 0% of each run, Pallas kernels for 0% -> 0%
where the time goes in v5:
time: 138 us; the launch traced here: 137 us
  blocking collectives  67.4 us (49%)
  waiting for transfers between devices  31.4 us (23%)
  starting transfers between devices  27.3 us (20%)
  Pallas kernels  8.94 us (6%)
  local copies, waits for them, and re-layouts  1.73 us (1%)
    all_to_all x4, waiting for transfers between devices, exchange_tiles(): return lax.all_to_all(tiles, axis, 0, 0, tiled=True)  31.4 us
    all_to_all x4, starting transfers between devices, exchange_tiles(): return lax.all_to_all(tiles, axis, 0, 0, tiled=True)  27.3 us
    all_gather x1, blocking collectives, per_device(): lax.all_gather(tile, ('z4', 'z2', 'z1'))  25.9 us
    all_gather x3, blocking collectives, both_cores(): return lax.all_gather(chips, CORE, axis=0, tiled=False).reshape(-1, 128)  20.4 us
    all_to_all x1, blocking collectives, exchange_tiles(): return lax.all_to_all(tiles, axis, 0, 0, tiled=True)  15.2 us
    all_gather x1, blocking collectives, per_device(): lax.all_gather(lax.all_gather(tile, ('z4', 'z2', 'z1')), 'xl')  5.81 us
    pallas_call x1, Pallas kernels, partial_exchange(): pl.pallas_call(exchange_kernel, out_shape=jax.ShapeDtypeStruct((SLABS * R...  4.59 us
  transfers between devices with their start and end apart: 4, of which 3 were waited for; matrix products, arithmetic and copies ran while one was open for 0% of the time, Pallas kernels for 0%

profile of v5, /device:TPU:1, one launch (start us, length us, event | category | flops | bytes accessed | tf_op | source)
XLA Modules:
  0.0 136.9 jit_solution(17828020058804448423)
XLA Ops:
  0.0 0.0 copy-start.3
  0.0 0.7 copy-done.3
  0.7 0.8 prepare.1
  1.6 0.0 copy-start.4
  1.6 0.0 copy-start.5
  1.6 10.3 %all-to-all-start = ((f32[16,56,128]{2,1,0:T(8,128)}), f32[16,56,128]{2,1,0:T(8,128)S(1)}, u32[]{:S(2)}, u32[]{:S(2)}) async-start(f32[16,56,128]{2,1,0:T(8,128)} %get-tuple-element.20), calls=%async_computation | async-start | bytes 917504 | tf_op jit(solution)/shard_map/all_to_all | solution.py:299
  11.9 25.9 %all-gather = f32[448,128]{1,0:T(8,128)S(1)} all-gather(f32[56,128]{1,0:T(8,128)S(1)} %get-tuple-element.21), channel_id=2, replica_groups=mesh['xl'=2,'z4'=2,'z2'=2,'z1'=2,'c'=2,'xh'=2,'y4'=2,'y2'=2,'y1'=2] {'z4..., dimensions={0}, use_global_device_ids=true | all-gather | bytes 258048 | tf_op jit(solution)/shard_map/all_gather | solution.py:309
  37.9 5.8 %all-gather.1 = f32[16,56,128]{2,1,0:T(8,128)} all-gather(f32[8,56,128]{2,1,0:T(8,128)S(1)} %bitcast.14), channel_id=3, replica_groups=mesh['xl'=2,'z4'=2,'z2'=2,'z1'=2,'c'=2,'xh'=2,'y4'=2,'y2'=2,'y1'=2] {'xl'}, dimensions={0}, use_global_device_ids=true | all-gather | bytes 688128 | tf_op jit(solution)/shard_map/all_gather | solution.py:309
  43.7 0.0 copy-start.2
  43.7 0.0 all-to-all-done
  43.7 8.9 %all-to-all-start.1 = ((f32[16,56,128]{2,1,0:T(8,128)}), f32[16,56,128]{2,1,0:T(8,128)S(1)}, u32[]{:S(2)}, u32[]{:S(2)}) async-start(f32[16,56,128]{2,1,0:T(8,128)} %all-gather.1), calls=%async_computation.1 | async-start | bytes 917504 | tf_op jit(solution)/shard_map/all_to_all | solution.py:299
  52.6 0.0 copy-done.4
  52.6 0.0 copy-done.5
  52.6 0.3 tables.1
  52.9 0.0 copy-start
  52.9 1.0 copy-done
  53.9 9.8 %all-to-all-done.1 = f32[16,56,128]{2,1,0:T(8,128)S(1)} async-done(((f32[16,56,128]{2,1,0:T(8,128)}), f32[16,56,128]{2,1,0:T(8,128)S(1)}, u32[]{:S(2)}, u32[]{:S(2)}) %all-to-all-start.1) | async-done | bytes 458784 | tf_op jit(solution)/shard_map/all_to_all | solution.py:299
  63.7 0.0 copy-start.1
  63.7 11.4 %all-gather.2 = f32[32,56,128]{2,1,0:T(8,128)S(1)} all-gather(f32[16,56,128]{2,1,0:T(8,128)S(1)} %all-to-all-done.1), channel_id=4, replica_groups=mesh['xl'=2,'z4'=2,'z2'=2,'z1'=2,'c'=2,'xh'=2,'y4'=2,'y2'=2,'y1'=2] {'c'}, dimensions={0}, use_global_device_ids=true | all-gather | bytes 1376256 | tf_op jit(solution)/shard_map/all_gather | solution.py:303
  75.1 0.0 copy-done.2
  75.1 0.0 copy-done.1
  75.1 4.6 %exchange.1 = f32[896,128]{1,0:T(8,128)} custom-call(f32[896,128]{1,0:T(8,128)S(1)} %bitcast.12, f32[1792,128]{1,0:T(8,128)S(1)} %bitcast.9, bf16[4,48,144]{2,1,0:T(8,128)(2,1)S(1)} %copy-done.2, bf16[2,2,256,512]{3,2,1,0:T(8,128)(2,1)S(1)} %get-tuple-element.30.wide_high, bf16[2,2,256,512]{3,2,1,0:T(8,128)(2,1)S(1)} %copy-done.1, ...), custom_call_target="tpu_custom_call" | custom-call | tf_op jit(solution)/shard_map/exchange/pallas_call | solution.py:185
  79.7 4.3 %all-to-all-start.2 = ((f32[16,56,128]{2,1,0:T(8,128)}), f32[16,56,128]{2,1,0:T(8,128)S(1)}, u32[]{:S(2)}, u32[]{:S(2)}) async-start(f32[16,56,128]{2,1,0:T(8,128)} %bitcast.5), calls=%async_computation.2 | async-start | bytes 917504 | tf_op jit(solution)/shard_map/all_to_all | solution.py:299
  84.0 3.0 %all-gather.3 = f32[32,56,128]{2,1,0:T(8,128)S(1)} all-gather(f32[16,56,128]{2,1,0:T(8,128)} %all-gather.1), channel_id=5, replica_groups=mesh['xl'=2,'z4'=2,'z2'=2,'z1'=2,'c'=2,'xh'=2,'y4'=2,'y2'=2,'y1'=2] {'c'}, dimensions={0}, use_global_device_ids=true | all-gather | bytes 1376256 | tf_op jit(solution)/shard_map/all_gather | solution.py:303
  87.0 10.7 %all-to-all-done.2.share_ref = f32[16,56,128]{2,1,0:T(8,128)S(1)} async-done(((f32[16,56,128]{2,1,0:T(8,128)}), f32[16,56,128]{2,1,0:T(8,128)S(1)}, u32[]{:S(2)}, u32[]{:S(2)}) %all-to-all-start.2) | async-done | bytes 458784 | tf_op jit(solution)/shard_map/all_to_all | solution.py:299
  97.7 0.2 column.1
  97.9 15.2 %all_to_all.25.parts_ref = f32[16,8,128]{2,1,0:T(8,128)S(1)} all-to-all(f32[16,8,128]{2,1,0:T(8,128)S(1)} %get-tuple-element.34), channel_id=1, replica_groups=mesh['xl'=2,'z4'=2,'z2'=2,'z1'=2,'c'=2,'xh'=2,'y4'=2,'y2'=2,'y1'=2] {'xh..., dimensions={0} | all-to-all | bytes 131072 | tf_op jit(solution)/shard_map/all_to_all | solution.py:299
  113.1 0.8 attach.1
  114.0 3.8 %all-to-all-start.4 = ((f32[16,56,128]{2,1,0:T(8,128)}), f32[16,56,128]{2,1,0:T(8,128)S(1)}, u32[]{:S(2)}, u32[]{:S(2)}) async-start(f32[16,56,128]{2,1,0:T(8,128)} %attach.1), calls=%async_computation.4 | async-start | bytes 917504 | tf_op jit(solution)/shard_map/all_to_all | solution.py:299
  117.7 10.8 %all-to-all-done.4 = f32[16,56,128]{2,1,0:T(8,128)S(1)} async-done(((f32[16,56,128]{2,1,0:T(8,128)}), f32[16,56,128]{2,1,0:T(8,128)S(1)}, u32[]{:S(2)}, u32[]{:S(2)}) %all-to-all-start.4) | async-done | bytes 458784 | tf_op jit(solution)/shard_map/all_to_all | solution.py:299
  128.6 6.1 %all-gather.4 = f32[32,56,128]{2,1,0:T(8,128)S(1)} all-gather(f32[16,56,128]{2,1,0:T(8,128)S(1)} %all-to-all-done.4), channel_id=6, replica_groups=mesh['xl'=2,'z4'=2,'z2'=2,'z1'=2,'c'=2,'xh'=2,'y4'=2,'y2'=2,'y1'=2] {'c'}, dimensions={0}, use_global_device_ids=true | all-gather | bytes 1376256 | tf_op jit(solution)/shard_map/all_gather | solution.py:303
  134.7 2.2 %finish.1 = f32[3,1,2304]{2,1,0:T(1,128)} custom-call(s32[1]{0:T(128)} %bitcast.band_ref, f32[1792,128]{1,0:T(8,128)S(1)} %bitcast.11), custom_call_target="tpu_custom_call" | custom-call | tf_op jit(solution)/shard_map/finish/pallas_call | solution.py:288
Async XLA Ops:
  0.0 0.7 copy-start.3
  1.6 51.0 %copy-start.4 = (bf16[2,48,128]{2,1,0:T(8,128)(2,1)S(1)}, bf16[2,48,128]{2,1,0:T(8,128)(2,1)}, u32[]{:S(2)}) copy-start(bf16[2,48,128]{2,1,0:T(8,128)(2,1)} %constant.36.clone.high_ref) | copy-start | bytes 73732
  1.6 51.1 %copy-start.5 = (bf16[2,48,128]{2,1,0:T(8,128)(2,1)S(1)}, bf16[2,48,128]{2,1,0:T(8,128)(2,1)}, u32[]{:S(2)}) copy-start(bf16[2,48,128]{2,1,0:T(8,128)(2,1)} %constant.37.clone.low_ref) | copy-start | bytes 73732
  1.6 42.1 %all-to-all-start = ((f32[16,56,128]{2,1,0:T(8,128)}), f32[16,56,128]{2,1,0:T(8,128)S(1)}, u32[]{:S(2)}, u32[]{:S(2)}) async-start(f32[16,56,128]{2,1,0:T(8,128)} %get-tuple-element.20), calls=%async_computation | async-start | bytes 917504 | tf_op jit(solution)/shard_map/all_to_all | solution.py:299
  43.7 31.4 %copy-start.2 = (bf16[4,48,144]{2,1,0:T(8,128)(2,1)S(1)}, bf16[4,48,144]{2,1,0:T(8,128)(2,1)}, u32[]{:S(2)}) copy-start(bf16[4,48,144]{2,1,0:T(8,128)(2,1)} %constant.38.clone.left_ref) | copy-start | bytes 165892
  43.7 20.0 %all-to-all-start.1 = ((f32[16,56,128]{2,1,0:T(8,128)}), f32[16,56,128]{2,1,0:T(8,128)S(1)}, u32[]{:S(2)}, u32[]{:S(2)}) async-start(f32[16,56,128]{2,1,0:T(8,128)} %all-gather.1), calls=%async_computation.1 | async-start | bytes 917504 | tf_op jit(solution)/shard_map/all_to_all | solution.py:299
  52.9 1.0 copy-start
  63.7 11.4 %copy-start.1 = (bf16[2,2,256,512]{3,2,1,0:T(8,128)(2,1)S(1)}, bf16[2,2,256,512]{3,2,1,0:T(8,128)(2,1)}, u32[]{:S(2)}) copy-start(bf16[2,2,256,512]{3,2,1,0:T(8,128)(2,1)} %copy-done) | copy-start | bytes 3145732
  79.7 18.0 %all-to-all-start.2 = ((f32[16,56,128]{2,1,0:T(8,128)}), f32[16,56,128]{2,1,0:T(8,128)S(1)}, u32[]{:S(2)}, u32[]{:S(2)}) async-start(f32[16,56,128]{2,1,0:T(8,128)} %bitcast.5), calls=%async_computation.2 | async-start | bytes 917504 | tf_op jit(solution)/shard_map/all_to_all | solution.py:299
  114.0 14.6 %all-to-all-start.4 = ((f32[16,56,128]{2,1,0:T(8,128)}), f32[16,56,128]{2,1,0:T(8,128)S(1)}, u32[]{:S(2)}, u32[]{:S(2)}) async-start(f32[16,56,128]{2,1,0:T(8,128)} %attach.1), calls=%async_computation.4 | async-start | bytes 917504 | tf_op jit(solution)/shard_map/all_to_all | solution.py:299

commit v6 on v5

--- a/solution.py
+++ b/solution.py
@@ -19,6 +19,7 @@
 CHIPS = BANDS // 2
 PAIR, CORE, GRID = ("xl", "z4", "z2", "z1"), ("c",), ("xh", "y4", "y2", "y1")
 BAND = PAIR + CORE
+PITCH = 56
 f32, bf16 = jnp.float32, jnp.bfloat16
 SMALL = pltpu.CompilerParams(vmem_limit_bytes=12 << 20)
 LARGE = pltpu.CompilerParams(vmem_limit_bytes=24 << 20)
@@ -114,9 +115,9 @@
 def exchange_kernel(
     own_ref, pair_ref, left_ref, wide_high, wide_low, coulomb, out_ref, rho_h, rho_l, za, zb, sol_h, sol_l
 ):
-    def column(ref, first, c):
+    def column(ref, first, c, step=ROWS):
         return jnp.concatenate(
-            [ref[pl.ds(first + COLS * p + c, SLABS, stride=ROWS), :] for p in range(PLANES)], 0
+            [ref[pl.ds(first + COLS * p + c, SLABS, stride=step), :] for p in range(PLANES)], 0
         )
 
     def partner(d, c):
@@ -126,7 +127,7 @@
         return slice(48 * (c // 3), 48 * (c // 3) + 48), slice(128 * (c % 3), 128 * (c % 3) + 128)
 
     for c in range(COLS):
-        own = column(own_ref, 0, c)
+        own = column(own_ref, 0, c, 2 * ROWS)
         rows, cols = place(c)
         for d in range(2):
             high, low = split(own * partner(d, c))
@@ -142,21 +143,25 @@
         for c in range(6):
             for i in range(4):
                 y = 8 * c + 4 * w + i
-                za[48 * y : 48 * y + 48, :] = out[48 * c : 48 * c + 48, 128 * i : 128 * i + 128]
+                za[PITCH * y : PITCH * y + NG, :] = out[48 * c : 48 * c + 48, 128 * i : 128 * i + 128]
+
+    def planes(ref, k):
+        return jnp.concatenate([ref[PITCH * i : PITCH * i + NG, :] for i in (k, k + 1)], 1)
+
+    def across(ref, k):
+        return jnp.concatenate([ref[pl.ds(i, NG, stride=PITCH), :] for i in (k, k + 1)], 1)
+
+    def put(ref, k, both):
+        for e in range(2):
+            ref[PITCH * (k + e) : PITCH * (k + e) + NG, :] = both[:, 128 * e : 128 * e + 128]
+
     for y in range(0, NG, 2):
-        both = jnp.concatenate([za[48 * y : 48 * y + 48, :], za[48 * y + 48 : 48 * y + 96, :]], 1)
-        both = left_mul(left_ref[0], both)
-        zb[48 * y : 48 * y + 48, :] = both[:, :128]
-        zb[48 * y + 48 : 48 * y + 96, :] = both[:, 128:]
+        put(zb, y, left_mul(left_ref[0], planes(za, y)))
     for k in range(0, NG, 2):
-        both = jnp.concatenate([zb[pl.ds(k, 48, stride=48), :], zb[pl.ds(k + 1, 48, stride=48), :]], 1)
-        both = left_mul(left_ref[1], both) * jnp.concatenate([coulomb[k], coulomb[k + 1]], 1)
-        both = left_mul(left_ref[2], both)
-        za[pl.ds(k, 48, stride=48), :] = both[:, :128]
-        za[pl.ds(k + 1, 48, stride=48), :] = both[:, 128:]
+        both = left_mul(left_ref[1], across(zb, k)) * jnp.concatenate([coulomb[k], coulomb[k + 1]], 1)
+        put(za, k, left_mul(left_ref[2], both))
     for y in range(0, NG, 2):
-        both = jnp.concatenate([za[48 * y : 48 * y + 48, :], za[48 * y + 48 : 48 * y + 96, :]], 1)
-        both = left_mul(left_ref[3], both)
+        both = left_mul(left_ref[3], across(za, y))
         for e in range(2):
             c, w, i = (y + e) // 8, ((y + e) % 8) // 4, (y + e) % 4
             high, low = split(both[:, 128 * e : 128 * e + 128])
@@ -180,7 +185,7 @@
 
 
 def partial_exchange(own, pair, made):
-    big = pltpu.VMEM((NG * NG, 128), f32)
+    big = pltpu.VMEM((NG * PITCH, 128), f32)
     rho, solved = pltpu.VMEM((2, 288, 384), bf16), pltpu.VMEM((2, 288, 512), bf16)
     return pl.pallas_call(
         exchange_kernel,
@@ -198,14 +203,30 @@
             r = COLS * p + c
             tile_ref[r : r + 1, :] = slab_ref[p, :, 128 * c : 128 * c + 128]
     tile = tile_ref[...]
-    for k in range(SLABS):
+    for k in range(CHIPS):
         copies_ref[k] = tile
 
 
 def prepare(slab):
     tile = jax.ShapeDtypeStruct((ROWS, 128), f32)
-    copies = jax.ShapeDtypeStruct((SLABS, ROWS, 128), f32)
+    copies = jax.ShapeDtypeStruct((CHIPS, ROWS, 128), f32)
     return pl.pallas_call(prepare_kernel, out_shape=(tile, copies), name="prepare", compiler_params=SMALL)(slab)
+
+
+def join_kernel(tile_ref, chips_ref, out_ref):
+    tile = tile_ref[...]
+    for k in range(SLABS):
+        out_ref[k, :ROWS, :] = tile
+        out_ref[k, ROWS:, :] = chips_ref[k]
+
+
+def join(tile, chips):
+    return pl.pallas_call(
+        join_kernel,
+        out_shape=jax.ShapeDtypeStruct((SLABS, 2 * ROWS, 128), f32),
+        name="join",
+        compiler_params=SMALL,
+    )(tile, chips)
 
 
 def column_kernel(share_ref, orbital_ref, field_ref, copies_ref):
@@ -249,8 +270,8 @@
     return (band % 2) * CHIPS + band // 2
 
 
-def finish_kernel(band_ref, field_ref, out_ref, flat):
-    band = band_ref[0]
+def finish_kernel(field_ref, out_ref, flat):
+    mine = lax.axis_index(CORE + PAIR)
     matrix = field_ref[pl.ds(USED, BANDS, stride=ROWS), :][:, :BANDS]
     definite = (matrix + matrix.T) * (-0.5 / float(NG**3))
     row = lax.broadcasted_iota(jnp.int32, (BANDS, 2 * BANDS), 0)
@@ -268,7 +289,6 @@
                 columns[j] = columns[j] - factor * columns[j][at[i] : at[i] + 1, :]
                 pivots[j] = pivots[j] - factor[at[j] : at[j] + 1, :] * pivots[i]
             state = state - factor * pivots[i]
-    mine = (band % 2) * CHIPS + band // 2
     picked = jnp.sum(jnp.where(row == mine, state, 0.0), axis=0, keepdims=True)
     pivot = jnp.sum(jnp.where(lane[:1] == mine, picked, 0.0), axis=1, keepdims=True)
     weights = picked * lax.rsqrt(pivot)
@@ -284,15 +304,14 @@
             out_ref[p, :, 128 * c : 128 * c + 128] = flat[r : r + 1, :]
 
 
-def finish(band, fields):
+def finish(fields):
     return pl.pallas_call(
         finish_kernel,
         out_shape=jax.ShapeDtypeStruct((PLANES, 1, NG * NG), f32),
-        in_specs=[pl.BlockSpec(memory_space=pltpu.SMEM), pl.BlockSpec(memory_space=pltpu.VMEM)],
         scratch_shapes=[pltpu.VMEM((ROWS, 128), f32)],
         name="finish",
         compiler_params=SMALL,
-    )(band, fields)
+    )(fields)
 
 
 def exchange_tiles(tiles, axis):
@@ -305,19 +324,16 @@
 
 def per_device(orbitals):
     tile, copies = prepare(jnp.transpose(orbitals, (1, 0, 2)))
-    own = exchange_tiles(copies, GRID)
-    chips = lax.all_gather(lax.all_gather(tile, ("z4", "z2", "z1")), "xl").reshape(CHIPS, ROWS, 128)
-    last = (jnp.asarray(LAST_HIGH), jnp.asarray(LAST_LOW))
-    own, chips, *last = lax.optimization_barrier((own, chips, *last))
-    pair, *made = lax.optimization_barrier((exchange_tiles(chips, GRID), *tables(*last)))
-    pair = both_cores(pair)
-    partial = partial_exchange(own.reshape(SLABS * ROWS, 128), pair, made)
+    made = tables(jnp.asarray(LAST_HIGH), jnp.asarray(LAST_LOW))
+    chips = exchange_tiles(copies, PAIR)
+    whole = exchange_tiles(join(tile, chips), GRID)
+    pair = both_cores(whole[:, ROWS:])
+    partial = partial_exchange(whole.reshape(SLABS * 2 * ROWS, 128), pair, made)
     shares = exchange_tiles(partial.reshape(SLABS, ROWS, 128), GRID)
     field, lines = column_part(shares, both_cores(chips))
     parts = exchange_tiles(lines, GRID)
     fields = both_cores(exchange_tiles(attach(field, parts), PAIR))
-    band = lax.axis_index(BAND).astype(jnp.int32).reshape(1)
-    return jnp.transpose(finish(band, fields), (1, 0, 2))
+    return jnp.transpose(finish(fields), (1, 0, 2))
 
 
 def solution(mesh):

time: 138 us -> 127 us (0.920)
  starting transfers between devices: 27.3 us -> 13.9 us
  blocking collectives: 67.4 us -> 72.6 us
  waiting for transfers between devices: 31.4 us -> 28.8 us
    all_to_all x1 -> x3, blocking collectives: 15.2 us -> 55.5 us  [exchange_tiles(): return lax.all_to_all(tiles, axis, 0, 0, tiled=True)]
    all_gather x2 -> x0, blocking collectives: 31.8 us -> none  [the longest x1 25.9 us: per_device(): lax.all_gather(tile, ('z4', 'z2', 'z1'))]
    all_to_all x4 -> x2, starting transfers between devices: 27.3 us -> 13.9 us  [exchange_tiles(): return lax.all_to_all(tiles, axis, 0, 0, tiled=True)]
    all_gather x3, blocking collectives: 20.4 us -> 17.1 us  [both_cores(): return lax.all_gather(chips, CORE, axis=0, tiled=False).reshape(-1, 128)]
    all_to_all x4 -> x2, waiting for transfers between devices: 31.4 us -> 28.8 us  [exchange_tiles(): return lax.all_to_all(tiles, axis, 0, 0, tiled=True)]
  transfers between devices with their start and end apart: 4 -> 2, of which waited for: 3 -> 2; matrix products, arithmetic and copies ran while one was open for 0% -> 0% of each run, Pallas kernels for 0% -> 0%
where the time goes in v6:
time: 127 us; the launch traced here: 126 us
  blocking collectives  72.6 us (57%)
  waiting for transfers between devices  28.8 us (23%)
  starting transfers between devices  13.9 us (11%)
  Pallas kernels  8.4 us (7%)
  local copies, waits for them, and re-layouts  2.77 us (2%)
    all_to_all x3, blocking collectives, exchange_tiles(): return lax.all_to_all(tiles, axis, 0, 0, tiled=True)  55.5 us
    all_to_all x2, waiting for transfers between devices, exchange_tiles(): return lax.all_to_all(tiles, axis, 0, 0, tiled=True)  28.8 us
    all_gather x3, blocking collectives, both_cores(): return lax.all_gather(chips, CORE, axis=0, tiled=False).reshape(-1, 128)  17.1 us
    all_to_all x2, starting transfers between devices, exchange_tiles(): return lax.all_to_all(tiles, axis, 0, 0, tiled=True)  13.9 us
    pallas_call x1, Pallas kernels, partial_exchange(): pl.pallas_call(exchange_kernel, out_shape=jax.ShapeDtypeStruct((SLABS * R...  4.6 us
    unnamed x16, local copies, waits for them, and re-layouts  2.74 us
  transfers between devices with their start and end apart: 2, of which 2 were waited for; matrix products, arithmetic and copies ran while one was open for 0% of the time, Pallas kernels for 0%

profile of v6, /device:TPU:1, one launch (start us, length us, event | category | flops | bytes accessed | tf_op | source)
XLA Modules:
  0.0 126.5 jit_solution(6193037585816691438)
XLA Ops:
  0.0 0.0 copy-start.5
  0.0 0.7 copy-done.5
  0.8 23.6 %all_to_all.25.chips_ref = f32[16,56,128]{2,1,0:T(8,128)S(1)} all-to-all(f32[16,56,128]{2,1,0:T(8,128)S(1)} %get-tuple-element.13), channel_id=1, replica_groups=mesh['xl'=2,'z4'=2,'z2'=2,'z1'=2,'c'=2,'xh'=2,'y4'=2,'y2'=2,'y1'=2] {'xl..., dimensions={0} | all-to-all | bytes 917504 | tf_op jit(solution)/shard_map/all_to_all | solution.py:318
  24.4 1.0 join.1
  25.4 0.0 copy-start.6
  25.4 0.0 copy-start.7
  25.4 9.2 %all-to-all-start.1 = ((f32[16,112,128]{2,1,0:T(8,128)}), f32[16,112,128]{2,1,0:T(8,128)S(1)}, u32[]{:S(2)}, u32[]{:S(2)}) async-start(f32[16,112,128]{2,1,0:T(8,128)} %join.1), calls=%async_computation.1 | async-start | bytes 1835008 | tf_op jit(solution)/shard_map/all_to_all | solution.py:318
  34.6 0.0 copy-done.6
  34.7 0.0 copy-done.7
  34.7 0.0 copy-start.4
  34.7 0.3 tables.1
  35.0 0.0 copy-start
  35.0 1.0 copy-done
  36.0 0.0 copy-start.2
  36.0 1.0 copy-done.2
  37.0 17.8 %all-to-all-done.1 = f32[16,112,128]{2,1,0:T(8,128)S(1)} async-done(((f32[16,112,128]{2,1,0:T(8,128)}), f32[16,112,128]{2,1,0:T(8,128)S(1)}, u32[]{:S(2)}, u32[]{:S(2)}) %all-to-all-start.1) | async-done | bytes 917536 | tf_op jit(solution)/shard_map/all_to_all | solution.py:318
  54.8 0.0 copy-start.1
  54.8 0.0 copy-start.3
  54.8 8.3 %all-gather = f32[32,56,128]{2,1,0:T(8,128)S(1)} all-gather(f32[16,56,128]{2,1,0:T(8,128)S(1)} %slice.4), channel_id=2, replica_groups=mesh['xl'=2,'z4'=2,'z2'=2,'z1'=2,'c'=2,'xh'=2,'y4'=2,'y2'=2,'y1'=2] {'c'}, dimensions={0}, use_global_device_ids=true | all-gather | bytes 1376256 | tf_op jit(solution)/shard_map/all_gather | solution.py:322
  63.1 0.0 copy-done.4
  63.1 0.0 copy-done.1
  63.1 0.0 copy-done.3
  63.1 4.6 %exchange.1 = f32[896,128]{1,0:T(8,128)} custom-call(f32[1792,128]{1,0:T(8,128)S(1)} %bitcast.7, f32[1792,128]{1,0:T(8,128)S(1)} %bitcast.10, bf16[4,48,144]{2,1,0:T(8,128)(2,1)S(1)} %copy-done.4, bf16[2,2,256,512]{3,2,1,0:T(8,128)(2,1)S(1)} %copy-done.1, bf16[2,2,256,512]{3,2,1,0:T(8,128)(2,1)S(1)} %copy-done.3, f32[48,48,128]{2,1,0:T(8,128)S(1)} %get-tuple-element.16.coulomb), custom_call_target="tpu_custom_call" | custom-call | tf_op jit(solution)/shard_map/exchange/pallas_call | solution.py:190
  67.7 4.6 %all-to-all-start.2 = ((f32[16,56,128]{2,1,0:T(8,128)}), f32[16,56,128]{2,1,0:T(8,128)S(1)}, u32[]{:S(2)}, u32[]{:S(2)}) async-start(f32[16,56,128]{2,1,0:T(8,128)} %bitcast.3), calls=%async_computation.2 | async-start | bytes 917504 | tf_op jit(solution)/shard_map/all_to_all | solution.py:318
  72.4 2.7 %all-gather.1 = f32[32,56,128]{2,1,0:T(8,128)S(1)} all-gather(f32[16,56,128]{2,1,0:T(8,128)S(1)} %all_to_all.25.chips_ref), channel_id=3, replica_groups=mesh['xl'=2,'z4'=2,'z2'=2,'z1'=2,'c'=2,'xh'=2,'y4'=2,'y2'=2,'y1'=2] {'c'}, dimensions={0}, use_global_device_ids=true | all-gather | bytes 1376256 | tf_op jit(solution)/shard_map/all_gather | solution.py:322
  75.1 10.9 %all-to-all-done.2.share_ref = f32[16,56,128]{2,1,0:T(8,128)S(1)} async-done(((f32[16,56,128]{2,1,0:T(8,128)}), f32[16,56,128]{2,1,0:T(8,128)S(1)}, u32[]{:S(2)}, u32[]{:S(2)}) %all-to-all-start.2) | async-done | bytes 458784 | tf_op jit(solution)/shard_map/all_to_all | solution.py:318
  86.1 0.2 column.1
  86.3 15.2 %all_to_all.26.parts_ref = f32[16,8,128]{2,1,0:T(8,128)S(1)} all-to-all(f32[16,8,128]{2,1,0:T(8,128)S(1)} %get-tuple-element.18), channel_id=1, replica_groups=mesh['xl'=2,'z4'=2,'z2'=2,'z1'=2,'c'=2,'xh'=2,'y4'=2,'y2'=2,'y1'=2] {'xh..., dimensions={0} | all-to-all | bytes 131072 | tf_op jit(solution)/shard_map/all_to_all | solution.py:318
  101.5 16.6 %all_to_all.27 = f32[16,56,128]{2,1,0:T(8,128)S(1)} all-to-all(f32[16,56,128]{2,1,0:T(8,128)S(1)} %attach.1), channel_id=1, replica_groups=mesh['xl'=2,'z4'=2,'z2'=2,'z1'=2,'c'=2,'xh'=2,'y4'=2,'y2'=2,'y1'=2] {'xl..., dimensions={0} | all-to-all | bytes 917504 | tf_op jit(solution)/shard_map/all_to_all | solution.py:318
  118.2 6.1 %all-gather.2 = f32[32,56,128]{2,1,0:T(8,128)S(1)} all-gather(f32[16,56,128]{2,1,0:T(8,128)S(1)} %all_to_all.27), channel_id=4, replica_groups=mesh['xl'=2,'z4'=2,'z2'=2,'z1'=2,'c'=2,'xh'=2,'y4'=2,'y2'=2,'y1'=2] {'c'}, dimensions={0}, use_global_device_ids=true | all-gather | bytes 1376256 | tf_op jit(solution)/shard_map/all_gather | solution.py:322
  124.3 2.2 %finish.1 = f32[3,1,2304]{2,1,0:T(1,128)} custom-call(f32[1792,128]{1,0:T(8,128)S(1)} %bitcast.9), custom_call_target="tpu_custom_call" | custom-call | tf_op jit(solution)/shard_map/finish/pallas_call | solution.py:308
  (3 shorter events, 0.1 us)
Async XLA Ops:
  0.0 0.7 copy-start.5
  25.4 9.2 %copy-start.6 = (bf16[2,48,128]{2,1,0:T(8,128)(2,1)S(1)}, bf16[2,48,128]{2,1,0:T(8,128)(2,1)}, u32[]{:S(2)}) copy-start(bf16[2,48,128]{2,1,0:T(8,128)(2,1)} %constant.6.clone.high_ref) | copy-start | bytes 73732
  25.4 9.2 %copy-start.7 = (bf16[2,48,128]{2,1,0:T(8,128)(2,1)S(1)}, bf16[2,48,128]{2,1,0:T(8,128)(2,1)}, u32[]{:S(2)}) copy-start(bf16[2,48,128]{2,1,0:T(8,128)(2,1)} %constant.7.clone.low_ref) | copy-start | bytes 73732
  25.4 29.4 %all-to-all-start.1 = ((f32[16,112,128]{2,1,0:T(8,128)}), f32[16,112,128]{2,1,0:T(8,128)S(1)}, u32[]{:S(2)}, u32[]{:S(2)}) async-start(f32[16,112,128]{2,1,0:T(8,128)} %join.1), calls=%async_computation.1 | async-start | bytes 1835008 | tf_op jit(solution)/shard_map/all_to_all | solution.py:318
  34.7 28.5 %copy-start.4 = (bf16[4,48,144]{2,1,0:T(8,128)(2,1)S(1)}, bf16[4,48,144]{2,1,0:T(8,128)(2,1)}, u32[]{:S(2)}) copy-start(bf16[4,48,144]{2,1,0:T(8,128)(2,1)} %constant.8.clone.left_ref) | copy-start | bytes 165892
  35.0 1.0 copy-start
  36.0 1.0 copy-start.2
  54.8 8.3 %copy-start.1 = (bf16[2,2,256,512]{3,2,1,0:T(8,128)(2,1)S(1)}, bf16[2,2,256,512]{3,2,1,0:T(8,128)(2,1)}, u32[]{:S(2)}) copy-start(bf16[2,2,256,512]{3,2,1,0:T(8,128)(2,1)} %copy-done) | copy-start | bytes 3145732
  54.8 8.3 %copy-start.3 = (bf16[2,2,256,512]{3,2,1,0:T(8,128)(2,1)S(1)}, bf16[2,2,256,512]{3,2,1,0:T(8,128)(2,1)}, u32[]{:S(2)}) copy-start(bf16[2,2,256,512]{3,2,1,0:T(8,128)(2,1)} %copy-done.2) | copy-start | bytes 3145732
  67.7 18.3 %all-to-all-start.2 = ((f32[16,56,128]{2,1,0:T(8,128)}), f32[16,56,128]{2,1,0:T(8,128)S(1)}, u32[]{:S(2)}, u32[]{:S(2)}) async-start(f32[16,56,128]{2,1,0:T(8,128)} %bitcast.3), calls=%async_computation.2 | async-start | bytes 917504 | tf_op jit(solution)/shard_map/all_to_all | solution.py:318

commit v7 on v6

--- a/solution.py
+++ b/solution.py
@@ -123,16 +123,19 @@
     def partner(d, c):
         return column(pair_ref, d * SLABS * ROWS, c)
 
-    def place(c):
-        return slice(48 * (c // 3), 48 * (c // 3) + 48), slice(128 * (c % 3), 128 * (c % 3) + 128)
-
-    for c in range(COLS):
-        own = column(own_ref, 0, c, 2 * ROWS)
-        rows, cols = place(c)
-        for d in range(2):
-            high, low = split(own * partner(d, c))
-            rho_h[d, rows, cols] = high
-            rho_l[d, rows, cols] = low
+    def rows_of(c):
+        return pl.ds(pl.multiple_of(NG * c, 16), NG)
+
+    def densities(c, _):
+        for k in range(3):
+            own = column(own_ref, 0, 3 * c + k, 2 * ROWS)
+            for d in range(2):
+                high, low = split(own * partner(d, 3 * c + k))
+                rho_h[d, rows_of(c), 128 * k : 128 * k + 128] = high
+                rho_l[d, rows_of(c), 128 * k : 128 * k + 128] = low
+        return 0
+
+    lax.fori_loop(0, 6, densities, 0)
     for w in range(2):
         window = slice(128 * w, 128 * w + 256)
         out = None
@@ -145,28 +148,44 @@
                 y = 8 * c + 4 * w + i
                 za[PITCH * y : PITCH * y + NG, :] = out[48 * c : 48 * c + 48, 128 * i : 128 * i + 128]
 
+    def plane(k):
+        return pl.ds(pl.multiple_of(PITCH * k, 8), NG)
+
     def planes(ref, k):
-        return jnp.concatenate([ref[PITCH * i : PITCH * i + NG, :] for i in (k, k + 1)], 1)
+        return jnp.concatenate([ref[plane(k), :], ref[plane(k + 1), :]], 1)
 
     def across(ref, k):
         return jnp.concatenate([ref[pl.ds(i, NG, stride=PITCH), :] for i in (k, k + 1)], 1)
 
     def put(ref, k, both):
         for e in range(2):
-            ref[PITCH * (k + e) : PITCH * (k + e) + NG, :] = both[:, 128 * e : 128 * e + 128]
-
-    for y in range(0, NG, 2):
-        put(zb, y, left_mul(left_ref[0], planes(za, y)))
-    for k in range(0, NG, 2):
-        both = left_mul(left_ref[1], across(zb, k)) * jnp.concatenate([coulomb[k], coulomb[k + 1]], 1)
-        put(za, k, left_mul(left_ref[2], both))
-    for y in range(0, NG, 2):
-        both = left_mul(left_ref[3], across(za, y))
-        for e in range(2):
-            c, w, i = (y + e) // 8, ((y + e) % 8) // 4, (y + e) % 4
-            high, low = split(both[:, 128 * e : 128 * e + 128])
-            sol_h[w, 48 * c : 48 * c + 48, 128 * i : 128 * i + 128] = high
-            sol_l[w, 48 * c : 48 * c + 48, 128 * i : 128 * i + 128] = low
+            ref[plane(k + e), :] = both[:, 128 * e : 128 * e + 128]
+
+    def first_edge(c, _):
+        for j in range(0, 8, 2):
+            put(zb, 8 * c + j, left_mul(left_ref[0], planes(za, 8 * c + j)))
+        return 0
+
+    def middle_edge(c, _):
+        for j in range(0, 8, 2):
+            k = 8 * c + j
+            both = left_mul(left_ref[1], across(zb, k)) * jnp.concatenate([coulomb[k], coulomb[k + 1]], 1)
+            put(za, k, left_mul(left_ref[2], both))
+        return 0
+
+    def first_edge_back(c, _):
+        for j in range(0, 8, 2):
+            both = left_mul(left_ref[3], across(za, 8 * c + j))
+            for e in range(2):
+                w, i = (j + e) // 4, (j + e) % 4
+                high, low = split(both[:, 128 * e : 128 * e + 128])
+                sol_h[w, rows_of(c), 128 * i : 128 * i + 128] = high
+                sol_l[w, rows_of(c), 128 * i : 128 * i + 128] = low
+        return 0
+
+    lax.fori_loop(0, 6, first_edge, 0)
+    lax.fori_loop(0, 6, middle_edge, 0)
+    lax.fori_loop(0, 6, first_edge_back, 0)
     thirds = []
     for d in range(2):
         a, b = [
@@ -175,7 +194,7 @@
         ]
         thirds.append((a[:, :128], a[:, 128:] + b[:, :128], b[:, 128:]))
     for c in range(COLS):
-        rows, _ = place(c)
+        rows = slice(48 * (c // 3), 48 * (c // 3) + 48)
         out = thirds[0][c % 3][rows] * partner(0, c)
         out = out + thirds[1][c % 3][rows] * partner(1, c)
         for p in range(PLANES):
@@ -326,11 +345,11 @@
     tile, copies = prepare(jnp.transpose(orbitals, (1, 0, 2)))
     made = tables(jnp.asarray(LAST_HIGH), jnp.asarray(LAST_LOW))
     chips = exchange_tiles(copies, PAIR)
-    whole = exchange_tiles(join(tile, chips), GRID)
+    whole, others = lax.optimization_barrier((exchange_tiles(join(tile, chips), GRID), both_cores(chips)))
     pair = both_cores(whole[:, ROWS:])
     partial = partial_exchange(whole.reshape(SLABS * 2 * ROWS, 128), pair, made)
     shares = exchange_tiles(partial.reshape(SLABS, ROWS, 128), GRID)
-    field, lines = column_part(shares, both_cores(chips))
+    field, lines = column_part(shares, others)
     parts = exchange_tiles(lines, GRID)
     fields = both_cores(exchange_tiles(attach(field, parts), PAIR))
     return jnp.transpose(finish(fields), (1, 0, 2))

time: 127 us -> 129 us (1.016)
  blocking collectives: 72.6 us -> 93.4 us
  waiting for transfers between devices: 28.8 us -> 12.4 us
  starting transfers between devices: 13.9 us -> 9.22 us
  Pallas kernels: 8.4 us -> 10.7 us
    all_to_all x3 -> x4, blocking collectives: 55.5 us -> 73.6 us  [exchange_tiles(): return lax.all_to_all(tiles, axis, 0, 0, tiled=True)]
    all_to_all x2 -> x1, waiting for transfers between devices: 28.8 us -> 12.4 us  [exchange_tiles(): return lax.all_to_all(tiles, axis, 0, 0, tiled=True)]
    all_to_all x2 -> x1, starting transfers between devices: 13.9 us -> 9.22 us  [exchange_tiles(): return lax.all_to_all(tiles, axis, 0, 0, tiled=True)]
    all_gather x3, blocking collectives: 17.1 us -> 19.8 us  [both_cores(): return lax.all_gather(chips, CORE, axis=0, tiled=False).reshape(-1, 128)]
    pallas_call x1, Pallas kernels: 4.6 us -> 6.92 us  [partial_exchange(): pl.pallas_call(exchange_kernel, out_shape=jax.ShapeDtypeStruct((SLABS * R...]
  transfers between devices with their start and end apart: 2 -> 1, of which waited for: 2 -> 1; matrix products, arithmetic and copies ran while one was open for 0% -> 0% of each run, Pallas kernels for 0% -> 0%
where the time goes in v7:
time: 129 us
  blocking collectives  93.4 us (72%)
  waiting for transfers between devices  12.4 us (10%)
  Pallas kernels  10.7 us (8%)
  starting transfers between devices  9.22 us (7%)
  local copies, waits for them, and re-layouts  2.76 us (2%)
    all_to_all x4, blocking collectives, exchange_tiles(): return lax.all_to_all(tiles, axis, 0, 0, tiled=True)  73.6 us
    all_gather x3, blocking collectives, both_cores(): return lax.all_gather(chips, CORE, axis=0, tiled=False).reshape(-1, 128)  19.8 us
    all_to_all x1, waiting for transfers between devices, exchange_tiles(): return lax.all_to_all(tiles, axis, 0, 0, tiled=True)  12.4 us
    all_to_all x1, starting transfers between devices, exchange_tiles(): return lax.all_to_all(tiles, axis, 0, 0, tiled=True)  9.22 us
    pallas_call x1, Pallas kernels, partial_exchange(): pl.pallas_call(exchange_kernel, out_shape=jax.ShapeDtypeStruct((SLABS * R...  6.92 us
    unnamed x16, local copies, waits for them, and re-layouts  2.73 us
  transfers between devices with their start and end apart: 1, of which 1 were waited for; matrix products, arithmetic and copies ran while one was open for 0% of the time, Pallas kernels for 0%

profile of v7, /device:TPU:1, one launch (start us, length us, event | category | flops | bytes accessed | tf_op | source)
XLA Modules:
  0.0 128.6 jit_solution(1414839842060057378)
XLA Ops:
  0.0 0.0 copy-start.5
  0.0 0.7 copy-done.5
  0.8 23.6 %all_to_all.25.chips_ref = f32[16,56,128]{2,1,0:T(8,128)S(1)} all-to-all(f32[16,56,128]{2,1,0:T(8,128)S(1)} %get-tuple-element.15), channel_id=1, replica_groups=mesh['xl'=2,'z4'=2,'z2'=2,'z1'=2,'c'=2,'xh'=2,'y4'=2,'y2'=2,'y1'=2] {'xl..., dimensions={0} | all-to-all | bytes 917504 | tf_op jit(solution)/shard_map/all_to_all | solution.py:337
  24.4 1.0 join.1
  25.4 0.0 copy-start.6
  25.4 0.0 copy-start.7
  25.4 9.2 %all-to-all-start.1 = ((f32[16,112,128]{2,1,0:T(8,128)}), f32[16,112,128]{2,1,0:T(8,128)S(1)}, u32[]{:S(2)}, u32[]{:S(2)}) async-start(f32[16,112,128]{2,1,0:T(8,128)} %join.1), calls=%async_computation.1 | async-start | bytes 1835008 | tf_op jit(solution)/shard_map/all_to_all | solution.py:337
  34.6 0.0 copy-done.6
  34.6 0.0 copy-done.7
  34.7 0.3 tables.1
  35.0 0.0 copy-start
  35.0 1.0 copy-done
  35.9 0.0 copy-start.2
  35.9 1.0 copy-done.2
  36.9 5.4 %all-gather = f32[32,56,128]{2,1,0:T(8,128)S(1)} all-gather(f32[16,56,128]{2,1,0:T(8,128)S(1)} %all_to_all.25.chips_ref), channel_id=2, replica_groups=mesh['xl'=2,'z4'=2,'z2'=2,'z1'=2,'c'=2,'xh'=2,'y4'=2,'y2'=2,'y1'=2] {'c'}, dimensions={0}, use_global_device_ids=true | all-gather | bytes 1376256 | tf_op jit(solution)/shard_map/all_gather | solution.py:341
  42.3 12.4 %all-to-all-done.1 = f32[16,112,128]{2,1,0:T(8,128)S(1)} async-done(((f32[16,112,128]{2,1,0:T(8,128)}), f32[16,112,128]{2,1,0:T(8,128)S(1)}, u32[]{:S(2)}, u32[]{:S(2)}) %all-to-all-start.1) | async-done | bytes 917536 | tf_op jit(solution)/shard_map/all_to_all | solution.py:337
  54.8 0.0 copy-start.1
  54.8 0.0 copy-start.3
  54.8 0.0 copy-start.4
  54.8 8.3 %all-gather.1 = f32[32,56,128]{2,1,0:T(8,128)S(1)} all-gather(f32[16,56,128]{2,1,0:T(8,128)S(1)} %slice.3), channel_id=3, replica_groups=mesh['xl'=2,'z4'=2,'z2'=2,'z1'=2,'c'=2,'xh'=2,'y4'=2,'y2'=2,'y1'=2] {'c'}, dimensions={0}, use_global_device_ids=true | all-gather | bytes 1376256 | tf_op jit(solution)/shard_map/all_gather | solution.py:341
  63.1 0.0 copy-done.1
  63.1 0.0 copy-done.3
  63.1 0.0 copy-done.4
  63.1 6.9 %exchange.1 = f32[896,128]{1,0:T(8,128)S(1)} custom-call(f32[1792,128]{1,0:T(8,128)S(1)} %bitcast.7, f32[1792,128]{1,0:T(8,128)S(1)} %bitcast.10, bf16[4,48,144]{2,1,0:T(8,128)(2,1)S(1)} %copy-done.4, bf16[2,2,256,512]{3,2,1,0:T(8,128)(2,1)S(1)} %copy-done.1, bf16[2,2,256,512]{3,2,1,0:T(8,128)(2,1)S(1)} %copy-done.3, ...), custom_call_target="tpu_custom_call" | custom-call | tf_op jit(solution)/shard_map/exchange/pallas_call | solution.py:209
  70.0 18.1 %all_to_all.26.share_ref = f32[16,56,128]{2,1,0:T(8,128)S(1)} all-to-all(f32[16,56,128]{2,1,0:T(8,128)S(1)} %bitcast.11), channel_id=1, replica_groups=mesh['xl'=2,'z4'=2,'z2'=2,'z1'=2,'c'=2,'xh'=2,'y4'=2,'y2'=2,'y1'=2] {'xh..., dimensions={0} | all-to-all | bytes 917504 | tf_op jit(solution)/shard_map/all_to_all | solution.py:337
  88.2 0.2 column.1
  88.4 15.2 %all_to_all.27.parts_ref = f32[16,8,128]{2,1,0:T(8,128)S(1)} all-to-all(f32[16,8,128]{2,1,0:T(8,128)S(1)} %get-tuple-element.22), channel_id=1, replica_groups=mesh['xl'=2,'z4'=2,'z2'=2,'z1'=2,'c'=2,'xh'=2,'y4'=2,'y2'=2,'y1'=2] {'xh..., dimensions={0} | all-to-all | bytes 131072 | tf_op jit(solution)/shard_map/all_to_all | solution.py:337
  103.6 16.6 %all_to_all.28 = f32[16,56,128]{2,1,0:T(8,128)S(1)} all-to-all(f32[16,56,128]{2,1,0:T(8,128)S(1)} %attach.1), channel_id=1, replica_groups=mesh['xl'=2,'z4'=2,'z2'=2,'z1'=2,'c'=2,'xh'=2,'y4'=2,'y2'=2,'y1'=2] {'xl..., dimensions={0} | all-to-all | bytes 917504 | tf_op jit(solution)/shard_map/all_to_all | solution.py:337
  120.3 6.1 %all-gather.2 = f32[32,56,128]{2,1,0:T(8,128)S(1)} all-gather(f32[16,56,128]{2,1,0:T(8,128)S(1)} %all_to_all.28), channel_id=4, replica_groups=mesh['xl'=2,'z4'=2,'z2'=2,'z1'=2,'c'=2,'xh'=2,'y4'=2,'y2'=2,'y1'=2] {'c'}, dimensions={0}, use_global_device_ids=true | all-gather | bytes 1376256 | tf_op jit(solution)/shard_map/all_gather | solution.py:341
  126.4 2.2 %finish.1 = f32[3,1,2304]{2,1,0:T(1,128)} custom-call(f32[1792,128]{1,0:T(8,128)S(1)} %bitcast.9), custom_call_target="tpu_custom_call" | custom-call | tf_op jit(solution)/shard_map/finish/pallas_call | solution.py:327
  (3 shorter events, 0.1 us)
Async XLA Ops:
  0.0 0.7 copy-start.5
  25.4 9.2 %copy-start.6 = (bf16[2,48,128]{2,1,0:T(8,128)(2,1)S(1)}, bf16[2,48,128]{2,1,0:T(8,128)(2,1)}, u32[]{:S(2)}) copy-start(bf16[2,48,128]{2,1,0:T(8,128)(2,1)} %constant.7.clone.low_ref) | copy-start | bytes 73732
  25.4 9.2 %copy-start.7 = (bf16[2,48,128]{2,1,0:T(8,128)(2,1)S(1)}, bf16[2,48,128]{2,1,0:T(8,128)(2,1)}, u32[]{:S(2)}) copy-start(bf16[2,48,128]{2,1,0:T(8,128)(2,1)} %constant.6.clone.high_ref) | copy-start | bytes 73732
  25.4 29.4 %all-to-all-start.1 = ((f32[16,112,128]{2,1,0:T(8,128)}), f32[16,112,128]{2,1,0:T(8,128)S(1)}, u32[]{:S(2)}, u32[]{:S(2)}) async-start(f32[16,112,128]{2,1,0:T(8,128)} %join.1), calls=%async_computation.1 | async-start | bytes 1835008 | tf_op jit(solution)/shard_map/all_to_all | solution.py:337
  35.0 1.0 copy-start
  35.9 1.0 copy-start.2
  54.8 8.3 %copy-start.1 = (bf16[2,2,256,512]{3,2,1,0:T(8,128)(2,1)S(1)}, bf16[2,2,256,512]{3,2,1,0:T(8,128)(2,1)}, u32[]{:S(2)}) copy-start(bf16[2,2,256,512]{3,2,1,0:T(8,128)(2,1)} %copy-done) | copy-start | bytes 3145732
  54.8 8.3 %copy-start.3 = (bf16[2,2,256,512]{3,2,1,0:T(8,128)(2,1)S(1)}, bf16[2,2,256,512]{3,2,1,0:T(8,128)(2,1)}, u32[]{:S(2)}) copy-start(bf16[2,2,256,512]{3,2,1,0:T(8,128)(2,1)} %copy-done.2) | copy-start | bytes 3145732
  54.8 8.3 %copy-start.4 = (bf16[4,48,144]{2,1,0:T(8,128)(2,1)S(1)}, bf16[4,48,144]{2,1,0:T(8,128)(2,1)}, u32[]{:S(2)}) copy-start(bf16[4,48,144]{2,1,0:T(8,128)(2,1)} %constant.8.clone.left_ref) | copy-start | bytes 165892

commit v8 on v6

--- a/solution.py
+++ b/solution.py
@@ -112,8 +112,15 @@
     )(last_high, last_low)
 
 
+HALF = 6 * NG
+
+
+def folded(x):
+    return x[:HALF] + x[HALF:]
+
+
 def exchange_kernel(
-    own_ref, pair_ref, left_ref, wide_high, wide_low, coulomb, out_ref, rho_h, rho_l, za, zb, sol_h, sol_l
+    own_ref, pair_ref, left_ref, wide_high, wide_low, coulomb, out_ref, rho, za, zb, solved
 ):
     def column(ref, first, c, step=ROWS):
         return jnp.concatenate(
@@ -131,14 +138,14 @@
         rows, cols = place(c)
         for d in range(2):
             high, low = split(own * partner(d, c))
-            rho_h[d, rows, cols] = high
-            rho_l[d, rows, cols] = low
+            rho[d, rows, cols] = high
+            rho[d, slice(HALF + rows.start, HALF + rows.stop), cols] = low
     for w in range(2):
         window = slice(128 * w, 128 * w + 256)
         out = None
         for d in range(2):
-            high, low = rho_h[d, :, window], rho_l[d, :, window]
-            term = dot(high, wide_high[w, d]) + dot(low, wide_high[w, d]) + dot(high, wide_low[w, d])
+            both = dot(rho[d, :, window], wide_high[w, d])
+            term = folded(both) + dot(rho[d, :HALF, window], wide_low[w, d])
             out = term if out is None else out + term
         for c in range(6):
             for i in range(4):
@@ -165,13 +172,12 @@
         for e in range(2):
             c, w, i = (y + e) // 8, ((y + e) % 8) // 4, (y + e) % 4
             high, low = split(both[:, 128 * e : 128 * e + 128])
-            sol_h[w, 48 * c : 48 * c + 48, 128 * i : 128 * i + 128] = high
-            sol_l[w, 48 * c : 48 * c + 48, 128 * i : 128 * i + 128] = low
+            solved[w, 48 * c : 48 * c + 48, 128 * i : 128 * i + 128] = high
+            solved[w, HALF + 48 * c : HALF + 48 * c + 48, 128 * i : 128 * i + 128] = low
     thirds = []
     for d in range(2):
         a, b = [
-            dot_t(sol_h[w], wide_high[w, d]) + dot_t(sol_l[w], wide_high[w, d]) + dot_t(sol_h[w], wide_low[w, d])
-            for w in range(2)
+            folded(dot_t(solved[w], wide_high[w, d])) + dot_t(solved[w, :HALF], wide_low[w, d]) for w in range(2)
         ]
         thirds.append((a[:, :128], a[:, 128:] + b[:, :128], b[:, 128:]))
     for c in range(COLS):
@@ -186,11 +192,11 @@
 
 def partial_exchange(own, pair, made):
     big = pltpu.VMEM((NG * PITCH, 128), f32)
-    rho, solved = pltpu.VMEM((2, 288, 384), bf16), pltpu.VMEM((2, 288, 512), bf16)
+    rho, solved = pltpu.VMEM((2, 2 * HALF, 384), bf16), pltpu.VMEM((2, 2 * HALF, 512), bf16)
     return pl.pallas_call(
         exchange_kernel,
         out_shape=jax.ShapeDtypeStruct((SLABS * ROWS, 128), f32),
-        scratch_shapes=[rho, rho, big, big, solved, solved],
+        scratch_shapes=[rho, big, big, solved],
         name="exchange",
         compiler_params=LARGE,
     )(own, pair, jnp.asarray(LEFTS), *made)
@@ -263,7 +269,7 @@
     return pl.pallas_call(attach_kernel, out_shape=copies, name="attach", compiler_params=SMALL)(field, parts)
 
 
-BLOCK = 4
+BLOCK = 8
 
 
 def place_of(band):
@@ -326,11 +332,11 @@
     tile, copies = prepare(jnp.transpose(orbitals, (1, 0, 2)))
     made = tables(jnp.asarray(LAST_HIGH), jnp.asarray(LAST_LOW))
     chips = exchange_tiles(copies, PAIR)
-    whole = exchange_tiles(join(tile, chips), GRID)
+    whole, others = lax.optimization_barrier((exchange_tiles(join(tile, chips), GRID), both_cores(chips)))
     pair = both_cores(whole[:, ROWS:])
     partial = partial_exchange(whole.reshape(SLABS * 2 * ROWS, 128), pair, made)
     shares = exchange_tiles(partial.reshape(SLABS, ROWS, 128), GRID)
-    field, lines = column_part(shares, both_cores(chips))
+    field, lines = column_part(shares, others)
     parts = exchange_tiles(lines, GRID)
     fields = both_cores(exchange_tiles(attach(field, parts), PAIR))
     return jnp.transpose(finish(fields), (1, 0, 2))

time: 127 us -> 126 us (level)
  blocking collectives: 72.6 us -> 93.4 us
  waiting for transfers between devices: 28.8 us -> 12.4 us
  starting transfers between devices: 13.9 us -> 9.22 us
    all_to_all x3 -> x4, blocking collectives: 55.5 us -> 73.6 us  [exchange_tiles(): return lax.all_to_all(tiles, axis, 0, 0, tiled=True)]
    all_to_all x2 -> x1, waiting for transfers between devices: 28.8 us -> 12.4 us  [exchange_tiles(): return lax.all_to_all(tiles, axis, 0, 0, tiled=True)]
    all_to_all x2 -> x1, starting transfers between devices: 13.9 us -> 9.22 us  [exchange_tiles(): return lax.all_to_all(tiles, axis, 0, 0, tiled=True)]
    all_gather x3, blocking collectives: 17.1 us -> 19.8 us  [both_cores(): return lax.all_gather(chips, CORE, axis=0, tiled=False).reshape(-1, 128)]
  transfers between devices with their start and end apart: 2 -> 1, of which waited for: 2 -> 1; matrix products, arithmetic and copies ran while one was open for 0% -> 0% of each run, Pallas kernels for 0% -> 0%
where the time goes in v8:
time: 126 us; the launch traced here: 125 us
  blocking collectives  93.4 us (74%)
  waiting for transfers between devices  12.4 us (10%)
  starting transfers between devices  9.22 us (7%)
  Pallas kernels  7.17 us (6%)
  local copies, waits for them, and re-layouts  2.76 us (2%)
    all_to_all x4, blocking collectives, exchange_tiles(): return lax.all_to_all(tiles, axis, 0, 0, tiled=True)  73.6 us
    all_gather x3, blocking collectives, both_cores(): return lax.all_gather(chips, CORE, axis=0, tiled=False).reshape(-1, 128)  19.8 us
    all_to_all x1, waiting for transfers between devices, exchange_tiles(): return lax.all_to_all(tiles, axis, 0, 0, tiled=True)  12.4 us
    all_to_all x1, starting transfers between devices, exchange_tiles(): return lax.all_to_all(tiles, axis, 0, 0, tiled=True)  9.22 us
    pallas_call x1, Pallas kernels, partial_exchange(): pl.pallas_call(exchange_kernel, out_shape=jax.ShapeDtypeStruct((SLABS * R...  3.82 us
    unnamed x16, local copies, waits for them, and re-layouts  2.73 us
  transfers between devices with their start and end apart: 1, of which 1 were waited for; matrix products, arithmetic and copies ran while one was open for 0% of the time, Pallas kernels for 0%

profile of v8, /device:TPU:1, one launch (start us, length us, event | category | flops | bytes accessed | tf_op | source)
XLA Modules:
  0.0 125.1 jit_solution(1781028692593075227)
XLA Ops:
  0.0 0.0 copy-start.5
  0.0 0.7 copy-done.5
  0.8 23.6 %all_to_all.25.chips_ref = f32[16,56,128]{2,1,0:T(8,128)S(1)} all-to-all(f32[16,56,128]{2,1,0:T(8,128)S(1)} %get-tuple-element.15), channel_id=1, replica_groups=mesh['xl'=2,'z4'=2,'z2'=2,'z1'=2,'c'=2,'xh'=2,'y4'=2,'y2'=2,'y1'=2] {'xl..., dimensions={0} | all-to-all | bytes 917504 | tf_op jit(solution)/shard_map/all_to_all | solution.py:324
  24.4 1.0 join.1
  25.4 0.0 copy-start.6
  25.4 0.0 copy-start.7
  25.4 9.2 %all-to-all-start.1 = ((f32[16,112,128]{2,1,0:T(8,128)}), f32[16,112,128]{2,1,0:T(8,128)S(1)}, u32[]{:S(2)}, u32[]{:S(2)}) async-start(f32[16,112,128]{2,1,0:T(8,128)} %join.1), calls=%async_computation.1 | async-start | bytes 1835008 | tf_op jit(solution)/shard_map/all_to_all | solution.py:324
  34.6 0.0 copy-done.6
  34.6 0.0 copy-done.7
  34.7 0.3 tables.1
  35.0 0.0 copy-start
  35.0 1.0 copy-done
  35.9 0.0 copy-start.2
  35.9 1.0 copy-done.2
  36.9 5.4 %all-gather = f32[32,56,128]{2,1,0:T(8,128)S(1)} all-gather(f32[16,56,128]{2,1,0:T(8,128)S(1)} %all_to_all.25.chips_ref), channel_id=2, replica_groups=mesh['xl'=2,'z4'=2,'z2'=2,'z1'=2,'c'=2,'xh'=2,'y4'=2,'y2'=2,'y1'=2] {'c'}, dimensions={0}, use_global_device_ids=true | all-gather | bytes 1376256 | tf_op jit(solution)/shard_map/all_gather | solution.py:328
  42.3 12.4 %all-to-all-done.1 = f32[16,112,128]{2,1,0:T(8,128)S(1)} async-done(((f32[16,112,128]{2,1,0:T(8,128)}), f32[16,112,128]{2,1,0:T(8,128)S(1)}, u32[]{:S(2)}, u32[]{:S(2)}) %all-to-all-start.1) | async-done | bytes 917536 | tf_op jit(solution)/shard_map/all_to_all | solution.py:324
  54.8 0.0 copy-start.1
  54.8 0.0 copy-start.3
  54.8 0.0 copy-start.4
  54.8 8.3 %all-gather.1 = f32[32,56,128]{2,1,0:T(8,128)S(1)} all-gather(f32[16,56,128]{2,1,0:T(8,128)S(1)} %slice.3), channel_id=3, replica_groups=mesh['xl'=2,'z4'=2,'z2'=2,'z1'=2,'c'=2,'xh'=2,'y4'=2,'y2'=2,'y1'=2] {'c'}, dimensions={0}, use_global_device_ids=true | all-gather | bytes 1376256 | tf_op jit(solution)/shard_map/all_gather | solution.py:328
  63.1 0.0 copy-done.1
  63.1 0.0 copy-done.3
  63.1 0.0 copy-done.4
  63.1 3.8 %exchange.1 = f32[896,128]{1,0:T(8,128)S(1)} custom-call(f32[1792,128]{1,0:T(8,128)S(1)} %bitcast.7, f32[1792,128]{1,0:T(8,128)S(1)} %bitcast.10, bf16[4,48,144]{2,1,0:T(8,128)(2,1)S(1)} %copy-done.4, bf16[2,2,256,512]{3,2,1,0:T(8,128)(2,1)S(1)} %copy-done.1, bf16[2,2,256,512]{3,2,1,0:T(8,128)(2,1)S(1)} %copy-done.3, ...), custom_call_target="tpu_custom_call" | custom-call | tf_op jit(solution)/shard_map/exchange/pallas_call | solution.py:196
  66.9 18.1 %all_to_all.26.share_ref = f32[16,56,128]{2,1,0:T(8,128)S(1)} all-to-all(f32[16,56,128]{2,1,0:T(8,128)S(1)} %bitcast.11), channel_id=1, replica_groups=mesh['xl'=2,'z4'=2,'z2'=2,'z1'=2,'c'=2,'xh'=2,'y4'=2,'y2'=2,'y1'=2] {'xh..., dimensions={0} | all-to-all | bytes 917504 | tf_op jit(solution)/shard_map/all_to_all | solution.py:324
  85.1 0.2 column.1
  85.3 15.2 %all_to_all.27.parts_ref = f32[16,8,128]{2,1,0:T(8,128)S(1)} all-to-all(f32[16,8,128]{2,1,0:T(8,128)S(1)} %get-tuple-element.22), channel_id=1, replica_groups=mesh['xl'=2,'z4'=2,'z2'=2,'z1'=2,'c'=2,'xh'=2,'y4'=2,'y2'=2,'y1'=2] {'xh..., dimensions={0} | all-to-all | bytes 131072 | tf_op jit(solution)/shard_map/all_to_all | solution.py:324
  100.5 16.6 %all_to_all.28 = f32[16,56,128]{2,1,0:T(8,128)S(1)} all-to-all(f32[16,56,128]{2,1,0:T(8,128)S(1)} %attach.1), channel_id=1, replica_groups=mesh['xl'=2,'z4'=2,'z2'=2,'z1'=2,'c'=2,'xh'=2,'y4'=2,'y2'=2,'y1'=2] {'xl..., dimensions={0} | all-to-all | bytes 917504 | tf_op jit(solution)/shard_map/all_to_all | solution.py:324
  117.2 6.1 %all-gather.2 = f32[32,56,128]{2,1,0:T(8,128)S(1)} all-gather(f32[16,56,128]{2,1,0:T(8,128)S(1)} %all_to_all.28), channel_id=4, replica_groups=mesh['xl'=2,'z4'=2,'z2'=2,'z1'=2,'c'=2,'xh'=2,'y4'=2,'y2'=2,'y1'=2] {'c'}, dimensions={0}, use_global_device_ids=true | all-gather | bytes 1376256 | tf_op jit(solution)/shard_map/all_gather | solution.py:328
  123.3 1.8 %finish.1 = f32[3,1,2304]{2,1,0:T(1,128)} custom-call(f32[1792,128]{1,0:T(8,128)S(1)} %bitcast.9), custom_call_target="tpu_custom_call" | custom-call | tf_op jit(solution)/shard_map/finish/pallas_call | solution.py:314
  (3 shorter events, 0.1 us)
Async XLA Ops:
  0.0 0.7 copy-start.5
  25.4 9.2 %copy-start.6 = (bf16[2,48,128]{2,1,0:T(8,128)(2,1)S(1)}, bf16[2,48,128]{2,1,0:T(8,128)(2,1)}, u32[]{:S(2)}) copy-start(bf16[2,48,128]{2,1,0:T(8,128)(2,1)} %constant.7.clone.low_ref) | copy-start | bytes 73732
  25.4 9.2 %copy-start.7 = (bf16[2,48,128]{2,1,0:T(8,128)(2,1)S(1)}, bf16[2,48,128]{2,1,0:T(8,128)(2,1)}, u32[]{:S(2)}) copy-start(bf16[2,48,128]{2,1,0:T(8,128)(2,1)} %constant.6.clone.high_ref) | copy-start | bytes 73732
  25.4 29.4 %all-to-all-start.1 = ((f32[16,112,128]{2,1,0:T(8,128)}), f32[16,112,128]{2,1,0:T(8,128)S(1)}, u32[]{:S(2)}, u32[]{:S(2)}) async-start(f32[16,112,128]{2,1,0:T(8,128)} %join.1), calls=%async_computation.1 | async-start | bytes 1835008 | tf_op jit(solution)/shard_map/all_to_all | solution.py:324
  35.0 1.0 copy-start
  35.9 1.0 copy-start.2
  54.8 8.3 %copy-start.1 = (bf16[2,2,256,512]{3,2,1,0:T(8,128)(2,1)S(1)}, bf16[2,2,256,512]{3,2,1,0:T(8,128)(2,1)}, u32[]{:S(2)}) copy-start(bf16[2,2,256,512]{3,2,1,0:T(8,128)(2,1)} %copy-done) | copy-start | bytes 3145732
  54.8 8.3 %copy-start.3 = (bf16[2,2,256,512]{3,2,1,0:T(8,128)(2,1)S(1)}, bf16[2,2,256,512]{3,2,1,0:T(8,128)(2,1)}, u32[]{:S(2)}) copy-start(bf16[2,2,256,512]{3,2,1,0:T(8,128)(2,1)} %copy-done.2) | copy-start | bytes 3145732
  54.8 8.3 %copy-start.4 = (bf16[4,48,144]{2,1,0:T(8,128)(2,1)S(1)}, bf16[4,48,144]{2,1,0:T(8,128)(2,1)}, u32[]{:S(2)}) copy-start(bf16[4,48,144]{2,1,0:T(8,128)(2,1)} %constant.8.clone.left_ref) | copy-start | bytes 165892

commit v9 on v8

--- a/solution.py
+++ b/solution.py
@@ -19,6 +19,8 @@
 CHIPS = BANDS // 2
 PAIR, CORE, GRID = ("xl", "z4", "z2", "z1"), ("c",), ("xh", "y4", "y2", "y1")
 BAND = PAIR + CORE
+CROSS = ("xl",) + GRID
+ROLES = [[(q ^ h) * 16 + h * 8 + y for h in range(2) for y in range(8)] for q in range(2)]
 PITCH = 56
 f32, bf16 = jnp.float32, jnp.bfloat16
 SMALL = pltpu.CompilerParams(vmem_limit_bytes=12 << 20)
@@ -202,7 +204,7 @@
     )(own, pair, jnp.asarray(LEFTS), *made)
 
 
-def prepare_kernel(slab_ref, tile_ref, copies_ref):
+def prepare_kernel(slab_ref, copies_ref, tile_ref):
     tile_ref[USED:ROWS, :] = jnp.zeros((ROWS - USED, 128), f32)
     for p in range(PLANES):
         for c in range(COLS):
@@ -214,25 +216,34 @@
 
 
 def prepare(slab):
-    tile = jax.ShapeDtypeStruct((ROWS, 128), f32)
-    copies = jax.ShapeDtypeStruct((CHIPS, ROWS, 128), f32)
-    return pl.pallas_call(prepare_kernel, out_shape=(tile, copies), name="prepare", compiler_params=SMALL)(slab)
-
-
-def join_kernel(tile_ref, chips_ref, out_ref):
-    tile = tile_ref[...]
+    return pl.pallas_call(
+        prepare_kernel,
+        out_shape=jax.ShapeDtypeStruct((CHIPS, ROWS, 128), f32),
+        scratch_shapes=[pltpu.VMEM((ROWS, 128), f32)],
+        name="prepare",
+        compiler_params=SMALL,
+    )(slab)
+
+
+def role_of(xl):
+    xh = lax.axis_index("xh")
+    return xl + xh - 2 * xl * xh
+
+
+def join_kernel(chips_ref, out_ref):
+    tile = chips_ref[role_of(lax.axis_index("xl")) * 8 + lax.axis_index(("z4", "z2", "z1"))]
     for k in range(SLABS):
         out_ref[k, :ROWS, :] = tile
         out_ref[k, ROWS:, :] = chips_ref[k]
 
 
-def join(tile, chips):
+def join(chips):
     return pl.pallas_call(
         join_kernel,
         out_shape=jax.ShapeDtypeStruct((SLABS, 2 * ROWS, 128), f32),
         name="join",
         compiler_params=SMALL,
-    )(tile, chips)
+    )(chips)
 
 
 def column_kernel(share_ref, orbital_ref, field_ref, copies_ref):
@@ -278,7 +289,9 @@
 
 def finish_kernel(field_ref, out_ref, flat):
     mine = lax.axis_index(CORE + PAIR)
-    matrix = field_ref[pl.ds(USED, BANDS, stride=ROWS), :][:, :BANDS]
+    starts = [ROWS * (CHIPS * core + 8 * role_of(xl)) for core in range(2) for xl in range(2)]
+    matrix = jnp.concatenate([field_ref[pl.ds(start + USED, 8, stride=ROWS), :] for start in starts], 0)
+    matrix = matrix[:, :BANDS]
     definite = (matrix + matrix.T) * (-0.5 / float(NG**3))
     row = lax.broadcasted_iota(jnp.int32, (BANDS, 2 * BANDS), 0)
     lane = lax.broadcasted_iota(jnp.int32, (BANDS, 2 * BANDS), 1)
@@ -301,7 +314,8 @@
     total = None
     for k in range(BANDS):
         weight = weights[:, BANDS + k : BANDS + k + 1]
-        term = weight * field_ref[ROWS * k : ROWS * k + ROWS, :]
+        start = pl.multiple_of(starts[k // 8] + ROWS * (k % 8), 8)
+        term = weight * field_ref[pl.ds(start, ROWS), :]
         total = term if total is None else total + term
     flat[...] = total
     for p in range(PLANES):
@@ -324,20 +338,24 @@
     return lax.all_to_all(tiles, axis, 0, 0, tiled=True)
 
 
+def exchange_roles(tiles):
+    return lax.all_to_all(tiles, CROSS, 0, 0, axis_index_groups=ROLES, tiled=True)
+
+
 def both_cores(chips):
     return lax.all_gather(chips, CORE, axis=0, tiled=False).reshape(-1, 128)
 
 
 def per_device(orbitals):
-    tile, copies = prepare(jnp.transpose(orbitals, (1, 0, 2)))
+    copies = prepare(jnp.transpose(orbitals, (1, 0, 2)))
     made = tables(jnp.asarray(LAST_HIGH), jnp.asarray(LAST_LOW))
     chips = exchange_tiles(copies, PAIR)
-    whole, others = lax.optimization_barrier((exchange_tiles(join(tile, chips), GRID), both_cores(chips)))
+    whole, others = lax.optimization_barrier((exchange_roles(join(chips)), both_cores(chips)))
     pair = both_cores(whole[:, ROWS:])
     partial = partial_exchange(whole.reshape(SLABS * 2 * ROWS, 128), pair, made)
-    shares = exchange_tiles(partial.reshape(SLABS, ROWS, 128), GRID)
+    shares = exchange_roles(partial.reshape(SLABS, ROWS, 128))
     field, lines = column_part(shares, others)
-    parts = exchange_tiles(lines, GRID)
+    parts = exchange_roles(lines)
     fields = both_cores(exchange_tiles(attach(field, parts), PAIR))
     return jnp.transpose(finish(fields), (1, 0, 2))
 

time: 126 us -> 124 us (0.984)
    all_to_all x4 -> x2, blocking collectives: 73.6 us -> 40.3 us  [exchange_tiles(): return lax.all_to_all(tiles, axis, 0, 0, tiled=True)]
    all_to_all x0 -> x2, blocking collectives: none -> 32.8 us  [exchange_roles(): lax.all_to_all(tiles, CROSS, 0, 0, axis_index_groups=ROLES, tiled=True)]
where the time goes in v9:
time: 124 us
  blocking collectives  92.7 us (75%)
  waiting for transfers between devices  12.3 us (10%)
  starting transfers between devices  8.85 us (7%)
  Pallas kernels  7.19 us (6%)
  local copies, waits for them, and re-layouts  2.76 us (2%)
    all_to_all x2, blocking collectives, exchange_tiles(): return lax.all_to_all(tiles, axis, 0, 0, tiled=True)  40.3 us
    all_to_all x2, blocking collectives, exchange_roles(): lax.all_to_all(tiles, CROSS, 0, 0, axis_index_groups=ROLES, tiled=True)  32.8 us
    all_gather x3, blocking collectives, both_cores(): return lax.all_gather(chips, CORE, axis=0, tiled=False).reshape(-1, 128)  19.6 us
    all_to_all x1, waiting for transfers between devices, exchange_roles(): lax.all_to_all(tiles, CROSS, 0, 0, axis_index_groups=ROLES, tiled=True)  12.3 us
    all_to_all x1, starting transfers between devices, exchange_roles(): lax.all_to_all(tiles, CROSS, 0, 0, axis_index_groups=ROLES, tiled=True)  8.85 us
    pallas_call x1, Pallas kernels, partial_exchange(): pl.pallas_call(exchange_kernel, out_shape=jax.ShapeDtypeStruct((SLABS * R...  3.82 us
    unnamed x16, local copies, waits for them, and re-layouts  2.73 us
  transfers between devices with their start and end apart: 1, of which 1 were waited for; matrix products, arithmetic and copies ran while one was open for 0% of the time, Pallas kernels for 0%

profile of v9, /device:TPU:1, one launch (start us, length us, event | category | flops | bytes accessed | tf_op | source)
XLA Modules:
  0.0 123.9 jit_solution(10878167759025340817)
XLA Ops:
  0.0 0.0 copy-start.5
  0.0 0.7 copy-done.5
  0.8 23.6 %all_to_all.25.chips_ref = f32[16,56,128]{2,1,0:T(8,128)S(1)} all-to-all(f32[16,56,128]{2,1,0:T(8,128)S(1)} %prepare.1), channel_id=1, replica_groups=mesh['xl'=2,'z4'=2,'z2'=2,'z1'=2,'c'=2,'xh'=2,'y4'=2,'y2'=2,'y1'=2] {'xl..., dimensions={0} | all-to-all | bytes 917504 | tf_op jit(solution)/shard_map/all_to_all | solution.py:338
  24.4 1.0 join.1
  25.4 0.0 copy-start.6
  25.4 0.0 copy-start.7
  25.4 8.9 %all-to-all-start.1 = ((f32[16,112,128]{2,1,0:T(8,128)}), f32[16,112,128]{2,1,0:T(8,128)S(1)}, u32[]{:S(2)}, u32[]{:S(2)}) async-start(f32[16,112,128]{2,1,0:T(8,128)} %join.1), calls=%async_computation.1 | async-start | bytes 1835008 | tf_op jit(solution)/shard_map/all_to_all | solution.py:342
  34.3 0.0 copy-done.6
  34.3 0.0 copy-done.7
  34.3 0.3 tables.1
  34.6 0.0 copy-start
  34.6 1.0 copy-done
  35.6 0.0 copy-start.2
  35.6 1.0 copy-done.2
  36.6 5.3 %all-gather = f32[32,56,128]{2,1,0:T(8,128)S(1)} all-gather(f32[16,56,128]{2,1,0:T(8,128)S(1)} %all_to_all.25.chips_ref), channel_id=2, replica_groups=mesh['xl'=2,'z4'=2,'z2'=2,'z1'=2,'c'=2,'xh'=2,'y4'=2,'y2'=2,'y1'=2] {'c'}, dimensions={0}, use_global_device_ids=true | all-gather | bytes 1376256 | tf_op jit(solution)/shard_map/all_gather | solution.py:346
  41.9 12.3 %all-to-all-done.1 = f32[16,112,128]{2,1,0:T(8,128)S(1)} async-done(((f32[16,112,128]{2,1,0:T(8,128)}), f32[16,112,128]{2,1,0:T(8,128)S(1)}, u32[]{:S(2)}, u32[]{:S(2)}) %all-to-all-start.1) | async-done | bytes 917536 | tf_op jit(solution)/shard_map/all_to_all | solution.py:342
  54.2 0.0 copy-start.1
  54.2 0.0 copy-start.3
  54.2 0.0 copy-start.4
  54.3 8.1 %all-gather.1 = f32[32,56,128]{2,1,0:T(8,128)S(1)} all-gather(f32[16,56,128]{2,1,0:T(8,128)S(1)} %slice.3), channel_id=3, replica_groups=mesh['xl'=2,'z4'=2,'z2'=2,'z1'=2,'c'=2,'xh'=2,'y4'=2,'y2'=2,'y1'=2] {'c'}, dimensions={0}, use_global_device_ids=true | all-gather | bytes 1376256 | tf_op jit(solution)/shard_map/all_gather | solution.py:346
  62.4 0.0 copy-done.1
  62.4 0.0 copy-done.3
  62.4 0.0 copy-done.4
  62.4 3.8 %exchange.1 = f32[896,128]{1,0:T(8,128)S(1)} custom-call(f32[1792,128]{1,0:T(8,128)S(1)} %bitcast.7, f32[1792,128]{1,0:T(8,128)S(1)} %bitcast.10, bf16[4,48,144]{2,1,0:T(8,128)(2,1)S(1)} %copy-done.4, bf16[2,2,256,512]{3,2,1,0:T(8,128)(2,1)S(1)} %copy-done.1, bf16[2,2,256,512]{3,2,1,0:T(8,128)(2,1)S(1)} %copy-done.3, ...), custom_call_target="tpu_custom_call" | custom-call | tf_op jit(solution)/shard_map/exchange/pallas_call | solution.py:198
  66.2 17.9 %all_to_all.26.share_ref = f32[16,56,128]{2,1,0:T(8,128)S(1)} all-to-all(f32[16,56,128]{2,1,0:T(8,128)S(1)} %bitcast.11), channel_id=1, replica_groups={{0,1,2,3,4,5,6,7,264,265,266,267,268,269,270,271},{256,257,258,259,260,..., dimensions={0} | all-to-all | bytes 917504 | tf_op jit(solution)/shard_map/all_to_all | solution.py:342
  84.1 0.2 column.1
  84.3 14.9 %all_to_all.27.parts_ref = f32[16,8,128]{2,1,0:T(8,128)S(1)} all-to-all(f32[16,8,128]{2,1,0:T(8,128)S(1)} %get-tuple-element.18), channel_id=1, replica_groups={{0,1,2,3,4,5,6,7,264,265,266,267,268,269,270,271},{256,257,258,259,260,..., dimensions={0} | all-to-all | bytes 131072 | tf_op jit(solution)/shard_map/all_to_all | solution.py:342
  99.3 16.7 %all_to_all.28 = f32[16,56,128]{2,1,0:T(8,128)S(1)} all-to-all(f32[16,56,128]{2,1,0:T(8,128)S(1)} %attach.1), channel_id=1, replica_groups=mesh['xl'=2,'z4'=2,'z2'=2,'z1'=2,'c'=2,'xh'=2,'y4'=2,'y2'=2,'y1'=2] {'xl..., dimensions={0} | all-to-all | bytes 917504 | tf_op jit(solution)/shard_map/all_to_all | solution.py:338
  116.0 6.1 %all-gather.2 = f32[32,56,128]{2,1,0:T(8,128)S(1)} all-gather(f32[16,56,128]{2,1,0:T(8,128)S(1)} %all_to_all.28), channel_id=4, replica_groups=mesh['xl'=2,'z4'=2,'z2'=2,'z1'=2,'c'=2,'xh'=2,'y4'=2,'y2'=2,'y1'=2] {'c'}, dimensions={0}, use_global_device_ids=true | all-gather | bytes 1376256 | tf_op jit(solution)/shard_map/all_gather | solution.py:346
  122.1 1.8 %finish.1 = f32[3,1,2304]{2,1,0:T(1,128)} custom-call(f32[1792,128]{1,0:T(8,128)S(1)} %bitcast.9), custom_call_target="tpu_custom_call" | custom-call | tf_op jit(solution)/shard_map/finish/pallas_call | solution.py:328
  (3 shorter events, 0.1 us)
Async XLA Ops:
  0.0 0.7 copy-start.5
  25.4 8.9 %copy-start.6 = (bf16[2,48,128]{2,1,0:T(8,128)(2,1)S(1)}, bf16[2,48,128]{2,1,0:T(8,128)(2,1)}, u32[]{:S(2)}) copy-start(bf16[2,48,128]{2,1,0:T(8,128)(2,1)} %constant.7.clone.low_ref) | copy-start | bytes 73732
  25.4 8.9 %copy-start.7 = (bf16[2,48,128]{2,1,0:T(8,128)(2,1)S(1)}, bf16[2,48,128]{2,1,0:T(8,128)(2,1)}, u32[]{:S(2)}) copy-start(bf16[2,48,128]{2,1,0:T(8,128)(2,1)} %constant.6.clone.high_ref) | copy-start | bytes 73732
  25.4 28.8 %all-to-all-start.1 = ((f32[16,112,128]{2,1,0:T(8,128)}), f32[16,112,128]{2,1,0:T(8,128)S(1)}, u32[]{:S(2)}, u32[]{:S(2)}) async-start(f32[16,112,128]{2,1,0:T(8,128)} %join.1), calls=%async_computation.1 | async-start | bytes 1835008 | tf_op jit(solution)/shard_map/all_to_all | solution.py:342
  34.6 1.0 copy-start
  35.6 1.0 copy-start.2
  54.2 8.2 %copy-start.1 = (bf16[2,2,256,512]{3,2,1,0:T(8,128)(2,1)S(1)}, bf16[2,2,256,512]{3,2,1,0:T(8,128)(2,1)}, u32[]{:S(2)}) copy-start(bf16[2,2,256,512]{3,2,1,0:T(8,128)(2,1)} %copy-done) | copy-start | bytes 3145732
  54.2 8.2 %copy-start.3 = (bf16[2,2,256,512]{3,2,1,0:T(8,128)(2,1)S(1)}, bf16[2,2,256,512]{3,2,1,0:T(8,128)(2,1)}, u32[]{:S(2)}) copy-start(bf16[2,2,256,512]{3,2,1,0:T(8,128)(2,1)} %copy-done.2) | copy-start | bytes 3145732
  54.2 8.2 %copy-start.4 = (bf16[4,48,144]{2,1,0:T(8,128)(2,1)S(1)}, bf16[4,48,144]{2,1,0:T(8,128)(2,1)}, u32[]{:S(2)}) copy-start(bf16[4,48,144]{2,1,0:T(8,128)(2,1)} %constant.8.clone.left_ref) | copy-start | bytes 165892

commit v10 on v9

--- a/solution.py
+++ b/solution.py
@@ -280,7 +280,7 @@
     return pl.pallas_call(attach_kernel, out_shape=copies, name="attach", compiler_params=SMALL)(field, parts)
 
 
-BLOCK = 8
+BLOCK = 16
 
 
 def place_of(band):
@@ -303,7 +303,8 @@
         columns = [jnp.broadcast_to(state[:, a : a + 1], (BANDS, 2 * BANDS)) for a in at]
         pivots = [state[a : a + 1, :] for a in at]
         for i in range(BLOCK):
-            factor = jnp.where(order > first + i, columns[i] / columns[i][at[i] : at[i] + 1, :], 0.0)
+            inverse = 1.0 / columns[i][at[i] : at[i] + 1, :]
+            factor = jnp.where(order > first + i, columns[i] * inverse, 0.0)
             for j in range(i + 1, BLOCK):
                 columns[j] = columns[j] - factor * columns[j][at[i] : at[i] + 1, :]
                 pivots[j] = pivots[j] - factor[at[j] : at[j] + 1, :] * pivots[i]

time: 124 us -> 124 us (level)
  no operation moved by 1% of the time
where the time goes in v10:
time: 124 us
  blocking collectives  92.7 us (75%)
  waiting for transfers between devices  12.3 us (10%)
  starting transfers between devices  8.85 us (7%)
  Pallas kernels  7.1 us (6%)
  local copies, waits for them, and re-layouts  2.76 us (2%)
    all_to_all x2, blocking collectives, exchange_tiles(): return lax.all_to_all(tiles, axis, 0, 0, tiled=True)  40.3 us
    all_to_all x2, blocking collectives, exchange_roles(): lax.all_to_all(tiles, CROSS, 0, 0, axis_index_groups=ROLES, tiled=True)  32.8 us
    all_gather x3, blocking collectives, both_cores(): return lax.all_gather(chips, CORE, axis=0, tiled=False).reshape(-1, 128)  19.6 us
    all_to_all x1, waiting for transfers between devices, exchange_roles(): lax.all_to_all(tiles, CROSS, 0, 0, axis_index_groups=ROLES, tiled=True)  12.3 us
    all_to_all x1, starting transfers between devices, exchange_roles(): lax.all_to_all(tiles, CROSS, 0, 0, axis_index_groups=ROLES, tiled=True)  8.85 us
    pallas_call x1, Pallas kernels, partial_exchange(): pl.pallas_call(exchange_kernel, out_shape=jax.ShapeDtypeStruct((SLABS * R...  3.82 us
    unnamed x16, local copies, waits for them, and re-layouts  2.73 us
  transfers between devices with their start and end apart: 1, of which 1 were waited for; matrix products, arithmetic and copies ran while one was open for 0% of the time, Pallas kernels for 0%

profile of v10, /device:TPU:1, one launch (start us, length us, event | category | flops | bytes accessed | tf_op | source)
XLA Modules:
  0.0 123.8 jit_solution(11694466593910539677)
XLA Ops:
  0.0 0.0 copy-start.5
  0.0 0.7 copy-done.5
  0.8 23.6 %all_to_all.25.chips_ref = f32[16,56,128]{2,1,0:T(8,128)S(1)} all-to-all(f32[16,56,128]{2,1,0:T(8,128)S(1)} %prepare.1), channel_id=1, replica_groups=mesh['xl'=2,'z4'=2,'z2'=2,'z1'=2,'c'=2,'xh'=2,'y4'=2,'y2'=2,'y1'=2] {'xl..., dimensions={0} | all-to-all | bytes 917504 | tf_op jit(solution)/shard_map/all_to_all | solution.py:339
  24.4 1.0 join.1
  25.4 0.0 copy-start.6
  25.4 0.0 copy-start.7
  25.4 8.9 %all-to-all-start.1 = ((f32[16,112,128]{2,1,0:T(8,128)}), f32[16,112,128]{2,1,0:T(8,128)S(1)}, u32[]{:S(2)}, u32[]{:S(2)}) async-start(f32[16,112,128]{2,1,0:T(8,128)} %join.1), calls=%async_computation.1 | async-start | bytes 1835008 | tf_op jit(solution)/shard_map/all_to_all | solution.py:343
  34.3 0.0 copy-done.6
  34.3 0.0 copy-done.7
  34.3 0.3 tables.1
  34.6 0.0 copy-start
  34.6 1.0 copy-done
  35.6 0.0 copy-start.2
  35.6 1.0 copy-done.2
  36.6 5.3 %all-gather = f32[32,56,128]{2,1,0:T(8,128)S(1)} all-gather(f32[16,56,128]{2,1,0:T(8,128)S(1)} %all_to_all.25.chips_ref), channel_id=2, replica_groups=mesh['xl'=2,'z4'=2,'z2'=2,'z1'=2,'c'=2,'xh'=2,'y4'=2,'y2'=2,'y1'=2] {'c'}, dimensions={0}, use_global_device_ids=true | all-gather | bytes 1376256 | tf_op jit(solution)/shard_map/all_gather | solution.py:347
  41.9 12.3 %all-to-all-done.1 = f32[16,112,128]{2,1,0:T(8,128)S(1)} async-done(((f32[16,112,128]{2,1,0:T(8,128)}), f32[16,112,128]{2,1,0:T(8,128)S(1)}, u32[]{:S(2)}, u32[]{:S(2)}) %all-to-all-start.1) | async-done | bytes 917536 | tf_op jit(solution)/shard_map/all_to_all | solution.py:343
  54.2 0.0 copy-start.1
  54.2 0.0 copy-start.3
  54.2 0.0 copy-start.4
  54.3 8.1 %all-gather.1 = f32[32,56,128]{2,1,0:T(8,128)S(1)} all-gather(f32[16,56,128]{2,1,0:T(8,128)S(1)} %slice.3), channel_id=3, replica_groups=mesh['xl'=2,'z4'=2,'z2'=2,'z1'=2,'c'=2,'xh'=2,'y4'=2,'y2'=2,'y1'=2] {'c'}, dimensions={0}, use_global_device_ids=true | all-gather | bytes 1376256 | tf_op jit(solution)/shard_map/all_gather | solution.py:347
  62.4 0.0 copy-done.1
  62.4 0.0 copy-done.3
  62.4 0.0 copy-done.4
  62.4 3.8 %exchange.1 = f32[896,128]{1,0:T(8,128)S(1)} custom-call(f32[1792,128]{1,0:T(8,128)S(1)} %bitcast.7, f32[1792,128]{1,0:T(8,128)S(1)} %bitcast.10, bf16[4,48,144]{2,1,0:T(8,128)(2,1)S(1)} %copy-done.4, bf16[2,2,256,512]{3,2,1,0:T(8,128)(2,1)S(1)} %copy-done.1, bf16[2,2,256,512]{3,2,1,0:T(8,128)(2,1)S(1)} %copy-done.3, ...), custom_call_target="tpu_custom_call" | custom-call | tf_op jit(solution)/shard_map/exchange/pallas_call | solution.py:198
  66.2 17.9 %all_to_all.26.share_ref = f32[16,56,128]{2,1,0:T(8,128)S(1)} all-to-all(f32[16,56,128]{2,1,0:T(8,128)S(1)} %bitcast.11), channel_id=1, replica_groups={{0,1,2,3,4,5,6,7,264,265,266,267,268,269,270,271},{256,257,258,259,260,..., dimensions={0} | all-to-all | bytes 917504 | tf_op jit(solution)/shard_map/all_to_all | solution.py:343
  84.1 0.2 column.1
  84.3 14.9 %all_to_all.27.parts_ref = f32[16,8,128]{2,1,0:T(8,128)S(1)} all-to-all(f32[16,8,128]{2,1,0:T(8,128)S(1)} %get-tuple-element.18), channel_id=1, replica_groups={{0,1,2,3,4,5,6,7,264,265,266,267,268,269,270,271},{256,257,258,259,260,..., dimensions={0} | all-to-all | bytes 131072 | tf_op jit(solution)/shard_map/all_to_all | solution.py:343
  99.3 16.7 %all_to_all.28 = f32[16,56,128]{2,1,0:T(8,128)S(1)} all-to-all(f32[16,56,128]{2,1,0:T(8,128)S(1)} %attach.1), channel_id=1, replica_groups=mesh['xl'=2,'z4'=2,'z2'=2,'z1'=2,'c'=2,'xh'=2,'y4'=2,'y2'=2,'y1'=2] {'xl..., dimensions={0} | all-to-all | bytes 917504 | tf_op jit(solution)/shard_map/all_to_all | solution.py:339
  116.0 6.1 %all-gather.2 = f32[32,56,128]{2,1,0:T(8,128)S(1)} all-gather(f32[16,56,128]{2,1,0:T(8,128)S(1)} %all_to_all.28), channel_id=4, replica_groups=mesh['xl'=2,'z4'=2,'z2'=2,'z1'=2,'c'=2,'xh'=2,'y4'=2,'y2'=2,'y1'=2] {'c'}, dimensions={0}, use_global_device_ids=true | all-gather | bytes 1376256 | tf_op jit(solution)/shard_map/all_gather | solution.py:347
  122.1 1.7 %finish.1 = f32[3,1,2304]{2,1,0:T(1,128)} custom-call(f32[1792,128]{1,0:T(8,128)S(1)} %bitcast.9), custom_call_target="tpu_custom_call" | custom-call | tf_op jit(solution)/shard_map/finish/pallas_call | solution.py:329
  (3 shorter events, 0.1 us)
Async XLA Ops:
  0.0 0.7 copy-start.5
  25.4 8.9 %copy-start.6 = (bf16[2,48,128]{2,1,0:T(8,128)(2,1)S(1)}, bf16[2,48,128]{2,1,0:T(8,128)(2,1)}, u32[]{:S(2)}) copy-start(bf16[2,48,128]{2,1,0:T(8,128)(2,1)} %constant.7.clone.low_ref) | copy-start | bytes 73732
  25.4 8.9 %copy-start.7 = (bf16[2,48,128]{2,1,0:T(8,128)(2,1)S(1)}, bf16[2,48,128]{2,1,0:T(8,128)(2,1)}, u32[]{:S(2)}) copy-start(bf16[2,48,128]{2,1,0:T(8,128)(2,1)} %constant.6.clone.high_ref) | copy-start | bytes 73732
  25.4 28.8 %all-to-all-start.1 = ((f32[16,112,128]{2,1,0:T(8,128)}), f32[16,112,128]{2,1,0:T(8,128)S(1)}, u32[]{:S(2)}, u32[]{:S(2)}) async-start(f32[16,112,128]{2,1,0:T(8,128)} %join.1), calls=%async_computation.1 | async-start | bytes 1835008 | tf_op jit(solution)/shard_map/all_to_all | solution.py:343
  34.6 1.0 copy-start
  35.6 1.0 copy-start.2
  54.2 8.2 %copy-start.1 = (bf16[2,2,256,512]{3,2,1,0:T(8,128)(2,1)S(1)}, bf16[2,2,256,512]{3,2,1,0:T(8,128)(2,1)}, u32[]{:S(2)}) copy-start(bf16[2,2,256,512]{3,2,1,0:T(8,128)(2,1)} %copy-done) | copy-start | bytes 3145732
  54.2 8.2 %copy-start.3 = (bf16[2,2,256,512]{3,2,1,0:T(8,128)(2,1)S(1)}, bf16[2,2,256,512]{3,2,1,0:T(8,128)(2,1)}, u32[]{:S(2)}) copy-start(bf16[2,2,256,512]{3,2,1,0:T(8,128)(2,1)} %copy-done.2) | copy-start | bytes 3145732
  54.2 8.2 %copy-start.4 = (bf16[4,48,144]{2,1,0:T(8,128)(2,1)S(1)}, bf16[4,48,144]{2,1,0:T(8,128)(2,1)}, u32[]{:S(2)}) copy-start(bf16[4,48,144]{2,1,0:T(8,128)(2,1)} %constant.8.clone.left_ref) | copy-start | bytes 165892

commit v11 on v9

--- a/solution.py
+++ b/solution.py
@@ -254,21 +254,21 @@
     ]
     high, low = split(jnp.concatenate(sums + [jnp.zeros((128 - BANDS, 128), f32)], 0))
     ones = jnp.ones((8, 128), bf16)
-    line = dot_t(ones, high) + dot_t(ones, low)
+    line = (dot_t(ones, high) + dot_t(ones, low))[:1]
     for k in range(SLABS):
         copies_ref[k] = line
 
 
 def column_part(shares, orbitals):
     field = jax.ShapeDtypeStruct((ROWS, 128), f32)
-    copies = jax.ShapeDtypeStruct((SLABS, 8, 128), f32)
+    copies = jax.ShapeDtypeStruct((SLABS, 1, 128), f32)
     return pl.pallas_call(column_kernel, out_shape=(field, copies), name="column", compiler_params=SMALL)(
         shares, orbitals
     )
 
 
 def attach_kernel(field_ref, parts_ref, copies_ref):
-    column = jnp.sum(parts_ref[...], axis=0)[:1]
+    column = sum(parts_ref[k] for k in range(SLABS))
     row = lax.broadcasted_iota(jnp.int32, (ROWS, 128), 0)
     tile = jnp.where(row == USED, column, field_ref[...])
     for k in range(CHIPS):

time: 124 us -> 124 us (level)
  no operation moved by 1% of the time
where the time goes in v11:
time: 124 us
  blocking collectives  92.7 us (75%)
  waiting for transfers between devices  12.3 us (10%)
  starting transfers between devices  8.85 us (7%)
  Pallas kernels  7.19 us (6%)
  local copies, waits for them, and re-layouts  2.76 us (2%)
    all_to_all x2, blocking collectives, exchange_tiles(): return lax.all_to_all(tiles, axis, 0, 0, tiled=True)  39.6 us
    all_to_all x2, blocking collectives, exchange_roles(): lax.all_to_all(tiles, CROSS, 0, 0, axis_index_groups=ROLES, tiled=True)  32.7 us
    all_gather x3, blocking collectives, both_cores(): return lax.all_gather(chips, CORE, axis=0, tiled=False).reshape(-1, 128)  20.5 us
    all_to_all x1, waiting for transfers between devices, exchange_roles(): lax.all_to_all(tiles, CROSS, 0, 0, axis_index_groups=ROLES, tiled=True)  12.3 us
    all_to_all x1, starting transfers between devices, exchange_roles(): lax.all_to_all(tiles, CROSS, 0, 0, axis_index_groups=ROLES, tiled=True)  8.85 us
    pallas_call x1, Pallas kernels, partial_exchange(): pl.pallas_call(exchange_kernel, out_shape=jax.ShapeDtypeStruct((SLABS * R...  3.82 us
    unnamed x16, local copies, waits for them, and re-layouts  2.73 us
  transfers between devices with their start and end apart: 1, of which 1 were waited for; matrix products, arithmetic and copies ran while one was open for 0% of the time, Pallas kernels for 0%

profile of v11, /device:TPU:1, one launch (start us, length us, event | category | flops | bytes accessed | tf_op | source)
XLA Modules:
  0.0 123.9 jit_solution(9039614029860330878)
XLA Ops:
  0.0 0.0 copy-start.5
  0.0 0.7 copy-done.5
  0.8 23.6 %all_to_all.25.chips_ref = f32[16,56,128]{2,1,0:T(8,128)S(1)} all-to-all(f32[16,56,128]{2,1,0:T(8,128)S(1)} %prepare.1), channel_id=1, replica_groups=mesh['xl'=2,'z4'=2,'z2'=2,'z1'=2,'c'=2,'xh'=2,'y4'=2,'y2'=2,'y1'=2] {'xl..., dimensions={0} | all-to-all | bytes 917504 | tf_op jit(solution)/shard_map/all_to_all | solution.py:338
  24.4 1.0 join.1
  25.4 0.0 copy-start.6
  25.4 0.0 copy-start.7
  25.4 8.9 %all-to-all-start.1 = ((f32[16,112,128]{2,1,0:T(8,128)}), f32[16,112,128]{2,1,0:T(8,128)S(1)}, u32[]{:S(2)}, u32[]{:S(2)}) async-start(f32[16,112,128]{2,1,0:T(8,128)} %join.1), calls=%async_computation.1 | async-start | bytes 1835008 | tf_op jit(solution)/shard_map/all_to_all | solution.py:342
  34.3 0.0 copy-done.6
  34.3 0.0 copy-done.7
  34.3 0.3 tables.1
  34.6 0.0 copy-start
  34.6 1.0 copy-done
  35.6 0.0 copy-start.2
  35.6 1.0 copy-done.2
  36.6 5.3 %all-gather = f32[32,56,128]{2,1,0:T(8,128)S(1)} all-gather(f32[16,56,128]{2,1,0:T(8,128)S(1)} %all_to_all.25.chips_ref), channel_id=2, replica_groups=mesh['xl'=2,'z4'=2,'z2'=2,'z1'=2,'c'=2,'xh'=2,'y4'=2,'y2'=2,'y1'=2] {'c'}, dimensions={0}, use_global_device_ids=true | all-gather | bytes 1376256 | tf_op jit(solution)/shard_map/all_gather | solution.py:346
  41.9 12.3 %all-to-all-done.1 = f32[16,112,128]{2,1,0:T(8,128)S(1)} async-done(((f32[16,112,128]{2,1,0:T(8,128)}), f32[16,112,128]{2,1,0:T(8,128)S(1)}, u32[]{:S(2)}, u32[]{:S(2)}) %all-to-all-start.1) | async-done | bytes 917536 | tf_op jit(solution)/shard_map/all_to_all | solution.py:342
  54.2 0.0 copy-start.1
  54.2 0.0 copy-start.3
  54.2 0.0 copy-start.4
  54.3 8.1 %all-gather.1 = f32[32,56,128]{2,1,0:T(8,128)S(1)} all-gather(f32[16,56,128]{2,1,0:T(8,128)S(1)} %slice.3), channel_id=3, replica_groups=mesh['xl'=2,'z4'=2,'z2'=2,'z1'=2,'c'=2,'xh'=2,'y4'=2,'y2'=2,'y1'=2] {'c'}, dimensions={0}, use_global_device_ids=true | all-gather | bytes 1376256 | tf_op jit(solution)/shard_map/all_gather | solution.py:346
  62.4 0.0 copy-done.1
  62.4 0.0 copy-done.3
  62.4 0.0 copy-done.4
  62.4 3.8 %exchange.1 = f32[896,128]{1,0:T(8,128)S(1)} custom-call(f32[1792,128]{1,0:T(8,128)S(1)} %bitcast.7, f32[1792,128]{1,0:T(8,128)S(1)} %bitcast.10, bf16[4,48,144]{2,1,0:T(8,128)(2,1)S(1)} %copy-done.4, bf16[2,2,256,512]{3,2,1,0:T(8,128)(2,1)S(1)} %copy-done.1, bf16[2,2,256,512]{3,2,1,0:T(8,128)(2,1)S(1)} %copy-done.3, ...), custom_call_target="tpu_custom_call" | custom-call | tf_op jit(solution)/shard_map/exchange/pallas_call | solution.py:198
  66.2 17.9 %all_to_all.26.share_ref = f32[16,56,128]{2,1,0:T(8,128)S(1)} all-to-all(f32[16,56,128]{2,1,0:T(8,128)S(1)} %bitcast.11), channel_id=1, replica_groups={{0,1,2,3,4,5,6,7,264,265,266,267,268,269,270,271},{256,257,258,259,260,..., dimensions={0} | all-to-all | bytes 917504 | tf_op jit(solution)/shard_map/all_to_all | solution.py:342
  84.1 0.2 column.1
  84.3 14.8 %all_to_all.27.parts_ref = f32[16,1,128]{2,1,0:T(1,128)S(1)} all-to-all(f32[16,1,128]{2,1,0:T(1,128)S(1)} %get-tuple-element.18), channel_id=1, replica_groups={{0,1,2,3,4,5,6,7,264,265,266,267,268,269,270,271},{256,257,258,259,260,..., dimensions={0} | all-to-all | bytes 16384 | tf_op jit(solution)/shard_map/all_to_all | solution.py:342
  99.2 16.0 %all_to_all.28 = f32[16,56,128]{2,1,0:T(8,128)S(1)} all-to-all(f32[16,56,128]{2,1,0:T(8,128)S(1)} %attach.1), channel_id=1, replica_groups=mesh['xl'=2,'z4'=2,'z2'=2,'z1'=2,'c'=2,'xh'=2,'y4'=2,'y2'=2,'y1'=2] {'xl..., dimensions={0} | all-to-all | bytes 917504 | tf_op jit(solution)/shard_map/all_to_all | solution.py:338
  115.1 7.0 %all-gather.2 = f32[32,56,128]{2,1,0:T(8,128)S(1)} all-gather(f32[16,56,128]{2,1,0:T(8,128)S(1)} %all_to_all.28), channel_id=4, replica_groups=mesh['xl'=2,'z4'=2,'z2'=2,'z1'=2,'c'=2,'xh'=2,'y4'=2,'y2'=2,'y1'=2] {'c'}, dimensions={0}, use_global_device_ids=true | all-gather | bytes 1376256 | tf_op jit(solution)/shard_map/all_gather | solution.py:346
  122.2 1.8 %finish.1 = f32[3,1,2304]{2,1,0:T(1,128)} custom-call(f32[1792,128]{1,0:T(8,128)S(1)} %bitcast.9), custom_call_target="tpu_custom_call" | custom-call | tf_op jit(solution)/shard_map/finish/pallas_call | solution.py:328
  (3 shorter events, 0.1 us)
Async XLA Ops:
  0.0 0.7 copy-start.5
  25.4 8.9 %copy-start.6 = (bf16[2,48,128]{2,1,0:T(8,128)(2,1)S(1)}, bf16[2,48,128]{2,1,0:T(8,128)(2,1)}, u32[]{:S(2)}) copy-start(bf16[2,48,128]{2,1,0:T(8,128)(2,1)} %constant.7.clone.low_ref) | copy-start | bytes 73732
  25.4 8.9 %copy-start.7 = (bf16[2,48,128]{2,1,0:T(8,128)(2,1)S(1)}, bf16[2,48,128]{2,1,0:T(8,128)(2,1)}, u32[]{:S(2)}) copy-start(bf16[2,48,128]{2,1,0:T(8,128)(2,1)} %constant.6.clone.high_ref) | copy-start | bytes 73732
  25.4 28.8 %all-to-all-start.1 = ((f32[16,112,128]{2,1,0:T(8,128)}), f32[16,112,128]{2,1,0:T(8,128)S(1)}, u32[]{:S(2)}, u32[]{:S(2)}) async-start(f32[16,112,128]{2,1,0:T(8,128)} %join.1), calls=%async_computation.1 | async-start | bytes 1835008 | tf_op jit(solution)/shard_map/all_to_all | solution.py:342
  34.6 1.0 copy-start
  35.6 1.0 copy-start.2
  54.2 8.2 %copy-start.1 = (bf16[2,2,256,512]{3,2,1,0:T(8,128)(2,1)S(1)}, bf16[2,2,256,512]{3,2,1,0:T(8,128)(2,1)}, u32[]{:S(2)}) copy-start(bf16[2,2,256,512]{3,2,1,0:T(8,128)(2,1)} %copy-done) | copy-start | bytes 3145732
  54.2 8.2 %copy-start.3 = (bf16[2,2,256,512]{3,2,1,0:T(8,128)(2,1)S(1)}, bf16[2,2,256,512]{3,2,1,0:T(8,128)(2,1)}, u32[]{:S(2)}) copy-start(bf16[2,2,256,512]{3,2,1,0:T(8,128)(2,1)} %copy-done.2) | copy-start | bytes 3145732
  54.2 8.2 %copy-start.4 = (bf16[4,48,144]{2,1,0:T(8,128)(2,1)S(1)}, bf16[4,48,144]{2,1,0:T(8,128)(2,1)}, u32[]{:S(2)}) copy-start(bf16[4,48,144]{2,1,0:T(8,128)(2,1)} %constant.8.clone.left_ref) | copy-start | bytes 165892

commit v12 on v11

--- a/solution.py
+++ b/solution.py
@@ -280,7 +280,7 @@
     return pl.pallas_call(attach_kernel, out_shape=copies, name="attach", compiler_params=SMALL)(field, parts)
 
 
-BLOCK = 8
+BLOCK = 16
 
 
 def place_of(band):
@@ -303,7 +303,8 @@
         columns = [jnp.broadcast_to(state[:, a : a + 1], (BANDS, 2 * BANDS)) for a in at]
         pivots = [state[a : a + 1, :] for a in at]
         for i in range(BLOCK):
-            factor = jnp.where(order > first + i, columns[i] / columns[i][at[i] : at[i] + 1, :], 0.0)
+            inverse = 1.0 / columns[i][at[i] : at[i] + 1, :]
+            factor = jnp.where(order > first + i, columns[i] * inverse, 0.0)
             for j in range(i + 1, BLOCK):
                 columns[j] = columns[j] - factor * columns[j][at[i] : at[i] + 1, :]
                 pivots[j] = pivots[j] - factor[at[j] : at[j] + 1, :] * pivots[i]

time: 124 us -> 124 us (level)
  no operation moved by 1% of the time
where the time goes in v12:
time: 124 us
  blocking collectives  92.7 us (75%)
  waiting for transfers between devices  12.3 us (10%)
  starting transfers between devices  8.85 us (7%)
  Pallas kernels  7.1 us (6%)
  local copies, waits for them, and re-layouts  2.76 us (2%)
    all_to_all x2, blocking collectives, exchange_tiles(): return lax.all_to_all(tiles, axis, 0, 0, tiled=True)  39.6 us
    all_to_all x2, blocking collectives, exchange_roles(): lax.all_to_all(tiles, CROSS, 0, 0, axis_index_groups=ROLES, tiled=True)  32.7 us
    all_gather x3, blocking collectives, both_cores(): return lax.all_gather(chips, CORE, axis=0, tiled=False).reshape(-1, 128)  20.5 us
    all_to_all x1, waiting for transfers between devices, exchange_roles(): lax.all_to_all(tiles, CROSS, 0, 0, axis_index_groups=ROLES, tiled=True)  12.3 us
    all_to_all x1, starting transfers between devices, exchange_roles(): lax.all_to_all(tiles, CROSS, 0, 0, axis_index_groups=ROLES, tiled=True)  8.85 us
    pallas_call x1, Pallas kernels, partial_exchange(): pl.pallas_call(exchange_kernel, out_shape=jax.ShapeDtypeStruct((SLABS * R...  3.82 us
    unnamed x16, local copies, waits for them, and re-layouts  2.73 us
  transfers between devices with their start and end apart: 1, of which 1 were waited for; matrix products, arithmetic and copies ran while one was open for 0% of the time, Pallas kernels for 0%

profile of v12, /device:TPU:1, one launch (start us, length us, event | category | flops | bytes accessed | tf_op | source)
XLA Modules:
  0.0 123.8 jit_solution(12153711485009532203)
XLA Ops:
  0.0 0.0 copy-start.5
  0.0 0.7 copy-done.5
  0.8 23.6 %all_to_all.25.chips_ref = f32[16,56,128]{2,1,0:T(8,128)S(1)} all-to-all(f32[16,56,128]{2,1,0:T(8,128)S(1)} %prepare.1), channel_id=1, replica_groups=mesh['xl'=2,'z4'=2,'z2'=2,'z1'=2,'c'=2,'xh'=2,'y4'=2,'y2'=2,'y1'=2] {'xl..., dimensions={0} | all-to-all | bytes 917504 | tf_op jit(solution)/shard_map/all_to_all | solution.py:339
  24.4 1.0 join.1
  25.4 0.0 copy-start.6
  25.4 0.0 copy-start.7
  25.4 8.9 %all-to-all-start.1 = ((f32[16,112,128]{2,1,0:T(8,128)}), f32[16,112,128]{2,1,0:T(8,128)S(1)}, u32[]{:S(2)}, u32[]{:S(2)}) async-start(f32[16,112,128]{2,1,0:T(8,128)} %join.1), calls=%async_computation.1 | async-start | bytes 1835008 | tf_op jit(solution)/shard_map/all_to_all | solution.py:343
  34.3 0.0 copy-done.6
  34.3 0.0 copy-done.7
  34.3 0.3 tables.1
  34.6 0.0 copy-start
  34.6 1.0 copy-done
  35.6 0.0 copy-start.2
  35.6 1.0 copy-done.2
  36.6 5.3 %all-gather = f32[32,56,128]{2,1,0:T(8,128)S(1)} all-gather(f32[16,56,128]{2,1,0:T(8,128)S(1)} %all_to_all.25.chips_ref), channel_id=2, replica_groups=mesh['xl'=2,'z4'=2,'z2'=2,'z1'=2,'c'=2,'xh'=2,'y4'=2,'y2'=2,'y1'=2] {'c'}, dimensions={0}, use_global_device_ids=true | all-gather | bytes 1376256 | tf_op jit(solution)/shard_map/all_gather | solution.py:347
  41.9 12.3 %all-to-all-done.1 = f32[16,112,128]{2,1,0:T(8,128)S(1)} async-done(((f32[16,112,128]{2,1,0:T(8,128)}), f32[16,112,128]{2,1,0:T(8,128)S(1)}, u32[]{:S(2)}, u32[]{:S(2)}) %all-to-all-start.1) | async-done | bytes 917536 | tf_op jit(solution)/shard_map/all_to_all | solution.py:343
  54.2 0.0 copy-start.1
  54.2 0.0 copy-start.3
  54.2 0.0 copy-start.4
  54.3 8.1 %all-gather.1 = f32[32,56,128]{2,1,0:T(8,128)S(1)} all-gather(f32[16,56,128]{2,1,0:T(8,128)S(1)} %slice.3), channel_id=3, replica_groups=mesh['xl'=2,'z4'=2,'z2'=2,'z1'=2,'c'=2,'xh'=2,'y4'=2,'y2'=2,'y1'=2] {'c'}, dimensions={0}, use_global_device_ids=true | all-gather | bytes 1376256 | tf_op jit(solution)/shard_map/all_gather | solution.py:347
  62.4 0.0 copy-done.1
  62.4 0.0 copy-done.3
  62.4 0.0 copy-done.4
  62.4 3.8 %exchange.1 = f32[896,128]{1,0:T(8,128)S(1)} custom-call(f32[1792,128]{1,0:T(8,128)S(1)} %bitcast.7, f32[1792,128]{1,0:T(8,128)S(1)} %bitcast.10, bf16[4,48,144]{2,1,0:T(8,128)(2,1)S(1)} %copy-done.4, bf16[2,2,256,512]{3,2,1,0:T(8,128)(2,1)S(1)} %copy-done.1, bf16[2,2,256,512]{3,2,1,0:T(8,128)(2,1)S(1)} %copy-done.3, ...), custom_call_target="tpu_custom_call" | custom-call | tf_op jit(solution)/shard_map/exchange/pallas_call | solution.py:198
  66.2 17.9 %all_to_all.26.share_ref = f32[16,56,128]{2,1,0:T(8,128)S(1)} all-to-all(f32[16,56,128]{2,1,0:T(8,128)S(1)} %bitcast.11), channel_id=1, replica_groups={{0,1,2,3,4,5,6,7,264,265,266,267,268,269,270,271},{256,257,258,259,260,..., dimensions={0} | all-to-all | bytes 917504 | tf_op jit(solution)/shard_map/all_to_all | solution.py:343
  84.1 0.2 column.1
  84.3 14.8 %all_to_all.27.parts_ref = f32[16,1,128]{2,1,0:T(1,128)S(1)} all-to-all(f32[16,1,128]{2,1,0:T(1,128)S(1)} %get-tuple-element.18), channel_id=1, replica_groups={{0,1,2,3,4,5,6,7,264,265,266,267,268,269,270,271},{256,257,258,259,260,..., dimensions={0} | all-to-all | bytes 16384 | tf_op jit(solution)/shard_map/all_to_all | solution.py:343
  99.2 16.0 %all_to_all.28 = f32[16,56,128]{2,1,0:T(8,128)S(1)} all-to-all(f32[16,56,128]{2,1,0:T(8,128)S(1)} %attach.1), channel_id=1, replica_groups=mesh['xl'=2,'z4'=2,'z2'=2,'z1'=2,'c'=2,'xh'=2,'y4'=2,'y2'=2,'y1'=2] {'xl..., dimensions={0} | all-to-all | bytes 917504 | tf_op jit(solution)/shard_map/all_to_all | solution.py:339
  115.1 7.0 %all-gather.2 = f32[32,56,128]{2,1,0:T(8,128)S(1)} all-gather(f32[16,56,128]{2,1,0:T(8,128)S(1)} %all_to_all.28), channel_id=4, replica_groups=mesh['xl'=2,'z4'=2,'z2'=2,'z1'=2,'c'=2,'xh'=2,'y4'=2,'y2'=2,'y1'=2] {'c'}, dimensions={0}, use_global_device_ids=true | all-gather | bytes 1376256 | tf_op jit(solution)/shard_map/all_gather | solution.py:347
  122.2 1.7 %finish.1 = f32[3,1,2304]{2,1,0:T(1,128)} custom-call(f32[1792,128]{1,0:T(8,128)S(1)} %bitcast.9), custom_call_target="tpu_custom_call" | custom-call | tf_op jit(solution)/shard_map/finish/pallas_call | solution.py:329
  (3 shorter events, 0.1 us)
Async XLA Ops:
  0.0 0.7 copy-start.5
  25.4 8.9 %copy-start.6 = (bf16[2,48,128]{2,1,0:T(8,128)(2,1)S(1)}, bf16[2,48,128]{2,1,0:T(8,128)(2,1)}, u32[]{:S(2)}) copy-start(bf16[2,48,128]{2,1,0:T(8,128)(2,1)} %constant.7.clone.low_ref) | copy-start | bytes 73732
  25.4 8.9 %copy-start.7 = (bf16[2,48,128]{2,1,0:T(8,128)(2,1)S(1)}, bf16[2,48,128]{2,1,0:T(8,128)(2,1)}, u32[]{:S(2)}) copy-start(bf16[2,48,128]{2,1,0:T(8,128)(2,1)} %constant.6.clone.high_ref) | copy-start | bytes 73732
  25.4 28.8 %all-to-all-start.1 = ((f32[16,112,128]{2,1,0:T(8,128)}), f32[16,112,128]{2,1,0:T(8,128)S(1)}, u32[]{:S(2)}, u32[]{:S(2)}) async-start(f32[16,112,128]{2,1,0:T(8,128)} %join.1), calls=%async_computation.1 | async-start | bytes 1835008 | tf_op jit(solution)/shard_map/all_to_all | solution.py:343
  34.6 1.0 copy-start
  35.6 1.0 copy-start.2
  54.2 8.2 %copy-start.1 = (bf16[2,2,256,512]{3,2,1,0:T(8,128)(2,1)S(1)}, bf16[2,2,256,512]{3,2,1,0:T(8,128)(2,1)}, u32[]{:S(2)}) copy-start(bf16[2,2,256,512]{3,2,1,0:T(8,128)(2,1)} %copy-done) | copy-start | bytes 3145732
  54.2 8.2 %copy-start.3 = (bf16[2,2,256,512]{3,2,1,0:T(8,128)(2,1)S(1)}, bf16[2,2,256,512]{3,2,1,0:T(8,128)(2,1)}, u32[]{:S(2)}) copy-start(bf16[2,2,256,512]{3,2,1,0:T(8,128)(2,1)} %copy-done.2) | copy-start | bytes 3145732
  54.2 8.2 %copy-start.4 = (bf16[4,48,144]{2,1,0:T(8,128)(2,1)S(1)}, bf16[4,48,144]{2,1,0:T(8,128)(2,1)}, u32[]{:S(2)}) copy-start(bf16[4,48,144]{2,1,0:T(8,128)(2,1)} %constant.8.clone.left_ref) | copy-start | bytes 165892
